TPU v7x, 256 devices: a whole 4x4x8 slice. The times are simulated.
256 devices in a mesh: half: 2 (over core), row: 16 (over x, y), col: 8 (over z).
Axes of the slice: x: 4, y: 4, z: 8, core: 2. Of those that a mesh axis runs over, the one named last changes fastest.
Arguments:
- particles: bfloat16 [512, 2, 64, 4096], P(('half', 'row', 'col')), may hold values from -9 to 9
- orient_bin: int32 [512], P(('half', 'row', 'col')), may hold values from 0 to 15
- tilt_slope: int32 [512, 2], P(('half', 'row', 'col')), may hold values from 12 to 40
- interp_table: bfloat16 [16, 3, 64, 64], replicated, may hold values from 0 to 1.6, as said below
Outputs:
- half_maps: float32 [2, 2, 64, 4096], P('half', None, 'row', 'col')
- shell_power: float32 [2, 29], replicated
- shell_correlation: float32 [2, 29], P('half')
Inputs may be any that keep to these rules, and one draw needn't show every extreme that they name: `interp_table`: nonnegative entries.
All inputs are finite; a program needn't handle non-finite values.
Results may differ from a plain program's by a relative error of at most 0.00063.
Values sent between devices are 32-bit elements; how exact they have to be, the bound alone decides.
No kernel may reach another device: no remote copies, remote signals or barrier semaphores. Data moves between devices by JAX's collectives and lax.ppermute only.
A program may use at most 64 MiB of HBM per device.

v0:
```python
import functools

import jax
import jax.numpy as jnp
from jax import lax
from jax.sharding import Mesh
from jax.sharding import PartitionSpec as P

SHELLS = 29
ROW = ("row_0", "row_1")
ROW_COL = ("row_0", "row_1", "col")
HALF_ROW_COL = ("half", "row_0", "row_1", "col")


def split_up(x, dim, size):
    before, after = (x.shape[:dim], x.shape[dim + 1 :])
    return jnp.moveaxis(x.reshape(*before, size, -1, *after), dim, 0)


def summed_on_arrival(x, axis, dim):
    size = lax.axis_size(axis)
    parts = lax.all_to_all(split_up(x, dim, size), axis, 0, 0, tiled=True)
    return jnp.sum(parts, axis=0)


def partner_2(value, axis, distance):
    mask = 2**distance
    pairs = [(source, source ^ mask) for source in range(lax.axis_size(axis))]
    return lax.ppermute(value, axis, pairs)


def one_axis_at_a_time(x, axes):
    return functools.reduce(lax.psum, axes, x)


def wedge_mask(tilt_limits, grid_size):
    centre = grid_size // 2
    wave_first = (jnp.arange(grid_size, dtype=jnp.int32) - centre)[:, None]
    wave_third = (jnp.arange(grid_size * grid_size, dtype=jnp.int32) % grid_size - centre)[None, :]
    tilt_limit = jnp.where(wave_first * wave_third >= 0, tilt_limits[0], tilt_limits[1])
    inside = 16 * jnp.abs(wave_third) <= tilt_limit * jnp.abs(wave_first)
    return inside.astype(jnp.float32)


def interpolate(stacked, kernels, grid_size):
    components = stacked.shape[0]
    along_first = jnp.einsum(
        "ax,cxm->cam", kernels[0], stacked, preferred_element_type=jnp.float32
    ).astype(jnp.bfloat16)
    along_first = along_first.reshape(components, grid_size, grid_size, grid_size)
    along_second = jnp.einsum(
        "by,cayz->cabz", kernels[1], along_first, preferred_element_type=jnp.float32
    ).astype(jnp.bfloat16)
    along_third = jnp.einsum(
        "dz,cabz->cabd", kernels[2], along_second, preferred_element_type=jnp.float32
    )
    return along_third.reshape(components, grid_size, grid_size * grid_size)


def shell_table(first_index, plane_index, grid_size, shells):
    centre = grid_size // 2
    wave_first = first_index - centre
    wave_second = plane_index // grid_size - centre
    wave_third = plane_index % grid_size - centre
    radius_sq = (
        wave_first * wave_first + wave_second * wave_second + wave_third * wave_third
    ).reshape(-1)
    bounds = jnp.arange(4, centre, dtype=jnp.int32)
    shell_index = jnp.sum(
        (radius_sq[:, None] >= (bounds * bounds)[None, :]).astype(jnp.int32), axis=1
    )
    within = radius_sq < centre * centre
    onehot = (shell_index[:, None] == jnp.arange(shells, dtype=jnp.int32)[None, :]) & within[
        :, None
    ]
    return onehot.astype(jnp.float32)


def spread_slabs(volume):
    slabs = summed_on_arrival(volume, ROW, 1)
    return summed_on_arrival(slabs, "col", 2)


def local(particles, orient_bin, tilt_slope, interp_table):
    grid_size = particles.shape[2]
    particle_count = particles.shape[0]
    rows_local = grid_size // lax.axis_size(ROW)
    cols_local = grid_size * grid_size // lax.axis_size("col")
    components = 3

    def insert_one(particle, partial_value):
        volume_data = lax.dynamic_index_in_dim(particles, particle, 0, keepdims=False)
        bin_row = lax.dynamic_index_in_dim(orient_bin, particle, 0, keepdims=False)
        tilt_limits = lax.dynamic_index_in_dim(tilt_slope, particle, 0, keepdims=False)
        weight = wedge_mask(tilt_limits, grid_size)
        stacked = jnp.stack([volume_data[0] * weight, volume_data[1] * weight, weight]).astype(
            jnp.bfloat16
        )
        kernels = lax.dynamic_index_in_dim(interp_table, bin_row, 0, keepdims=False)
        return partial_value + interpolate(stacked, kernels, grid_size)

    partial_value = jnp.zeros((components, grid_size, grid_size * grid_size), jnp.float32)
    partial_value = lax.fori_loop(0, particle_count, insert_one, partial_value)
    sums = spread_slabs(partial_value)
    weight_sum = sums[2]
    half_maps = (sums[:2] / (weight_sum[None] + 1.0))[None]
    partner = partner_2(half_maps, "half", 0)
    on_first = lax.axis_index("half") == 0
    map_first = jnp.where(on_first, half_maps, partner)[0]
    map_second = jnp.where(on_first, partner, half_maps)[0]
    cross_term = (map_first[0] * map_second[0] + map_first[1] * map_second[1]).reshape(-1)
    power_first = (map_first[0] * map_first[0] + map_first[1] * map_first[1]).reshape(-1)
    power_second = (map_second[0] * map_second[0] + map_second[1] * map_second[1]).reshape(-1)
    products = jnp.stack([cross_term, power_first, power_second])
    first_index = (
        lax.axis_index(ROW) * rows_local + jnp.arange(rows_local, dtype=jnp.int32)[:, None]
    )
    plane_index = (
        lax.axis_index("col") * cols_local + jnp.arange(cols_local, dtype=jnp.int32)[None, :]
    )
    onehot = shell_table(first_index, plane_index, grid_size, SHELLS)
    spectra = jnp.dot(products, onehot, precision=lax.Precision.HIGHEST)
    counts = jnp.sum(onehot, axis=0)
    spectra, counts = (one_axis_at_a_time(spectra, ROW_COL), one_axis_at_a_time(counts, ROW_COL))
    shell_power = spectra[1:3] / counts[None, :]
    shell_correlation = (spectra[0] / jnp.sqrt(spectra[1] * spectra[2] + 1e-06))[None]
    return (half_maps, shell_power, shell_correlation)


def solution(mesh):
    torus = Mesh(
        mesh.devices.reshape(mesh.shape["half"], 4, 4, mesh.shape["col"]),
        ("half", "row_0", "row_1", "col"),
    )
    in_specs = (P(HALF_ROW_COL, None, None, None), P(HALF_ROW_COL), P(HALF_ROW_COL, None), P())
    out_specs = (P("half", None, ROW, "col"), P(), P("half", None))
    return jax.shard_map(local, mesh=torus, in_specs=in_specs, out_specs=out_specs, check_vma=False)
```

profile of v0, /device:TPU:2, one launch (start us, length us, event | category | flops | bytes accessed | tf_op | source)
XLA Modules:
  0.0 170.0 jit_solution(13505677544732401227)
XLA Ops:
  0.6 57.2 %while.17 = (s32[]{:T(128)}, f32[3,64,4096]{2,1,0:T(8,128)}, s32[2,2]{1,0:T(2,128)}, bf16[2,2,64,4096]{3,2,1,0:T(8,128)(2,1)}, s32[2]{0:T(128)}, /*index=5*/bf16...) while((s32[]{:T(128)}, f32[3,64,4096]{2,1,0:T(8,128)}, ...), condition=%wide.region_1.2_spmd.clone, body=%wide.region_0.1_spmd.clone.sunk | while | flops 314609792 | bytes 29511420 | solution.py:103
  1.9 2.9 %fusion.57 = (bf16[1,64,4096]{2,1,0:T(8,128)(2,1)S(1)}, bf16[1,64,4096]{2,1,0:T(8,128)(2,1)S(1)}) fusion(bf16[2,2,64,4096]{3,2,1,0:T(8,128)(2,1)} %get-tuple-element.314, s32[]{:T(128)} %get-tuple-element.300, s32[64]{0:T(128)S(1)} %get-tuple-element.281, s32[]{:T(128)} %bitcast.81, s32[]{:T(128)} %bitcast.82, s32[4096]{0:T(1024)S(1)} %get-tuple-element.284, ...), kind=kLoop, calls=%fused_computation.15.clone.1 | loop fusion | flops 2883584 | bytes 2130448 | tf_op jit(solution)/shard_map/convert.2
  4.8 1.6 convert_convert_fusion.2
  9.6 2.4 %fusion.58 = bf16[3,64,4096]{2,1,0:T(8,128)(2,1)} fusion(bf16[1,64,4096]{2,1,0:T(8,128)(2,1)S(1)} %convert_convert_fusion.2, bf16[1,64,4096]{2,1,0:T(8,128)(2,1)S(1)} %get-tuple-element.287, bf16[1,64,4096]{2,1,0:T(8,128)(2,1)S(1)} %get-tuple-element.288, bf16[16,3,64,64]{3,2,1,0:T(8,128)(2,1)} %get-tuple-element.316, s32[]{:T(128)S(6)} %select_n.174), kind=kOutput, calls=%fused_computation.1.clone.1 | convolution fusion | flops 106168320 | bytes 3162116 | tf_op jit(solution)/shard_map/while/body/eval_jaxpr/ax,cxm->cam/dot_general | solution.py:47
  12.1 4.3 %reshape.637 = bf16[3,64,64,64]{3,2,1,0:T(8,128)(2,1)S(1)} reshape(bf16[3,64,4096]{2,1,0:T(8,128)(2,1)} %fusion.58) | data formatting | bytes 3145728 | tf_op jit(solution)/shard_map/while/body/eval_jaxpr/reshape | solution.py:50
  16.4 5.4 %fusion.59 = f32[3,64,64,64]{3,2,1,0:T(8,128)} fusion(bf16[3,64,64,64]{3,2,1,0:T(8,128)(2,1)S(1)} %reshape.637, bf16[16,3,64,64]{3,2,1,0:T(8,128)(2,1)} %get-tuple-element.316, s32[]{:T(128)S(6)} %select_n.174, s32[]{:T(128)S(6)} %add.406, s32[]{:T(128)S(6)} %add.404), kind=kOutput, calls=%fused_computation.2.clone.1 | convolution fusion | flops 202113024 | bytes 4753408 | tf_op jit(solution)/shard_map/while/body/eval_jaxpr/dz,cabz->cabd/dot_general | solution.py:54
  21.8 4.5 %reshape.638 = f32[3,64,4096]{2,1,0:T(8,128)S(1)} reshape(f32[3,64,64,64]{3,2,1,0:T(8,128)} %fusion.59) | data formatting | bytes 6291456 | tf_op jit(solution)/shard_map/while/body/eval_jaxpr/reshape | solution.py:57
  26.2 2.1 %select_add_fusion.2 = f32[3,64,4096]{2,1,0:T(8,128)} fusion(f32[3,64,4096]{2,1,0:T(8,128)S(1)} %reshape.638, f32[3,64,4096]{2,1,0:T(8,128)} %get-tuple-element.301, pred[]{:T(512)S(6)} %compare.17), kind=kLoop, calls=%fused_computation.4.clone.1 | loop fusion | flops 1572864 | bytes 9437185 | tf_op jit(solution)/shard_map/while/body/eval_jaxpr/add | solution.py:100
  29.6 2.9 %fusion.57 = (bf16[1,64,4096]{2,1,0:T(8,128)(2,1)S(1)}, bf16[1,64,4096]{2,1,0:T(8,128)(2,1)S(1)}) fusion(bf16[2,2,64,4096]{3,2,1,0:T(8,128)(2,1)} %get-tuple-element.314, s32[]{:T(128)} %get-tuple-element.300, s32[64]{0:T(128)S(1)} %get-tuple-element.281, s32[]{:T(128)} %bitcast.81, s32[]{:T(128)} %bitcast.82, s32[4096]{0:T(1024)S(1)} %get-tuple-element.284, ...), kind=kLoop, calls=%fused_computation.15.clone.1 | loop fusion | flops 2883584 | bytes 2130448 | tf_op jit(solution)/shard_map/convert.2
  32.5 1.6 convert_convert_fusion.2
  37.3 2.4 %fusion.58 = bf16[3,64,4096]{2,1,0:T(8,128)(2,1)} fusion(bf16[1,64,4096]{2,1,0:T(8,128)(2,1)S(1)} %convert_convert_fusion.2, bf16[1,64,4096]{2,1,0:T(8,128)(2,1)S(1)} %get-tuple-element.287, bf16[1,64,4096]{2,1,0:T(8,128)(2,1)S(1)} %get-tuple-element.288, bf16[16,3,64,64]{3,2,1,0:T(8,128)(2,1)} %get-tuple-element.316, s32[]{:T(128)S(6)} %select_n.174), kind=kOutput, calls=%fused_computation.1.clone.1 | convolution fusion | flops 106168320 | bytes 3162116 | tf_op jit(solution)/shard_map/while/body/eval_jaxpr/ax,cxm->cam/dot_general | solution.py:47
  39.7 4.3 %reshape.637 = bf16[3,64,64,64]{3,2,1,0:T(8,128)(2,1)S(1)} reshape(bf16[3,64,4096]{2,1,0:T(8,128)(2,1)} %fusion.58) | data formatting | bytes 3145728 | tf_op jit(solution)/shard_map/while/body/eval_jaxpr/reshape | solution.py:50
  44.0 5.4 %fusion.59 = f32[3,64,64,64]{3,2,1,0:T(8,128)} fusion(bf16[3,64,64,64]{3,2,1,0:T(8,128)(2,1)S(1)} %reshape.637, bf16[16,3,64,64]{3,2,1,0:T(8,128)(2,1)} %get-tuple-element.316, s32[]{:T(128)S(6)} %select_n.174, s32[]{:T(128)S(6)} %add.406, s32[]{:T(128)S(6)} %add.404), kind=kOutput, calls=%fused_computation.2.clone.1 | convolution fusion | flops 202113024 | bytes 4753408 | tf_op jit(solution)/shard_map/while/body/eval_jaxpr/dz,cabz->cabd/dot_general | solution.py:54
  49.4 4.5 %reshape.638 = f32[3,64,4096]{2,1,0:T(8,128)S(1)} reshape(f32[3,64,64,64]{3,2,1,0:T(8,128)} %fusion.59) | data formatting | bytes 6291456 | tf_op jit(solution)/shard_map/while/body/eval_jaxpr/reshape | solution.py:57
  53.9 4.0 %select_add_fusion.2 = f32[3,64,4096]{2,1,0:T(8,128)} fusion(f32[3,64,4096]{2,1,0:T(8,128)S(1)} %reshape.638, f32[3,64,4096]{2,1,0:T(8,128)} %get-tuple-element.301, pred[]{:T(512)S(6)} %compare.17), kind=kLoop, calls=%fused_computation.4.clone.1 | loop fusion | flops 1572864 | bytes 9437185 | tf_op jit(solution)/shard_map/while/body/eval_jaxpr/add | solution.py:100
  57.8 3.1 %reshape.624 = f32[3,16,4,4096]{3,2,1,0:T(4,128)S(1)} reshape(f32[3,64,4096]{2,1,0:T(8,128)} %get-tuple-element.181) | data formatting | bytes 6291456 | tf_op jit(solution)/shard_map/reshape | solution.py:17
  60.9 1.9 %copy.13 = f32[16,3,4,4096]{3,2,1,0:T(4,128)} copy(f32[16,3,4,4096]{3,2,0,1:T(4,128)S(1)} %bitcast.84) | data formatting | bytes 6291456 | tf_op jit(solution)/shard_map/transpose | solution.py:17
  62.8 7.5 %all-to-all-start = ((f32[16,3,4,4096]{3,2,1,0:T(4,128)}), f32[16,3,4,4096]{3,2,1,0:T(4,128)S(1)}, u32[]{:S(2)}, u32[]{:S(2)}) async-start(f32[16,3,4,4096]{3,2,1,0:T(4,128)} %copy.13), calls=%async_computation | async-start | bytes 6291456 | tf_op jit(solution)/shard_map/all_to_all | solution.py:22
  70.3 41.1 %all-to-all-done = f32[16,3,4,4096]{3,2,1,0:T(4,128)S(1)} async-done(((f32[16,3,4,4096]{3,2,1,0:T(4,128)}), f32[16,3,4,4096]{3,2,1,0:T(4,128)S(1)}, u32[]{:S(2)}, u32[]{:S(2)}) %all-to-all-start) | async-done | bytes 3145760 | tf_op jit(solution)/shard_map/all_to_all | solution.py:22
  113.1 8.5 %all-to-all-start.1 = ((f32[8,3,4,512]{3,2,1,0:T(4,128)}), f32[8,3,4,512]{3,2,1,0:T(4,128)S(1)}, u32[]{:S(2)}, u32[]{:S(2)}) async-start(f32[8,3,4,512]{3,2,1,0:T(4,128)} %copy.14), calls=%async_computation.1 | async-start | bytes 393216 | tf_op jit(solution)/shard_map/all_to_all | solution.py:22
  121.8 9.6 %all-to-all-done.1 = f32[8,3,4,512]{3,2,1,0:T(4,128)S(1)} async-done(((f32[8,3,4,512]{3,2,1,0:T(4,128)}), f32[8,3,4,512]{3,2,1,0:T(4,128)S(1)}, u32[]{:S(2)}, u32[]{:S(2)}) %all-to-all-start.1) | async-done | bytes 196640 | tf_op jit(solution)/shard_map/all_to_all | solution.py:22
  133.0 9.0 %all-reduce.2 = (f32[3,29]{1,0:T(4,128)S(1)}, f32[29]{0:T(128)S(1)}) all-reduce(f32[3,29]{1,0:T(4,128)S(1)} %fusion.23, f32[29]{0:T(128)S(1)} %convert_reduce_fusion), channel_id=1, replica_groups=mesh['half'=2,'row_0'=4,'row_1'=4,'col'=8] {'row_0'}, use_global_device_ids=true, to_apply=%region_5.6 | all-reduce | flops 116 | bytes 928 | tf_op jit(solution)/shard_map/psum | solution.py:33
  142.1 12.1 %all-reduce.1 = (f32[3,29]{1,0:T(4,128)S(1)}, f32[29]{0:T(128)S(1)}) all-reduce(f32[3,29]{1,0:T(4,128)S(1)} %get-tuple-element.219, f32[29]{0:T(128)S(1)} %get-tuple-element.220), channel_id=1, replica_groups=mesh['half'=2,'row_0'=4,'row_1'=4,'col'=8] {'row_1'}, use_global_device_ids=true, to_apply=%region_6.7 | all-reduce | flops 116 | bytes 928 | tf_op jit(solution)/shard_map/psum | solution.py:33
  154.2 14.7 %all-reduce = (f32[3,29]{1,0:T(4,128)S(1)}, f32[29]{0:T(128)S(1)}) all-reduce(f32[3,29]{1,0:T(4,128)S(1)} %get-tuple-element.217, f32[29]{0:T(128)S(1)} %get-tuple-element.218), channel_id=1, replica_groups=mesh['half'=2,'row_0'=4,'row_1'=4,'col'=8] {'col'}, use_global_device_ids=true, to_apply=%region_7.8 | all-reduce | flops 116 | bytes 928 | tf_op jit(solution)/shard_map/psum | solution.py:33
  (37 shorter events, 9.6 us)
Async XLA Ops:
  62.8 48.7 %all-to-all-start = ((f32[16,3,4,4096]{3,2,1,0:T(4,128)}), f32[16,3,4,4096]{3,2,1,0:T(4,128)S(1)}, u32[]{:S(2)}, u32[]{:S(2)}) async-start(f32[16,3,4,4096]{3,2,1,0:T(4,128)} %copy.13), calls=%async_computation | async-start | bytes 6291456 | tf_op jit(solution)/shard_map/all_to_all | solution.py:22
  113.1 18.2 %all-to-all-start.1 = ((f32[8,3,4,512]{3,2,1,0:T(4,128)}), f32[8,3,4,512]{3,2,1,0:T(4,128)S(1)}, u32[]{:S(2)}, u32[]{:S(2)}) async-start(f32[8,3,4,512]{3,2,1,0:T(4,128)} %copy.14), calls=%async_computation.1 | async-start | bytes 393216 | tf_op jit(solution)/shard_map/all_to_all | solution.py:22
  131.5 38.5 %copy-start = (f32[1,2,4,512]{3,2,1,0:T(4,128)}, f32[1,2,4,512]{3,2,1,0:T(4,128)S(1)}, u32[]{:S(2)}) copy-start(f32[1,2,4,512]{3,2,1,0:T(4,128)S(1)} %fusion.32) | copy-start | bytes 49156
  131.5 1.3 collective-permute-start
where the time goes:
time: 171 us; the launch traced here: 170 us
  waiting for transfers between devices  51.8 us (30%)
  blocking collectives  35.8 us (21%)
  local copies, waits for them, and re-layouts  28.5 us (17%)
  other arithmetic  17.3 us (10%)
  starting transfers between devices  16 us (9%)
  matrix products  15.9 us (9%)
  loops' own time  3.98 us (2%)
    all_to_all x2, waiting for transfers between devices, summed_on_arrival(): parts = lax.all_to_all(split_up(x, dim, size), axis, 0, 0, tiled=True)  50.8 us
    psum x3, blocking collectives, one_axis_at_a_time(): return functools.reduce(lax.psum, axes, x)  35.8 us
    all_to_all x2, starting transfers between devices, summed_on_arrival(): parts = lax.all_to_all(split_up(x, dim, size), axis, 0, 0, tiled=True)  15.9 us
    dot_general x2, matrix products, interpolate(): jnp.einsum('dz,cabz->cabd', kernels[2], along_second, preferred_element_t...  10.8 us
    another operation x4, other arithmetic  8.98 us
    reshape x2, local copies, waits for them, and re-layouts, interpolate(): return along_third.reshape(components, grid_size, grid_size * grid_size)  8.9 us
    reshape x2, local copies, waits for them, and re-layouts, interpolate(): along_first.reshape(components, grid_size, grid_size, grid_size)  8.61 us
    add x2, other arithmetic, insert_one(): return partial_value + interpolate(stacked, kernels, grid_size)  6.01 us
  transfers between devices with their start and end apart: 3, of which 3 were waited for; matrix products, arithmetic and copies ran while one was open for 0% of the time, Pallas kernels for 0%

commit v1 on v0

v1 whole, which is shorter than its diff:
```python
import functools

import jax
import jax.numpy as jnp
import numpy as np
from jax import lax
from jax.experimental import pallas as pl
from jax.experimental.pallas import tpu as pltpu
from jax.sharding import Mesh
from jax.sharding import PartitionSpec as P

SHELLS = 29
GRID = 64
CENTRE = GRID // 2
BINS = 16
ROWS = 16
COLS = 8
FIRST = GRID // ROWS
SECOND = GRID // COLS
SLOPE_MIN = 12
SLOPES = 29
PITCH = 72
BLOCK = FIRST * GRID
OWN = FIRST * SECOND
ROW = ("row_0", "row_1")
HALF_ROW_COL = ("half", "row_0", "row_1", "col")
F32 = jnp.float32
BF16 = jnp.bfloat16
VMEM = pl.BlockSpec(memory_space=pltpu.VMEM)
SMEM = pl.BlockSpec(memory_space=pltpu.SMEM)


def iota(shape, dim):
    return lax.broadcasted_iota(jnp.int32, shape, dim)


def wedge_tile(slope_first, slope_second):
    wave_first = iota((GRID, 128), 0) - CENTRE
    wave_third = iota((GRID, 128), 1) % GRID - CENTRE
    limit = jnp.where(wave_first * wave_third >= 0, slope_first, slope_second)
    inside = 16 * jnp.abs(wave_third) <= limit * jnp.abs(wave_first)
    return jnp.where(inside, 1.0, 0.0).astype(BF16)


def histogram_tile(bins, slopes):
    row, lane = iota((8, 128), 0), iota((8, 128), 1)
    total = jnp.zeros((8, 128), F32)
    for p in range(2):
        for quadrant in range(2):
            place = (bins[p] // 8) * 64 + quadrant * 32 + slopes[p, quadrant] - SLOPE_MIN
            total += jnp.where((row == bins[p] % 8) & (lane == place), 1.0, 0.0)
    return total


def insert_kernel(bins, slopes, particles, table, out, planes, third, chosen, sem):
    step = pl.program_id(0)

    @pl.when(step == 0)
    def _():
        copies = [
            pltpu.make_async_copy(table.at[bins[p]], chosen.at[p], sem.at[p]) for p in range(2)
        ]
        for copy in copies:
            copy.start()
        for copy in copies:
            copy.wait()
        third[...] = jnp.zeros_like(third)
        for p in range(2):
            transposed = chosen[p, 2].astype(F32).T.astype(BF16)
            for c in range(2):
                third[p * 128 + c * 64 : p * 128 + c * 64 + 64, c * 64 : c * 64 + 64] = transposed
        low = iota((GRID, 128), 1) < GRID
        for p in range(2):
            wedge = wedge_tile(slopes[p, 0], slopes[p, 1])
            wedge = jnp.concatenate([wedge] * 4, axis=1)
            first = chosen[p, 0]

            @pl.loop(0, 16, unroll=4)
            def _(chunk):
                lanes = pl.ds(pl.multiple_of(chunk * 256, 256), 256)
                volume = jnp.concatenate([particles[p, 0, :, lanes], particles[p, 1, :, lanes]], axis=1)
                along = jnp.dot(first, volume * wedge, preferred_element_type=F32)
                for j in range(2):
                    real = along[:, j * 128 : j * 128 + 128]
                    imag = along[:, 256 + j * 128 : 256 + j * 128 + 128]
                    even = jnp.where(low, real, pltpu.roll(imag, 64, 1))
                    odd = jnp.where(low, pltpu.roll(real, 64, 1), imag)
                    base = pl.multiple_of((chunk * 4 + j * 2) * PITCH, 8)
                    planes[p, pl.ds(base, GRID), :] = even
                    planes[p, pl.ds(base + PITCH, GRID), :] = odd

    for i in range(FIRST):
        parts = []
        for p in range(2):
            plane = planes[p, pl.ds(step * FIRST + i, GRID, stride=PITCH), :].astype(BF16)
            parts.append(jnp.dot(chosen[p, 1], plane, preferred_element_type=F32).astype(BF16))
        along = jnp.concatenate(parts, axis=1)
        full = jnp.dot(along, third[...], preferred_element_type=F32)
        for q in range(COLS):
            out[0, q * OWN + i * SECOND : q * OWN + (i + 1) * SECOND, :] = full[
                q * SECOND : (q + 1) * SECOND
            ]
    out[0, BLOCK : BLOCK + 8, :] = histogram_tile(bins, slopes)


def insert(particles, orient_bin, tilt_slope, table):
    return pl.pallas_call(
        insert_kernel,
        grid=(ROWS,),
        out_shape=jax.ShapeDtypeStruct((ROWS, BLOCK + 8, 128), F32),
        in_specs=[SMEM, SMEM, VMEM, pl.BlockSpec(memory_space=pl.ANY)],
        out_specs=pl.BlockSpec((1, BLOCK + 8, 128), lambda r: (r, 0, 0)),
        scratch_shapes=[
            pltpu.VMEM((2, GRID * PITCH, 128), F32),
            pltpu.VMEM((256, 128), BF16),
            pltpu.VMEM((2, 3, GRID, GRID), BF16),
            pltpu.SemaphoreType.DMA((2,)),
        ],
        compiler_params=pltpu.CompilerParams(vmem_limit_bytes=40 * 2**20),
        cost_estimate=pl.CostEstimate(flops=4 * 10**9, bytes_accessed=4 * 2**20, transcendentals=0),
        name="insert",
    )(orient_bin, tilt_slope, particles, table)


def row_sum_kernel(parts, out):
    total = parts[0]
    for k in range(1, ROWS):
        total = total + parts[k]
    for q in range(COLS):
        out[q, 0:OWN, :] = total[q * OWN : (q + 1) * OWN]
        out[q, OWN : OWN + 8, :] = total[BLOCK : BLOCK + 8]


def row_sum(parts):
    return pl.pallas_call(
        row_sum_kernel,
        out_shape=jax.ShapeDtypeStruct((COLS, OWN + 8, 128), F32),
        in_specs=[VMEM],
        out_specs=VMEM,
        name="row_sum",
    )(parts)


def quadrant_masks():
    shape = (GRID, SLOPES * 128)
    wave_first = iota(shape, 0) - CENTRE
    lane = iota(shape, 1)
    wave_third = lane % GRID - CENTRE
    quadrant = (lane // GRID) % 2
    slope = lane // 128 + SLOPE_MIN
    inside = 16 * jnp.abs(wave_third) <= slope * jnp.abs(wave_first)
    own = jnp.where(wave_first * wave_third >= 0, 0, 1) == quadrant
    return (inside & own).astype(BF16)


def spread_masks():
    shape = (128, SLOPES * 128)
    row, lane = iota(shape, 0), iota(shape, 1)
    return ((row % 32 == lane // 128) & ((row // 32) % 2 == (lane // GRID) % 2)).astype(BF16)


def divide_kernel(parts, grown, spread, second_sums, third, out, left):
    total = parts[0]
    for k in range(1, COLS):
        total = total + parts[k]
    counts = total[OWN : OWN + 8]
    low = iota((8, 128), 1) < GRID
    blocks = [jnp.where(low, counts, 0.0), jnp.where(low, 0.0, counts)] * FIRST
    counts = jnp.concatenate(blocks, axis=0).astype(BF16)
    held = jnp.zeros((FIRST * BINS, 128), F32)
    for k in range(SLOPES):
        lanes = slice(k * 128, k * 128 + 128)
        held += grown[:, lanes] * jnp.dot(counts, spread[:, lanes], preferred_element_type=F32)
    for k in range(BINS):
        sums = second_sums[k]
        for i in range(FIRST):
            value = sums * held[i * BINS + k : i * BINS + k + 1, :]
            upper = value.astype(BF16)
            left[i * SECOND : (i + 1) * SECOND, k * 128 : k * 128 + 128] = value
    value = left[...]
    upper = value.astype(BF16)
    lower = (value - upper.astype(F32)).astype(BF16)
    weight = jnp.dot(upper, third[...], preferred_element_type=F32)
    weight += jnp.dot(lower, third[...], preferred_element_type=F32)
    out[...] = total[0:OWN] / (weight + 1.0)


def divide(parts, grown, spread, second_sums, third):
    return pl.pallas_call(
        divide_kernel,
        out_shape=jax.ShapeDtypeStruct((OWN, 128), F32),
        in_specs=[VMEM] * 5,
        out_specs=VMEM,
        scratch_shapes=[pltpu.VMEM((OWN, BINS * 128), F32)],
        name="divide",
    )(parts, grown, spread, second_sums, third)


def spectra_kernel(place, own, other, out, rows):
    on_first = place[2] == 0
    a, b = own[...], other[...]
    cross = a * b
    own_power, other_power = a * a, b * b
    power_first = jnp.where(on_first, own_power, other_power)
    power_second = jnp.where(on_first, other_power, own_power)
    index = iota((OWN, 128), 0)
    first = index // SECOND + place[0] * FIRST - CENTRE
    second = index % SECOND + place[1] * SECOND - CENTRE
    third = iota((OWN, 128), 1) % GRID - CENTRE
    radius_sq = first * first + second * second + third * third
    rows[...] = jnp.zeros_like(rows)
    for k in range(SHELLS):
        least = 0 if k == 0 else (k + 3) ** 2
        inside = (radius_sq >= least) & (radius_sq < (k + 4) ** 2)
        for j, value in enumerate((cross, power_first, power_second)):
            rows[j * 32 + k : j * 32 + k + 1, :] = jnp.sum(
                jnp.where(inside, value, 0.0), axis=0, keepdims=True
            )
    rest = rows[...]
    ones = jnp.ones((8, 128), BF16)
    total = jnp.zeros((8, 128), F32)
    for _ in range(3):
        piece = rest.astype(BF16)
        rest = rest - piece.astype(F32)
        total += lax.dot_general(ones, piece, (((1,), (1,)), ((), ())), preferred_element_type=F32)
    for k in range(ROWS):
        out[k] = total


def spectra(place, own, other):
    return pl.pallas_call(
        spectra_kernel,
        out_shape=jax.ShapeDtypeStruct((ROWS, 8, 128), F32),
        in_specs=[SMEM, VMEM, VMEM],
        out_specs=VMEM,
        scratch_shapes=[pltpu.VMEM((128, 128), F32)],
        name="spectra",
    )(place, own, other)


def spread_kernel(parts, out):
    total = jnp.sum(parts[...], axis=0)
    for k in range(COLS):
        out[k] = total


def spread_sum(parts):
    return pl.pallas_call(
        spread_kernel,
        out_shape=jax.ShapeDtypeStruct((COLS, 8, 128), F32),
        in_specs=[VMEM],
        out_specs=VMEM,
        name="spread_sum",
    )(parts)


def finish_kernel(parts, counts, power, correlation):
    total = jnp.sum(parts[...], axis=0)
    cross = total[0:1, 0:SHELLS]
    first = total[0:1, 32 : 32 + SHELLS]
    second = total[0:1, 64 : 64 + SHELLS]
    power[0:1, :] = first / counts[...]
    power[1:2, :] = second / counts[...]
    correlation[...] = cross / jnp.sqrt(first * second + 1e-06)


def finish(parts, counts):
    return pl.pallas_call(
        finish_kernel,
        out_shape=(
            jax.ShapeDtypeStruct((2, SHELLS), F32),
            jax.ShapeDtypeStruct((1, SHELLS), F32),
        ),
        in_specs=[VMEM, VMEM],
        out_specs=(VMEM, VMEM),
        name="finish",
    )(parts, counts)


def shell_counts():
    wave = np.arange(GRID) - CENTRE
    radius_sq = (wave[:, None, None] ** 2 + wave[None, :, None] ** 2 + wave[None, None, :] ** 2).reshape(-1)
    bounds = np.arange(4, CENTRE) ** 2
    shell = np.searchsorted(bounds, radius_sq, side="right")
    inside = radius_sq < CENTRE * CENTRE
    return np.bincount(shell[inside], minlength=SHELLS).astype(np.float32)[None]


def local(particles, orient_bin, tilt_slope, table):
    row, col, half = lax.axis_index(ROW), lax.axis_index("col"), lax.axis_index("half")
    place = jnp.stack([row, col, half]).astype(jnp.int32)
    first = lax.dynamic_slice(table, (0, 0, row * FIRST, 0), (BINS, 1, FIRST, GRID))[:, 0]
    first = jnp.swapaxes(first, 0, 1).reshape(FIRST * BINS, GRID)
    grown = jnp.dot(first, quadrant_masks(), preferred_element_type=F32)
    second = lax.dynamic_slice(table, (0, 1, col * SECOND, 0), (BINS, 1, SECOND, GRID))[:, 0]
    second_sums = jnp.broadcast_to(
        jnp.sum(second.astype(F32), axis=2, keepdims=True), (BINS, SECOND, 128)
    )
    third = jnp.swapaxes(table[:, 2], 1, 2)
    third = jnp.broadcast_to(third[:, None, :, None, :], (BINS, 2, GRID, 2, GRID)).reshape(
        BINS * 128, 128
    )
    blocks = insert(particles, orient_bin, tilt_slope, table)
    parts = lax.all_to_all(blocks, ROW, 0, 0, tiled=True)
    blocks = row_sum(parts)
    parts = lax.all_to_all(blocks, "col", 0, 0, tiled=True)
    own = divide(parts, grown, spread_masks(), second_sums, third)
    other = lax.ppermute(own, "half", [(0, 1), (1, 0)])
    parts = lax.all_to_all(spectra(place, own, other), ROW, 0, 0, tiled=True)
    parts = lax.all_to_all(spread_sum(parts), "col", 0, 0, tiled=True)
    power, correlation = finish(parts, jnp.asarray(shell_counts()))
    half_maps = own.reshape(FIRST, SECOND, 2, GRID).transpose(2, 0, 1, 3)
    return half_maps.reshape(1, 2, FIRST, SECOND * GRID), power, correlation


def solution(mesh):
    torus = Mesh(
        mesh.devices.reshape(mesh.shape["half"], 4, 4, mesh.shape["col"]),
        ("half", "row_0", "row_1", "col"),
    )
    in_specs = (P(HALF_ROW_COL, None, None, None), P(HALF_ROW_COL), P(HALF_ROW_COL, None), P())
    out_specs = (P("half", None, ROW, "col"), P(), P("half", None))
    return jax.shard_map(local, mesh=torus, in_specs=in_specs, out_specs=out_specs, check_vma=False)
```

time: 171 us -> 111 us (0.65)
  blocking collectives: 35.8 us -> 13.6 us
  Pallas kernels: 0 us -> 22 us
  local copies, waits for them, and re-layouts: 28.5 us -> 13 us
  waiting for transfers between devices: 51.8 us -> 36.4 us
  other arithmetic: 17.3 us -> 2.94 us
  matrix products: 15.9 us -> 1.64 us
  loops' own time: 3.98 us -> 0 us
  starting transfers between devices: 16 us -> 19.3 us
    psum x3 -> x0, blocking collectives: 35.8 us -> none  [one_axis_at_a_time(): return functools.reduce(lax.psum, axes, x)]
    pallas_call x0 -> x6, Pallas kernels: none -> 22 us  [the longest x1 11.9 us: insert(): pl.pallas_call(insert_kernel, grid=(ROWS,), out_shape=jax.ShapeDtypeStruc...]
    reshape x6 -> x3, local copies, waits for them, and re-layouts: 20.7 us -> 2.78 us  [the longest x1 1.29 us: local(): jnp.broadcast_to(third[:, None, :, None, :], (BINS, 2, GRID, 2, GRID))]
    all_to_all x2 -> x3, waiting for transfers between devices: 50.8 us -> 35.6 us  [the longest x1 21.4 us: local(): parts = lax.all_to_all(blocks, ROW, 0, 0, tiled=True)]
    dot_general x5 -> x1, matrix products: 15.9 us -> 1.64 us  [local(): grown = jnp.dot(first, quadrant_masks(), preferred_element_type=F32)]
    all_to_all x0 -> x1, blocking collectives: none -> 13.6 us  [local(): parts = lax.all_to_all(spectra(place, own, other), ROW, 0, 0, tiled=True)]
    another operation x4 -> x1, other arithmetic: 8.98 us -> 0.59 us  [local(): place = jnp.stack([row, col, half]).astype(jnp.int32)]
    unnamed x6 -> x16, local copies, waits for them, and re-layouts: 0.04 us -> 6.61 us
  transfers between devices with their start and end apart: 3 -> 4, of which waited for: 3 -> 4; matrix products, arithmetic and copies ran while one was open for 0% -> 9% of each run, Pallas kernels for 0% -> 0%
where the time goes in v1:
time: 111 us; the launch traced here: 110 us
  waiting for transfers between devices  36.4 us (33%)
  Pallas kernels  22 us (20%)
  starting transfers between devices  19.3 us (17%)
  blocking collectives  13.6 us (12%)
  local copies, waits for them, and re-layouts  13 us (12%)
  other arithmetic  2.94 us (3%)
  matrix products  1.64 us (1%)
    all_to_all x1, waiting for transfers between devices, local(): parts = lax.all_to_all(blocks, ROW, 0, 0, tiled=True)  21.4 us
    all_to_all x1, blocking collectives, local(): parts = lax.all_to_all(spectra(place, own, other), ROW, 0, 0, tiled=True)  13.6 us
    pallas_call x1, Pallas kernels, insert(): pl.pallas_call(insert_kernel, grid=(ROWS,), out_shape=jax.ShapeDtypeStruc...  11.9 us
    all_to_all x1, starting transfers between devices, local(): parts = lax.all_to_all(blocks, 'col', 0, 0, tiled=True)  8.47 us
    all_to_all x1, waiting for transfers between devices, local(): parts = lax.all_to_all(blocks, 'col', 0, 0, tiled=True)  7.79 us
    all_to_all x1, starting transfers between devices, local(): parts = lax.all_to_all(blocks, ROW, 0, 0, tiled=True)  7.49 us
    unnamed x16, local copies, waits for them, and re-layouts  6.61 us
    all_to_all x1, waiting for transfers between devices, local(): parts = lax.all_to_all(spread_sum(parts), 'col', 0, 0, tiled=True)  6.44 us
  transfers between devices with their start and end apart: 4, of which 4 were waited for; matrix products, arithmetic and copies ran while one was open for 9% of the time, Pallas kernels for 0%

profile of v1, /device:TPU:2, one launch (start us, length us, event | category | flops | bytes accessed | tf_op | source)
XLA Modules:
  0.0 109.7 jit_solution(11001703646455709179)
XLA Ops:
  0.6 1.1 %copy-done = bf16[16,3,64,64]{3,2,1,0:T(8,128)(2,1)S(1)} copy-done((bf16[16,3,64,64]{3,2,1,0:T(8,128)(2,1)S(1)}, bf16[16,3,64,64]{3,2,1,0:T(8,128)(2,1)}, u32[]{:S(2)}) %copy-start) | copy-done | bytes 393240
  1.8 1.6 %copy-done.1 = bf16[2,2,64,4096]{3,2,1,0:T(8,128)(2,1)S(1)} copy-done((bf16[2,2,64,4096]{3,2,1,0:T(8,128)(2,1)S(1)}, bf16[2,2,64,4096]{3,2,1,0:T(8,128)(2,1)}, u32[]{:S(2)}) %copy-start.1) | copy-done | bytes 2097176
  4.7 11.9 %insert.1 = f32[16,264,128]{2,1,0:T(8,128)} custom-call(s32[2]{0:T(128)S(1)} %copy-done.3, s32[2,2]{1,0:T(2,128)S(1)} %copy-done.2, bf16[2,2,64,4096]{3,2,1,0:T(8,128)(2,1)S(1)} %copy-done.1, bf16[16,3,64,64]{3,2,1,0:T(8,128)(2,1)S(1)} %copy-done), custom_call_target="tpu_custom_call" | custom-call | flops 4000000000 | bytes 4194304 | tf_op jit(solution)/shard_map/insert/pallas_call | solution.py:107
  16.6 7.5 %all-to-all-start = ((f32[16,264,128]{2,1,0:T(8,128)}), f32[16,264,128]{2,1,0:T(8,128)S(1)}, u32[]{:S(2)}, u32[]{:S(2)}) async-start(f32[16,264,128]{2,1,0:T(8,128)} %insert.1), calls=%async_computation | async-start | bytes 4325376 | tf_op jit(solution)/shard_map/all_to_all | solution.py:304
  24.1 1.0 slice_bitcast_fusion
  26.1 0.9 broadcast_in_dim.9
  27.0 1.3 %reshape.22.third = bf16[2048,128]{1,0:T(8,128)(2,1)} reshape(bf16[16,2,64,2,64]{4,3,2,1,0:T(2,128)(2,1)S(1)} %broadcast_in_dim.9) | data formatting | bytes 1048576 | tf_op jit(solution)/shard_map/reshape | solution.py:300
  28.3 0.8 convert_reduce_fusion
  29.3 1.4 %fusion.4.spread = bf16[128,3712]{1,0:T(8,128)(2,1)} fusion(s32[3712]{0:T(1024)S(1)} %get-tuple-element.9, s32[3712]{0:T(1024)S(1)} %get-tuple-element.15, s32[128]{0:T(128)S(1)} %get-tuple-element.19, s32[128]{0:T(128)S(1)} %get-tuple-element.21, s32[3712]{0:T(1024)S(1)} %get-tuple-element.10, s32[3712]{0:T(1024)S(1)} %get-tuple-element.16, ...), kind=kLoop, calls=%fused_computation.15 | loop fusion | flops 14254080 | bytes 1019392 | tf_op jit(solution)/shard_map/convert_element_type | solution.py:159
  30.7 21.4 %all-to-all-done.parts = f32[16,264,128]{2,1,0:T(8,128)S(1)} async-done(((f32[16,264,128]{2,1,0:T(8,128)}), f32[16,264,128]{2,1,0:T(8,128)S(1)}, u32[]{:S(2)}, u32[]{:S(2)}) %all-to-all-start) | async-done | bytes 2162720 | tf_op jit(solution)/shard_map/all_to_all | solution.py:304
  52.1 1.4 %copy-done.4 = f32[16,264,128]{2,1,0:T(8,128)} copy-done((f32[16,264,128]{2,1,0:T(8,128)}, f32[16,264,128]{2,1,0:T(8,128)S(1)}, u32[]{:S(2)}) %copy-start.4) | copy-done | bytes 2162712
  53.4 2.4 %row_sum.1 = f32[8,40,128]{2,1,0:T(8,128)} custom-call(f32[16,264,128]{2,1,0:T(8,128)} %copy-done.4), custom_call_target="tpu_custom_call" | custom-call | tf_op jit(solution)/shard_map/row_sum/pallas_call | solution.py:135
  55.8 8.5 %all-to-all-start.1 = ((f32[8,40,128]{2,1,0:T(8,128)}), f32[8,40,128]{2,1,0:T(8,128)S(1)}, u32[]{:S(2)}, u32[]{:S(2)}) async-start(f32[8,40,128]{2,1,0:T(8,128)} %row_sum.1), calls=%async_computation.1 | async-start | bytes 327680 | tf_op jit(solution)/shard_map/all_to_all | solution.py:306
  64.3 1.6 %fusion.8.grown = f32[64,3712]{1,0:T(8,128)} fusion(bf16[64,64]{1,0:T(8,128)(2,1)S(1)} %bitcast.17, s32[3712]{0:T(1024)S(1)} %get-tuple-element.9, s32[3712]{0:T(1024)S(1)} %get-tuple-element.15, s32[64]{0:T(128)S(1)} %get-tuple-element.17, s32[64]{0:T(128)S(1)} %get-tuple-element.18, s32[3712]{0:T(1024)S(1)} %get-tuple-element.10, ...), kind=kOutput, calls=%fused_computation.27 | convolution fusion | flops 36347904 | bytes 1059200 | tf_op jit(solution)/shard_map/dot_general | solution.py:294
  65.9 7.8 %all-to-all-done.1.parts = f32[8,40,128]{2,1,0:T(8,128)S(1)} async-done(((f32[8,40,128]{2,1,0:T(8,128)}), f32[8,40,128]{2,1,0:T(8,128)S(1)}, u32[]{:S(2)}, u32[]{:S(2)}) %all-to-all-start.1) | async-done | bytes 163872 | tf_op jit(solution)/shard_map/all_to_all | solution.py:306
  74.4 3.0 %divide.1.own = f32[32,128]{1,0:T(8,128)} custom-call(f32[8,40,128]{2,1,0:T(8,128)} %copy-done.5, f32[64,3712]{1,0:T(8,128)} %fusion.8.grown, bf16[128,3712]{1,0:T(8,128)(2,1)} %fusion.4.spread, f32[16,8,128]{2,1,0:T(8,128)} %broadcast_in_dim.8.second_sums, bf16[2048,128]{1,0:T(8,128)(2,1)} %reshape.22.third), custom_call_target="tpu_custom_call" | custom-call | tf_op jit(solution)/shard_map/divide/pallas_call | solution.py:189
  78.0 0.8 collective-permute-done.other
  79.4 1.8 %spectra.1 = f32[16,8,128]{2,1,0:T(8,128)} custom-call(s32[3]{0:T(128)} %pad_add_fusion.place, f32[32,128]{1,0:T(8,128)} %divide.1.own, f32[32,128]{1,0:T(8,128)} %copy-done.7), custom_call_target="tpu_custom_call" | custom-call | tf_op jit(solution)/shard_map/spectra/pallas_call | solution.py:231
  81.2 13.6 %all_to_all.20.parts = f32[16,8,128]{2,1,0:T(8,128)} all-to-all(f32[16,8,128]{2,1,0:T(8,128)} %spectra.1), channel_id=1, replica_groups=mesh['half'=2,'row_0'=4,'row_1'=4,'col'=8] {'row_0','row_1'}, dimensions={0} | all-to-all | bytes 131072 | tf_op jit(solution)/shard_map/all_to_all | solution.py:309
  94.8 1.5 %spread_sum.1 = f32[8,8,128]{2,1,0:T(8,128)} custom-call(f32[16,8,128]{2,1,0:T(8,128)} %all_to_all.20.parts), custom_call_target="tpu_custom_call" | custom-call | tf_op jit(solution)/shard_map/spread_sum/pallas_call | solution.py:248
  96.3 3.3 %all-to-all-start.3 = ((f32[8,8,128]{2,1,0:T(8,128)}), f32[8,8,128]{2,1,0:T(8,128)S(1)}, u32[]{:S(2)}, u32[]{:S(2)}) async-start(f32[8,8,128]{2,1,0:T(8,128)} %spread_sum.1), calls=%async_computation.3 | async-start | bytes 65536 | tf_op jit(solution)/shard_map/all_to_all | solution.py:310
  99.6 0.8 reshape.23
  101.1 6.4 %all-to-all-done.3.parts = f32[8,8,128]{2,1,0:T(8,128)S(1)} async-done(((f32[8,8,128]{2,1,0:T(8,128)}), f32[8,8,128]{2,1,0:T(8,128)S(1)}, u32[]{:S(2)}, u32[]{:S(2)}) %all-to-all-start.3) | async-done | bytes 32800 | tf_op jit(solution)/shard_map/all_to_all | solution.py:310
  108.2 1.5 %finish.1 = (f32[2,29]{1,0:T(2,128)}, f32[1,29]{1,0:T(1,128)}) custom-call(f32[8,8,128]{2,1,0:T(8,128)} %copy-done.6, f32[1,29]{1,0:T(1,128)} %constant.148.clone.counts), custom_call_target="tpu_custom_call" | custom-call | tf_op jit(solution)/shard_map/finish/pallas_call | solution.py:268
  (30 shorter events, 5.5 us)
Async XLA Ops:
  0.6 1.1 %copy-start = (bf16[16,3,64,64]{3,2,1,0:T(8,128)(2,1)S(1)}, bf16[16,3,64,64]{3,2,1,0:T(8,128)(2,1)}, u32[]{:S(2)}) copy-start(bf16[16,3,64,64]{3,2,1,0:T(8,128)(2,1)} %table.1) | copy-start | bytes 1179652
  1.8 1.6 %copy-start.1 = (bf16[2,2,64,4096]{3,2,1,0:T(8,128)(2,1)S(1)}, bf16[2,2,64,4096]{3,2,1,0:T(8,128)(2,1)}, u32[]{:S(2)}) copy-start(bf16[2,2,64,4096]{3,2,1,0:T(8,128)(2,1)} %particles.1) | copy-start | bytes 6291460
  3.4 0.7 copy-start.2
  4.0 0.7 copy-start.3
  16.6 35.5 %all-to-all-start = ((f32[16,264,128]{2,1,0:T(8,128)}), f32[16,264,128]{2,1,0:T(8,128)S(1)}, u32[]{:S(2)}, u32[]{:S(2)}) async-start(f32[16,264,128]{2,1,0:T(8,128)} %insert.1), calls=%async_computation | async-start | bytes 4325376 | tf_op jit(solution)/shard_map/all_to_all | solution.py:304
  52.1 1.4 %copy-start.4 = (f32[16,264,128]{2,1,0:T(8,128)}, f32[16,264,128]{2,1,0:T(8,128)S(1)}, u32[]{:S(2)}) copy-start(f32[16,264,128]{2,1,0:T(8,128)S(1)} %all-to-all-done.parts) | copy-start | bytes 6488068
  55.8 17.9 %all-to-all-start.1 = ((f32[8,40,128]{2,1,0:T(8,128)}), f32[8,40,128]{2,1,0:T(8,128)S(1)}, u32[]{:S(2)}, u32[]{:S(2)}) async-start(f32[8,40,128]{2,1,0:T(8,128)} %row_sum.1), calls=%async_computation.1 | async-start | bytes 327680 | tf_op jit(solution)/shard_map/all_to_all | solution.py:306
  73.7 0.7 copy-start.5
  77.4 1.4 %collective-permute-start = (f32[32,128]{1,0:T(8,128)}, f32[32,128]{1,0:T(8,128)S(1)}, u32[]{:S(2)}, u32[]{:S(2)}) collective-permute-start(f32[32,128]{1,0:T(8,128)} %divide.1.own), channel_id=1, source_target_pairs={{0,128},{128,0},{1,129},{129,1},{2,130},{130,2},{3,131},{131,3},{4... | collective-permute-start | bytes 49160 | tf_op jit(solution)/shard_map/ppermute | solution.py:308
  78.8 0.6 copy-start.7
  96.3 11.3 %all-to-all-start.3 = ((f32[8,8,128]{2,1,0:T(8,128)}), f32[8,8,128]{2,1,0:T(8,128)S(1)}, u32[]{:S(2)}, u32[]{:S(2)}) async-start(f32[8,8,128]{2,1,0:T(8,128)} %spread_sum.1), calls=%async_computation.3 | async-start | bytes 65536 | tf_op jit(solution)/shard_map/all_to_all | solution.py:310
  107.6 0.6 copy-start.6

commit v2 on v1

v2 whole, which is shorter than its diff:
```python
import functools

import jax
import jax.numpy as jnp
import numpy as np
from jax import lax
from jax.experimental import pallas as pl
from jax.experimental.pallas import tpu as pltpu
from jax.sharding import Mesh
from jax.sharding import PartitionSpec as P

SHELLS = 29
GRID = 64
CENTRE = GRID // 2
BINS = 16
ROWS = 16
COLS = 8
FIRST = GRID // ROWS
SECOND = GRID // COLS
SLOPE_MIN = 12
SLOPES = 29
OWN = FIRST * SECOND
ROW = ("row_0", "row_1")
HALF_ROW_COL = ("half", "row_0", "row_1", "col")
F32 = jnp.float32
BF16 = jnp.bfloat16
VMEM = pl.BlockSpec(memory_space=pltpu.VMEM)
SMEM = pl.BlockSpec(memory_space=pltpu.SMEM)
ANY = pl.BlockSpec(memory_space=pl.ANY)
SMALL = pltpu.CompilerParams(vmem_limit_bytes=6 * 2**20)
PARTS = 1


def iota(shape, dim):
    return lax.broadcasted_iota(jnp.int32, shape, dim)


def wedge_tile(slope_first, slope_second):
    wave_first = iota((GRID, 128), 0) - CENTRE
    wave_third = iota((GRID, 128), 1) % GRID - CENTRE
    limit = jnp.where(wave_first * wave_third >= 0, slope_first, slope_second)
    inside = 16 * jnp.abs(wave_third) <= limit * jnp.abs(wave_first)
    return jnp.where(inside, 1.0, 0.0).astype(BF16)


def histogram_tile(bins, slopes):
    row, lane = iota((8, 128), 0), iota((8, 128), 1)
    total = jnp.zeros((8, 128), F32)
    for p in range(2):
        for quadrant in range(2):
            place = (bins[p] // 8) * 64 + quadrant * 32 + slopes[p, quadrant] - SLOPE_MIN
            total += jnp.where((row == bins[p] % 8) & (lane == place), 1.0, 0.0)
    return total


def insert_kernel(part, bins, slopes, particles, table, out, volume, planes, third, chosen, blocks, sem_in, sem_out):
    count = FIRST // PARTS
    height = ROWS * count
    pitch = height + 8
    tables = [
        pltpu.make_async_copy(table.at[bins[p]], chosen.at[p], sem_in.at[4 + p]) for p in range(2)
    ]
    volumes = [
        [
            pltpu.make_async_copy(particles.at[p, c], volume.at[p, c], sem_in.at[p * 2 + c])
            for c in range(2)
        ]
        for p in range(2)
    ]
    for copy in (*tables, *volumes[0], *volumes[1]):
        copy.start()
    third[...] = jnp.zeros_like(third)
    row = iota((height, GRID), 0)
    chosen_row = (row // count) * FIRST + part * count + row % count
    select = (iota((height, GRID), 1) == chosen_row).astype(BF16)
    wedges = [
        jnp.concatenate([wedge_tile(slopes[p, 0], slopes[p, 1])] * 4, axis=1) for p in range(2)
    ]
    for copy in tables:
        copy.wait()
    for p in range(2):
        transposed = chosen[p, 2].astype(F32).T.astype(BF16)
        for c in range(2):
            third[p * 128 + c * 64 : p * 128 + c * 64 + 64, c * 64 : c * 64 + 64] = transposed
    low = iota((height, 128), 1) < GRID
    for p in range(2):
        first = chosen[p, 0]
        if PARTS > 1:
            first = jnp.dot(select, first, preferred_element_type=F32).astype(BF16)
        for copy in volumes[p]:
            copy.wait()

        @pl.loop(0, 16, unroll=4)
        def _(chunk):
            lanes = pl.ds(pl.multiple_of(chunk * 256, 256), 256)
            both = jnp.concatenate([volume[p, 0, :, lanes], volume[p, 1, :, lanes]], axis=1)
            along = jnp.dot(first, both * wedges[p], preferred_element_type=F32)
            for j in range(2):
                real = along[:, j * 128 : j * 128 + 128]
                imag = along[:, 256 + j * 128 : 256 + j * 128 + 128]
                even = jnp.where(low, real, pltpu.roll(imag, 64, 1))
                odd = jnp.where(low, pltpu.roll(real, 64, 1), imag)
                base = pl.multiple_of((chunk * 4 + j * 2) * pitch, 8)
                planes[p, pl.ds(base, height), :] = even
                planes[p, pl.ds(base + pitch, height), :] = odd

    last = part == PARTS - 1
    size = COLS * count * SECOND
    if last:
        tile = histogram_tile(bins, slopes)
        for r in range(ROWS):
            blocks[r, size : size + 8, :] = tile
    group = 8 // count

    @pl.loop(0, ROWS // group)
    def _(step):
        for g in range(group):
            r = step * group + g
            for i in range(count):
                parts = []
                for p in range(2):
                    plane = planes[p, pl.ds(r * count + i, GRID, stride=pitch), :].astype(BF16)
                    along = jnp.dot(chosen[p, 1], plane, preferred_element_type=F32)
                    parts.append(along.astype(BF16))
                full = jnp.dot(
                    jnp.concatenate(parts, axis=1), third[...], preferred_element_type=F32
                )
                for q in range(COLS):
                    start = (q * count + i) * SECOND
                    blocks[r, start : start + SECOND, :] = full[q * SECOND : (q + 1) * SECOND]
        span = pl.ds(step * group, group)
        pltpu.make_async_copy(blocks.at[span], out.at[span], sem_out).start()

    pltpu.make_async_copy(blocks, out, sem_out).wait()


def insert(part, particles, orient_bin, tilt_slope, table):
    count = FIRST // PARTS
    rows = COLS * count * SECOND + (8 if part == PARTS - 1 else 0)
    return pl.pallas_call(
        functools.partial(insert_kernel, part),
        out_shape=jax.ShapeDtypeStruct((ROWS, rows, 128), F32),
        in_specs=[SMEM, SMEM, ANY, ANY],
        out_specs=ANY,
        scratch_shapes=[
            pltpu.VMEM((2, 2, GRID, GRID * GRID), BF16),
            pltpu.VMEM((2, GRID * (ROWS * count + 8), 128), F32),
            pltpu.VMEM((256, 128), BF16),
            pltpu.VMEM((2, 3, GRID, GRID), BF16),
            pltpu.VMEM((ROWS, rows, 128), F32),
            pltpu.SemaphoreType.DMA((6,)),
            pltpu.SemaphoreType.DMA,
        ],
        cost_estimate=pl.CostEstimate(flops=10**9, bytes_accessed=4 * 2**20, transcendentals=0),
        name=f"insert_{part}",
    )(orient_bin, tilt_slope, particles, table)


def row_sum_kernel(*refs):
    *parts, out = refs
    span = OWN // PARTS
    for n, part in enumerate(parts):
        total = part[0]
        for k in range(1, ROWS):
            total = total + part[k]
        for q in range(COLS):
            out[q, n * span : (n + 1) * span, :] = total[q * span : (q + 1) * span]
        if n == PARTS - 1:
            for q in range(COLS):
                out[q, OWN : OWN + 8, :] = total[COLS * span : COLS * span + 8]


def row_sum(*parts):
    return pl.pallas_call(
        row_sum_kernel,
        out_shape=jax.ShapeDtypeStruct((COLS, OWN + 8, 128), F32),
        in_specs=[VMEM] * len(parts),
        out_specs=VMEM,
        compiler_params=SMALL,
        name="row_sum",
    )(*parts)


def quadrant_masks():
    shape = (GRID, SLOPES * 128)
    wave_first = iota(shape, 0) - CENTRE
    lane = iota(shape, 1)
    wave_third = lane % GRID - CENTRE
    quadrant = (lane // GRID) % 2
    slope = lane // 128 + SLOPE_MIN
    inside = 16 * jnp.abs(wave_third) <= slope * jnp.abs(wave_first)
    own = jnp.where(wave_first * wave_third >= 0, 0, 1) == quadrant
    return (inside & own).astype(BF16)


def divide_kernel(parts, grown, second_sums, third, out, left):
    total = parts[0]
    for k in range(1, COLS):
        total = total + parts[k]
    counts = total[OWN : OWN + 8]
    low = iota((8, 128), 1) < GRID
    held = [[jnp.zeros((8, 128), F32) for _ in range(2)] for _ in range(FIRST)]
    for k in range(SLOPES):
        for upper in range(2):
            lane = upper * 64 + k
            spread = jnp.where(
                low,
                jnp.broadcast_to(counts[:, lane : lane + 1], (8, 128)),
                jnp.broadcast_to(counts[:, lane + 32 : lane + 33], (8, 128)),
            )
            for i in range(FIRST):
                start = i * BINS + upper * 8
                held[i][upper] += spread * grown[start : start + 8, k * 128 : k * 128 + 128]
    for k in range(BINS):
        sums = jnp.broadcast_to(second_sums[:, k : k + 1], (8, 128))
        for i in range(FIRST):
            value = sums * held[i][k // 8][k % 8 : k % 8 + 1, :]
            upper = value.astype(BF16)
            lower = (value - upper.astype(F32)).astype(BF16)
            lanes = slice(k * 128, k * 128 + 128)
            left[i * SECOND : (i + 1) * SECOND, lanes] = upper.astype(F32)
            left[OWN + i * SECOND : OWN + (i + 1) * SECOND, lanes] = lower.astype(F32)
    weight = jnp.dot(left[...].astype(BF16), third[...], preferred_element_type=F32)
    out[...] = total[0:OWN] / (weight[0:OWN] + weight[OWN:] + 1.0)


def divide(parts, grown, second_sums, third):
    return pl.pallas_call(
        divide_kernel,
        out_shape=jax.ShapeDtypeStruct((OWN, 128), F32),
        in_specs=[VMEM] * 4,
        out_specs=VMEM,
        scratch_shapes=[pltpu.VMEM((2 * OWN, BINS * 128), F32)],
        compiler_params=SMALL,
        name="divide",
    )(parts, grown, second_sums, third)


def spectra_kernel(own, other, out, maps, rows):
    on_first = lax.axis_index("half") == 0
    a, b = own[...], other[...]
    cross = a * b
    own_power, other_power = a * a, b * b
    power_first = jnp.where(on_first, own_power, other_power)
    power_second = jnp.where(on_first, other_power, own_power)
    index = iota((OWN, 128), 0)
    first = index // SECOND + lax.axis_index(ROW) * FIRST - CENTRE
    second = index % SECOND + lax.axis_index("col") * SECOND - CENTRE
    third = iota((OWN, 128), 1) % GRID - CENTRE
    radius_sq = first * first + second * second + third * third
    rows[...] = jnp.zeros_like(rows)
    for k in range(SHELLS):
        least = 0 if k == 0 else (k + 3) ** 2
        inside = (radius_sq >= least) & (radius_sq < (k + 4) ** 2)
        for j, value in enumerate((cross, power_first, power_second)):
            rows[j * 32 + k : j * 32 + k + 1, :] = jnp.sum(
                jnp.where(inside, value, 0.0), axis=0, keepdims=True
            )
    rest = rows[...]
    ones = jnp.ones((8, 128), BF16)
    total = jnp.zeros((8, 128), F32)
    for _ in range(3):
        piece = rest.astype(BF16)
        rest = rest - piece.astype(F32)
        total += lax.dot_general(ones, piece, (((1,), (1,)), ((), ())), preferred_element_type=F32)
    for k in range(ROWS):
        out[k] = total
    low = iota((SECOND // 2, 128), 1) < GRID
    for i in range(FIRST):
        even = own[pl.ds(i * SECOND, SECOND // 2, stride=2), :]
        odd = own[pl.ds(i * SECOND + 1, SECOND // 2, stride=2), :]
        real = jnp.where(low, even, pltpu.roll(odd, 64, 1))
        imag = jnp.where(low, pltpu.roll(even, 64, 1), odd)
        for j in range(SECOND // 2):
            lanes = slice(j * 128, j * 128 + 128)
            maps[0, 0, i : i + 1, lanes] = real[j : j + 1]
            maps[0, 1, i : i + 1, lanes] = imag[j : j + 1]


def spectra(own, other):
    return pl.pallas_call(
        spectra_kernel,
        out_shape=(
            jax.ShapeDtypeStruct((ROWS, 8, 128), F32),
            jax.ShapeDtypeStruct((1, 2, FIRST, SECOND * GRID), F32),
        ),
        in_specs=[VMEM, VMEM],
        out_specs=(VMEM, VMEM),
        scratch_shapes=[pltpu.VMEM((128, 128), F32)],
        compiler_params=SMALL,
        name="spectra",
    )(own, other)


def spread_kernel(parts, out):
    total = jnp.sum(parts[...], axis=0)
    for k in range(COLS):
        out[k] = total


def spread_sum(parts):
    return pl.pallas_call(
        spread_kernel,
        out_shape=jax.ShapeDtypeStruct((COLS, 8, 128), F32),
        in_specs=[VMEM],
        out_specs=VMEM,
        compiler_params=SMALL,
        name="spread_sum",
    )(parts)


def finish_kernel(parts, counts, power, correlation):
    total = jnp.sum(parts[...], axis=0)
    cross = total[0:1, 0:SHELLS]
    first = total[0:1, 32 : 32 + SHELLS]
    second = total[0:1, 64 : 64 + SHELLS]
    power[0:1, :] = first / counts[...]
    power[1:2, :] = second / counts[...]
    correlation[...] = cross / jnp.sqrt(first * second + 1e-06)


def finish(parts, counts):
    return pl.pallas_call(
        finish_kernel,
        out_shape=(
            jax.ShapeDtypeStruct((2, SHELLS), F32),
            jax.ShapeDtypeStruct((1, SHELLS), F32),
        ),
        in_specs=[VMEM, VMEM],
        out_specs=(VMEM, VMEM),
        compiler_params=SMALL,
        name="finish",
    )(parts, counts)


def shell_counts():
    wave = np.arange(GRID) - CENTRE
    radius_sq = (wave[:, None, None] ** 2 + wave[None, :, None] ** 2 + wave[None, None, :] ** 2).reshape(-1)
    bounds = np.arange(4, CENTRE) ** 2
    shell = np.searchsorted(bounds, radius_sq, side="right")
    inside = radius_sq < CENTRE * CENTRE
    return np.bincount(shell[inside], minlength=SHELLS).astype(np.float32)[None]


def local(particles, orient_bin, tilt_slope, table):
    row, col = lax.axis_index(ROW), lax.axis_index("col")
    first = lax.dynamic_slice(table, (0, 0, row * FIRST, 0), (BINS, 1, FIRST, GRID))[:, 0]
    first = jnp.swapaxes(first, 0, 1).reshape(FIRST * BINS, GRID)
    grown = jnp.dot(first, quadrant_masks(), preferred_element_type=F32)
    second = lax.dynamic_slice(table, (0, 1, col * SECOND, 0), (BINS, 1, SECOND, GRID))[:, 0]
    second_sums = jnp.sum(second.astype(F32), axis=2).T
    third = jnp.swapaxes(table[:, 2], 1, 2)
    third = jnp.broadcast_to(third[:, None, :, None, :], (BINS, 2, GRID, 2, GRID)).reshape(
        BINS * 128, 128
    )
    parts = []
    for n in range(PARTS):
        blocks = insert(n, particles, orient_bin, tilt_slope, table)
        parts.append(lax.all_to_all(blocks, ROW, 0, 0, tiled=True))
    parts, grown, second_sums, third = lax.optimization_barrier(
        (parts, grown, second_sums, third)
    )
    blocks = row_sum(*parts)
    parts = lax.all_to_all(blocks, "col", 0, 0, tiled=True)
    own = divide(parts, grown, second_sums, third)
    other = lax.ppermute(own, "half", [(0, 1), (1, 0)])
    sums, half_maps = spectra(own, other)
    parts = lax.all_to_all(sums, ROW, 0, 0, tiled=True)
    parts = lax.all_to_all(spread_sum(parts), "col", 0, 0, tiled=True)
    power, correlation = finish(parts, jnp.asarray(shell_counts()))
    return half_maps, power, correlation


def solution(mesh):
    torus = Mesh(
        mesh.devices.reshape(mesh.shape["half"], 4, 4, mesh.shape["col"]),
        ("half", "row_0", "row_1", "col"),
    )
    in_specs = (P(HALF_ROW_COL, None, None, None), P(HALF_ROW_COL), P(HALF_ROW_COL, None), P())
    out_specs = (P("half", None, ROW, "col"), P(), P("half", None))
    return jax.shard_map(local, mesh=torus, in_specs=in_specs, out_specs=out_specs, check_vma=False)
```

time: 111 us -> 89.9 us (0.81)
  blocking collectives: 13.6 us -> 41.1 us
  waiting for transfers between devices: 36.4 us -> 20.2 us
  starting transfers between devices: 19.3 us -> 7.58 us
  Pallas kernels: 22 us -> 10.9 us
  local copies, waits for them, and re-layouts: 13 us -> 6.35 us
  other arithmetic: 2.94 us -> 0.89 us
    all_to_all x1 -> x3, blocking collectives: 13.6 us -> 41.1 us  [the longest x1 17.8 us: local(): parts = lax.all_to_all(blocks, 'col', 0, 0, tiled=True)]
    all_to_all x3 -> x1, waiting for transfers between devices: 35.6 us -> 19 us  [local(): parts.append(lax.all_to_all(blocks, ROW, 0, 0, tiled=True))]
    all_to_all x3 -> x1, starting transfers between devices: 19.3 us -> 7.49 us  [local(): parts.append(lax.all_to_all(blocks, ROW, 0, 0, tiled=True))]
    unnamed x16 -> x4, local copies, waits for them, and re-layouts: 6.61 us -> 0.01 us
    pallas_call x2, Pallas kernels: 13.7 us -> 9.62 us  [the longest x1 8.69 us: insert(): pl.pallas_call(functools.partial(insert_kernel, part), out_shape=jax.Shap...]
    pallas_call x1, Pallas kernels: 2.96 us -> 0.48 us  [divide(): pl.pallas_call(divide_kernel, out_shape=jax.ShapeDtypeStruct((OWN, 128),...]
    pallas_call x1, Pallas kernels: 2.38 us -> 0.1 us  [row_sum(): pl.pallas_call(row_sum_kernel, out_shape=jax.ShapeDtypeStruct((COLS, OWN...]
    reshape x2 -> x0, local copies, waits for them, and re-layouts: 1.49 us -> none  [the longest x1 0.8 us: local(): half_maps = own.reshape(FIRST, SECOND, 2, GRID).transpose(2, 0, 1, 3)]
  transfers between devices with their start and end apart: 4 -> 2, of which waited for: 4 -> 2; matrix products, arithmetic and copies ran while one was open for 9% -> 10% of each run, Pallas kernels for 0% -> 0%
where the time goes in v2:
time: 89.9 us; the launch traced here: 89.4 us
  blocking collectives  41.1 us (46%)
  waiting for transfers between devices  20.2 us (22%)
  Pallas kernels  10.9 us (12%)
  starting transfers between devices  7.58 us (8%)
  local copies, waits for them, and re-layouts  6.35 us (7%)
  matrix products  1.65 us (2%)
    all_to_all x1, waiting for transfers between devices, local(): parts.append(lax.all_to_all(blocks, ROW, 0, 0, tiled=True))  19 us
    all_to_all x1, blocking collectives, local(): parts = lax.all_to_all(blocks, 'col', 0, 0, tiled=True)  17.8 us
    all_to_all x1, blocking collectives, local(): parts = lax.all_to_all(sums, ROW, 0, 0, tiled=True)  12.8 us
    all_to_all x1, blocking collectives, local(): parts = lax.all_to_all(spread_sum(parts), 'col', 0, 0, tiled=True)  10.4 us
    pallas_call x1, Pallas kernels, insert(): pl.pallas_call(functools.partial(insert_kernel, part), out_shape=jax.Shap...  8.69 us
    all_to_all x1, starting transfers between devices, local(): parts.append(lax.all_to_all(blocks, ROW, 0, 0, tiled=True))  7.49 us
    reshape x1, local copies, waits for them, and re-layouts, local(): jnp.broadcast_to(third[:, None, :, None, :], (BINS, 2, GRID, 2, GRID))  2.41 us
    broadcast_in_dim x1, local copies, waits for them, and re-layouts, local(): jnp.broadcast_to(third[:, None, :, None, :], (BINS, 2, GRID, 2, GRID))  1.92 us
  transfers between devices with their start and end apart: 2, of which 2 were waited for; matrix products, arithmetic and copies ran while one was open for 10% of the time, Pallas kernels for 0%

profile of v2, /device:TPU:2, one launch (start us, length us, event | category | flops | bytes accessed | tf_op | source)
XLA Modules:
  0.0 89.4 jit_solution(733082318953202900)
XLA Ops:
  0.6 8.7 %insert_0.1 = f32[16,264,128]{2,1,0:T(8,128)} custom-call(s32[2]{0:T(128)} %bins.1, s32[2,2]{1,0:T(2,128)} %slopes.1, bf16[2,2,64,4096]{3,2,1,0:T(8,128)(2,1)} %particles.1, bf16[16,3,64,64]{3,2,1,0:T(8,128)(2,1)} %table.1), custom_call_target="tpu_custom_call" | custom-call | flops 1000000000 | bytes 4194304 | tf_op jit(solution)/shard_map/insert_0/pallas_call | solution.py:140
  9.3 7.5 %all-to-all-start = ((f32[16,264,128]{2,1,0:T(8,128)}), f32[16,264,128]{2,1,0:T(8,128)S(1)}, u32[]{:S(2)}, u32[]{:S(2)}) async-start(f32[16,264,128]{2,1,0:T(8,128)} %insert_0.1), calls=%async_computation | async-start | bytes 4325376 | tf_op jit(solution)/shard_map/all_to_all | solution.py:359
  16.8 0.8 constant_dynamic-slice_fusion
  17.6 0.9 convert_reduce_fusion
  18.5 0.1 copy.12
  18.5 1.0 %slice_bitcast_fusion = bf16[16,64,64]{1,2,0:T(8,128)(2,1)S(1)} fusion(bf16[16,3,64,64]{3,2,1,0:T(8,128)(2,1)} %table.1), kind=kLoop, calls=%fused_computation.32 | loop fusion | bytes 262144 | tf_op jit(solution)/shard_map/transpose | solution.py:352
  19.5 0.2 copy.13
  19.7 1.9 %broadcast_in_dim.6 = bf16[16,2,64,2,64]{4,3,2,1,0:T(2,128)(2,1)} broadcast(bf16[16,64,64]{2,1,0:T(8,128)(2,1)S(1)} %copy.13), dimensions={0,2,4} | broadcast | bytes 655360 | tf_op jit(solution)/shard_map/broadcast_in_dim | solution.py:353
  21.6 2.4 %reshape.15.third = bf16[2048,128]{1,0:T(8,128)(2,1)S(1)} reshape(bf16[16,2,64,2,64]{4,3,2,1,0:T(2,128)(2,1)} %broadcast_in_dim.6) | data formatting | bytes 1048576 | tf_op jit(solution)/shard_map/reshape | solution.py:353
  24.1 1.6 %fusion.3.grown = f32[64,3712]{1,0:T(8,128)} fusion(bf16[64,64]{1,0:T(8,128)(2,1)S(1)} %bitcast.12, s32[3712]{0:T(1024)S(1)} %get-tuple-element.19, s32[3712]{0:T(1024)S(1)} %get-tuple-element.25, s32[64]{0:T(128)S(1)} %get-tuple-element.27, s32[64]{0:T(128)S(1)} %get-tuple-element.28, s32[3712]{0:T(1024)S(1)} %get-tuple-element.20, ...), kind=kOutput, calls=%fused_computation.11 | convolution fusion | flops 36347904 | bytes 1059200 | tf_op jit(solution)/shard_map/dot_general | solution.py:349
  25.8 19.0 %all-to-all-done.refs_0_ = f32[16,264,128]{2,1,0:T(8,128)S(1)} async-done(((f32[16,264,128]{2,1,0:T(8,128)}), f32[16,264,128]{2,1,0:T(8,128)S(1)}, u32[]{:S(2)}, u32[]{:S(2)}) %all-to-all-start) | async-done | bytes 2162720 | tf_op jit(solution)/shard_map/all_to_all | solution.py:359
  44.8 0.0 copy-start
  44.8 0.0 copy-start.1
  44.8 0.1 row_sum.1
  44.9 17.8 %all_to_all.20.parts = f32[8,40,128]{2,1,0:T(8,128)S(1)} all-to-all(f32[8,40,128]{2,1,0:T(8,128)S(1)} %row_sum.1), channel_id=1, replica_groups=mesh['half'=2,'row_0'=4,'row_1'=4,'col'=8] {'col'}, dimensions={0} | all-to-all | bytes 327680 | tf_op jit(solution)/shard_map/all_to_all | solution.py:364
  62.7 0.0 copy-done
  62.7 0.5 divide.1.own
  63.2 0.1 collective-permute-start
  63.3 1.2 %collective-permute-done.other = f32[32,128]{1,0:T(8,128)S(1)} collective-permute-done((f32[32,128]{1,0:T(8,128)S(1)}, f32[32,128]{1,0:T(8,128)S(1)}, u32[]{:S(2)}, u32[]{:S(2)}) %collective-permute-start) | collective-permute-done | bytes 16416 | tf_op jit(solution)/shard_map/ppermute | solution.py:366
  64.5 0.9 %spectra.1 = (f32[16,8,128]{2,1,0:T(8,128)S(1)}, f32[1,2,4,512]{3,2,1,0:T(4,128)}) custom-call(f32[32,128]{1,0:T(8,128)S(1)} %divide.1.own, f32[32,128]{1,0:T(8,128)S(1)} %collective-permute-done.other), custom_call_target="tpu_custom_call" | custom-call | tf_op jit(solution)/shard_map/spectra/pallas_call | solution.py:281
  65.4 12.8 %all_to_all.21.parts = f32[16,8,128]{2,1,0:T(8,128)S(1)} all-to-all(f32[16,8,128]{2,1,0:T(8,128)S(1)} %get-tuple-element.16), channel_id=1, replica_groups=mesh['half'=2,'row_0'=4,'row_1'=4,'col'=8] {'row_0','row_1'}, dimensions={0} | all-to-all | bytes 131072 | tf_op jit(solution)/shard_map/all_to_all | solution.py:368
  78.3 10.4 %all_to_all.22.parts = f32[8,8,128]{2,1,0:T(8,128)S(1)} all-to-all(f32[8,8,128]{2,1,0:T(8,128)S(1)} %spread_sum.1), channel_id=1, replica_groups=mesh['half'=2,'row_0'=4,'row_1'=4,'col'=8] {'col'}, dimensions={0} | all-to-all | bytes 65536 | tf_op jit(solution)/shard_map/all_to_all | solution.py:369
  88.7 0.0 copy-done.1
  88.7 0.7 finish.1
  (8 shorter events, 0.1 us)
Async XLA Ops:
  9.3 35.5 %all-to-all-start = ((f32[16,264,128]{2,1,0:T(8,128)}), f32[16,264,128]{2,1,0:T(8,128)S(1)}, u32[]{:S(2)}, u32[]{:S(2)}) async-start(f32[16,264,128]{2,1,0:T(8,128)} %insert_0.1), calls=%async_computation | async-start | bytes 4325376 | tf_op jit(solution)/shard_map/all_to_all | solution.py:359
  44.8 17.9 %copy-start = (f32[64,3712]{1,0:T(8,128)S(1)}, f32[64,3712]{1,0:T(8,128)}, u32[]{:S(2)}) copy-start(f32[64,3712]{1,0:T(8,128)} %fusion.3.grown) | copy-start | bytes 2850820
  44.8 43.9 %copy-start.1 = (f32[1,29]{1,0:T(1,128)S(1)}, f32[1,29]{1,0:T(1,128)}, u32[]{:S(2)}) copy-start(f32[1,29]{1,0:T(1,128)} %constant.85.clone.counts) | copy-start | bytes 352
  63.2 1.3 %collective-permute-start = (f32[32,128]{1,0:T(8,128)S(1)}, f32[32,128]{1,0:T(8,128)S(1)}, u32[]{:S(2)}, u32[]{:S(2)}) collective-permute-start(f32[32,128]{1,0:T(8,128)S(1)} %divide.1.own), channel_id=1, source_target_pairs={{0,128},{128,0},{1,129},{129,1},{2,130},{130,2},{3,131},{131,3},{4... | collective-permute-start | bytes 49160 | tf_op jit(solution)/shard_map/ppermute | solution.py:366

commit v3 on v2

--- a/solution.py
+++ b/solution.py
@@ -19,8 +19,12 @@
 SECOND = GRID // COLS
 SLOPE_MIN = 12
 SLOPES = 29
+SIDE = 4
+PITCH = 72
+BLOCK = FIRST * GRID
 OWN = FIRST * SECOND
 ROW = ("row_0", "row_1")
+HALF_ROW = ("half", "row_0", "row_1")
 HALF_ROW_COL = ("half", "row_0", "row_1", "col")
 F32 = jnp.float32
 BF16 = jnp.bfloat16
@@ -28,7 +32,6 @@
 SMEM = pl.BlockSpec(memory_space=pltpu.SMEM)
 ANY = pl.BlockSpec(memory_space=pl.ANY)
 SMALL = pltpu.CompilerParams(vmem_limit_bytes=6 * 2**20)
-PARTS = 1
 
 
 def iota(shape, dim):
@@ -53,10 +56,7 @@
     return total
 
 
-def insert_kernel(part, bins, slopes, particles, table, out, volume, planes, third, chosen, blocks, sem_in, sem_out):
-    count = FIRST // PARTS
-    height = ROWS * count
-    pitch = height + 8
+def insert_kernel(bins, slopes, particles, table, out, volume, planes, third, chosen, blocks, sem_in, sem_out):
     tables = [
         pltpu.make_async_copy(table.at[bins[p]], chosen.at[p], sem_in.at[4 + p]) for p in range(2)
     ]
@@ -70,23 +70,20 @@
     for copy in (*tables, *volumes[0], *volumes[1]):
         copy.start()
     third[...] = jnp.zeros_like(third)
-    row = iota((height, GRID), 0)
-    chosen_row = (row // count) * FIRST + part * count + row % count
-    select = (iota((height, GRID), 1) == chosen_row).astype(BF16)
     wedges = [
         jnp.concatenate([wedge_tile(slopes[p, 0], slopes[p, 1])] * 4, axis=1) for p in range(2)
     ]
+    counts = histogram_tile(bins, slopes)
+    for k in range(SIDE):
+        blocks[k, SIDE * BLOCK : SIDE * BLOCK + 8, :] = counts
     for copy in tables:
         copy.wait()
     for p in range(2):
         transposed = chosen[p, 2].astype(F32).T.astype(BF16)
         for c in range(2):
             third[p * 128 + c * 64 : p * 128 + c * 64 + 64, c * 64 : c * 64 + 64] = transposed
-    low = iota((height, 128), 1) < GRID
+    low = iota((GRID, 128), 1) < GRID
     for p in range(2):
-        first = chosen[p, 0]
-        if PARTS > 1:
-            first = jnp.dot(select, first, preferred_element_type=F32).astype(BF16)
         for copy in volumes[p]:
             copy.wait()
 
@@ -94,91 +91,90 @@
         def _(chunk):
             lanes = pl.ds(pl.multiple_of(chunk * 256, 256), 256)
             both = jnp.concatenate([volume[p, 0, :, lanes], volume[p, 1, :, lanes]], axis=1)
-            along = jnp.dot(first, both * wedges[p], preferred_element_type=F32)
+            along = jnp.dot(chosen[p, 0], both * wedges[p], preferred_element_type=F32)
             for j in range(2):
                 real = along[:, j * 128 : j * 128 + 128]
                 imag = along[:, 256 + j * 128 : 256 + j * 128 + 128]
                 even = jnp.where(low, real, pltpu.roll(imag, 64, 1))
                 odd = jnp.where(low, pltpu.roll(real, 64, 1), imag)
-                base = pl.multiple_of((chunk * 4 + j * 2) * pitch, 8)
-                planes[p, pl.ds(base, height), :] = even
-                planes[p, pl.ds(base + pitch, height), :] = odd
-
-    last = part == PARTS - 1
-    size = COLS * count * SECOND
-    if last:
-        tile = histogram_tile(bins, slopes)
-        for r in range(ROWS):
-            blocks[r, size : size + 8, :] = tile
-    group = 8 // count
-
-    @pl.loop(0, ROWS // group)
+                base = pl.multiple_of((chunk * 4 + j * 2) * PITCH, 8)
+                planes[p, pl.ds(base, GRID), :] = even
+                planes[p, pl.ds(base + PITCH, GRID), :] = odd
+
+    on_first = lax.axis_index("half") == 0
+
+    @pl.loop(0, ROWS // 2)
     def _(step):
-        for g in range(group):
-            r = step * group + g
-            for i in range(count):
+        outer = step // 2
+        for g in range(2):
+            inner = (step % 2) * 2 + g
+            row = jnp.where(on_first, outer * SIDE + inner, inner * SIDE + outer)
+            for i in range(FIRST):
                 parts = []
                 for p in range(2):
-                    plane = planes[p, pl.ds(r * count + i, GRID, stride=pitch), :].astype(BF16)
+                    plane = planes[p, pl.ds(row * FIRST + i, GRID, stride=PITCH), :].astype(BF16)
                     along = jnp.dot(chosen[p, 1], plane, preferred_element_type=F32)
                     parts.append(along.astype(BF16))
                 full = jnp.dot(
                     jnp.concatenate(parts, axis=1), third[...], preferred_element_type=F32
                 )
                 for q in range(COLS):
-                    start = (q * count + i) * SECOND
-                    blocks[r, start : start + SECOND, :] = full[q * SECOND : (q + 1) * SECOND]
-        span = pl.ds(step * group, group)
-        pltpu.make_async_copy(blocks.at[span], out.at[span], sem_out).start()
+                    start = inner * BLOCK + (q * FIRST + i) * SECOND
+                    start = pl.multiple_of(start, 8)
+                    blocks[outer, pl.ds(start, SECOND), :] = full[q * SECOND : (q + 1) * SECOND]
+
+        @pl.when(step % 2 == 1)
+        def _():
+            pltpu.make_async_copy(blocks.at[outer], out.at[outer], sem_out).start()
 
     pltpu.make_async_copy(blocks, out, sem_out).wait()
 
 
-def insert(part, particles, orient_bin, tilt_slope, table):
-    count = FIRST // PARTS
-    rows = COLS * count * SECOND + (8 if part == PARTS - 1 else 0)
-    return pl.pallas_call(
-        functools.partial(insert_kernel, part),
-        out_shape=jax.ShapeDtypeStruct((ROWS, rows, 128), F32),
+def insert(particles, orient_bin, tilt_slope, table):
+    rows = SIDE * BLOCK + 8
+    return pl.pallas_call(
+        insert_kernel,
+        out_shape=jax.ShapeDtypeStruct((SIDE, rows, 128), F32),
         in_specs=[SMEM, SMEM, ANY, ANY],
         out_specs=ANY,
         scratch_shapes=[
             pltpu.VMEM((2, 2, GRID, GRID * GRID), BF16),
-            pltpu.VMEM((2, GRID * (ROWS * count + 8), 128), F32),
+            pltpu.VMEM((2, GRID * PITCH, 128), F32),
             pltpu.VMEM((256, 128), BF16),
             pltpu.VMEM((2, 3, GRID, GRID), BF16),
-            pltpu.VMEM((ROWS, rows, 128), F32),
+            pltpu.VMEM((SIDE, rows, 128), F32),
             pltpu.SemaphoreType.DMA((6,)),
             pltpu.SemaphoreType.DMA,
         ],
         cost_estimate=pl.CostEstimate(flops=10**9, bytes_accessed=4 * 2**20, transcendentals=0),
-        name=f"insert_{part}",
+        name="insert",
     )(orient_bin, tilt_slope, particles, table)
 
 
-def row_sum_kernel(*refs):
-    *parts, out = refs
-    span = OWN // PARTS
-    for n, part in enumerate(parts):
-        total = part[0]
-        for k in range(1, ROWS):
-            total = total + part[k]
-        for q in range(COLS):
-            out[q, n * span : (n + 1) * span, :] = total[q * span : (q + 1) * span]
-        if n == PARTS - 1:
-            for q in range(COLS):
-                out[q, OWN : OWN + 8, :] = total[COLS * span : COLS * span + 8]
-
-
-def row_sum(*parts):
-    return pl.pallas_call(
-        row_sum_kernel,
-        out_shape=jax.ShapeDtypeStruct((COLS, OWN + 8, 128), F32),
-        in_specs=[VMEM] * len(parts),
+def reduce_kernel(owners, size, parts, out):
+    senders = parts.shape[0]
+    tail = pl.ds(owners * size, 8)
+    counts = parts[0, tail, :]
+    for k in range(1, senders):
+        counts = counts + parts[k, tail, :]
+    for n in range(owners):
+        span = pl.ds(n * size, size)
+        total = parts[0, span, :]
+        for k in range(1, senders):
+            total = total + parts[k, span, :]
+        out[n, 0:size, :] = total
+        out[n, size : size + 8, :] = counts
+
+
+def reduce(parts, owners, size):
+    return pl.pallas_call(
+        functools.partial(reduce_kernel, owners, size),
+        out_shape=jax.ShapeDtypeStruct((owners, size + 8, 128), F32),
+        in_specs=[VMEM],
         out_specs=VMEM,
         compiler_params=SMALL,
-        name="row_sum",
-    )(*parts)
+        name=f"reduce_{owners}",
+    )(parts)
 
 
 def quadrant_masks():
@@ -333,6 +329,13 @@
     )(parts, counts)
 
 
+def groups(swapped):
+    along_x = [[x * SIDE + y for x in range(SIDE)] for y in range(SIDE)]
+    along_y = [[x * SIDE + y for y in range(SIDE)] for x in range(SIDE)]
+    first, second = (along_y, along_x) if swapped else (along_x, along_y)
+    return first + [[ROWS + k for k in group] for group in second]
+
+
 def shell_counts():
     wave = np.arange(GRID) - CENTRE
     radius_sq = (wave[:, None, None] ** 2 + wave[None, :, None] ** 2 + wave[None, None, :] ** 2).reshape(-1)
@@ -353,14 +356,14 @@
     third = jnp.broadcast_to(third[:, None, :, None, :], (BINS, 2, GRID, 2, GRID)).reshape(
         BINS * 128, 128
     )
-    parts = []
-    for n in range(PARTS):
-        blocks = insert(n, particles, orient_bin, tilt_slope, table)
-        parts.append(lax.all_to_all(blocks, ROW, 0, 0, tiled=True))
+    blocks = insert(particles, orient_bin, tilt_slope, table)
+    parts = lax.all_to_all(blocks, HALF_ROW, 0, 0, axis_index_groups=groups(False), tiled=True)
     parts, grown, second_sums, third = lax.optimization_barrier(
         (parts, grown, second_sums, third)
     )
-    blocks = row_sum(*parts)
+    blocks = reduce(parts, SIDE, BLOCK)
+    parts = lax.all_to_all(blocks, HALF_ROW, 0, 0, axis_index_groups=groups(True), tiled=True)
+    blocks = reduce(parts, COLS, OWN)
     parts = lax.all_to_all(blocks, "col", 0, 0, tiled=True)
     own = divide(parts, grown, second_sums, third)
     other = lax.ppermute(own, "half", [(0, 1), (1, 0)])

time: 89.9 us -> 84.7 us (0.942)
  waiting for transfers between devices: 20.2 us -> 7.33 us
  blocking collectives: 41.1 us -> 50.2 us
  starting transfers between devices: 7.58 us -> 5.92 us
    all_to_all x1, waiting for transfers between devices: 19 us -> 6.16 us  [local(): lax.all_to_all(blocks, HALF_ROW, 0, 0, axis_index_groups=groups(False), t...]
    all_to_all x0 -> x1, blocking collectives: none -> 11.6 us  [local(): lax.all_to_all(blocks, HALF_ROW, 0, 0, axis_index_groups=groups(True), ti...]
    all_to_all x1, blocking collectives: 12.8 us -> 10.6 us  [local(): parts = lax.all_to_all(sums, ROW, 0, 0, tiled=True)]
    all_to_all x1, starting transfers between devices: 7.49 us -> 5.83 us  [local(): lax.all_to_all(blocks, HALF_ROW, 0, 0, axis_index_groups=groups(False), t...]
    pallas_call x2 -> x3, Pallas kernels: 8.8 us -> 8.9 us  [the longest x1 8.78 us: insert(): pl.pallas_call(insert_kernel, out_shape=jax.ShapeDtypeStruct((SIDE, rows,...]
  transfers between devices with their start and end apart: 2 -> 2, of which waited for: 2 -> 2; matrix products, arithmetic and copies ran while one was open for 10% -> 11% of each run, Pallas kernels for 0% -> 0%
where the time goes in v3:
time: 84.7 us; the launch traced here: 84.2 us
  blocking collectives  50.2 us (59%)
  Pallas kernels  11.1 us (13%)
  waiting for transfers between devices  7.33 us (9%)
  local copies, waits for them, and re-layouts  6.37 us (8%)
  starting transfers between devices  5.92 us (7%)
  matrix products  1.65 us (2%)
  other arithmetic  0.89 us (1%)
    all_to_all x1, blocking collectives, local(): parts = lax.all_to_all(blocks, 'col', 0, 0, tiled=True)  17.7 us
    all_to_all x1, blocking collectives, local(): lax.all_to_all(blocks, HALF_ROW, 0, 0, axis_index_groups=groups(True), ti...  11.6 us
    all_to_all x1, blocking collectives, local(): parts = lax.all_to_all(sums, ROW, 0, 0, tiled=True)  10.6 us
    all_to_all x1, blocking collectives, local(): parts = lax.all_to_all(spread_sum(parts), 'col', 0, 0, tiled=True)  10.4 us
    pallas_call x1, Pallas kernels, insert(): pl.pallas_call(insert_kernel, out_shape=jax.ShapeDtypeStruct((SIDE, rows,...  8.78 us
    all_to_all x1, waiting for transfers between devices, local(): lax.all_to_all(blocks, HALF_ROW, 0, 0, axis_index_groups=groups(False), t...  6.16 us
    all_to_all x1, starting transfers between devices, local(): lax.all_to_all(blocks, HALF_ROW, 0, 0, axis_index_groups=groups(False), t...  5.83 us
    reshape x1, local copies, waits for them, and re-layouts, local(): jnp.broadcast_to(third[:, None, :, None, :], (BINS, 2, GRID, 2, GRID))  2.41 us
  transfers between devices with their start and end apart: 2, of which 2 were waited for; matrix products, arithmetic and copies ran while one was open for 11% of the time, Pallas kernels for 0%

profile of v3, /device:TPU:2, one launch (start us, length us, event | category | flops | bytes accessed | tf_op | source)
XLA Modules:
  0.0 84.2 jit_solution(8385632164151757598)
XLA Ops:
  0.6 8.8 %insert.1 = f32[4,1032,128]{2,1,0:T(8,128)} custom-call(s32[2]{0:T(128)} %bins.1, s32[2,2]{1,0:T(2,128)} %slopes.1, bf16[2,2,64,4096]{3,2,1,0:T(8,128)(2,1)} %particles.1, bf16[16,3,64,64]{3,2,1,0:T(8,128)(2,1)} %table.1), custom_call_target="tpu_custom_call" | custom-call | flops 1000000000 | bytes 4194304 | tf_op jit(solution)/shard_map/insert/pallas_call | solution.py:135
  9.4 5.8 %all-to-all-start = ((f32[4,1032,128]{2,1,0:T(8,128)}), f32[4,1032,128]{2,1,0:T(8,128)S(1)}, u32[]{:S(2)}, u32[]{:S(2)}) async-start(f32[4,1032,128]{2,1,0:T(8,128)} %insert.1), calls=%async_computation | async-start | bytes 4227072 | tf_op jit(solution)/shard_map/all_to_all | solution.py:360
  15.2 0.8 constant_dynamic-slice_fusion
  16.0 0.9 %convert_reduce_fusion = f32[16,8]{1,0:T(8,128)S(1)} fusion(bf16[16,3,64,64]{3,2,1,0:T(8,128)(2,1)} %table.1, s32[]{:T(128)S(6)} %select_n.35), kind=kLoop, calls=%fused_computation.33 | loop fusion | flops 16256 | bytes 16900 | tf_op jit(solution)/shard_map/reduce_sum | solution.py:354
  16.9 0.1 copy.12
  17.0 1.0 %slice_bitcast_fusion = bf16[16,64,64]{1,2,0:T(8,128)(2,1)S(1)} fusion(bf16[16,3,64,64]{3,2,1,0:T(8,128)(2,1)} %table.1), kind=kLoop, calls=%fused_computation.32 | loop fusion | bytes 262144 | tf_op jit(solution)/shard_map/transpose | solution.py:355
  17.9 0.2 copy.13
  18.1 1.9 %broadcast_in_dim.6 = bf16[16,2,64,2,64]{4,3,2,1,0:T(2,128)(2,1)} broadcast(bf16[16,64,64]{2,1,0:T(8,128)(2,1)S(1)} %copy.13), dimensions={0,2,4} | broadcast | bytes 655360 | tf_op jit(solution)/shard_map/broadcast_in_dim | solution.py:356
  20.1 2.4 %reshape.15.third = bf16[2048,128]{1,0:T(8,128)(2,1)S(1)} reshape(bf16[16,2,64,2,64]{4,3,2,1,0:T(2,128)(2,1)} %broadcast_in_dim.6) | data formatting | bytes 1048576 | tf_op jit(solution)/shard_map/reshape | solution.py:356
  22.6 1.7 %fusion.3.grown = f32[64,3712]{1,0:T(8,128)} fusion(bf16[64,64]{1,0:T(8,128)(2,1)S(1)} %bitcast.12, s32[3712]{0:T(1024)S(1)} %get-tuple-element.19, s32[3712]{0:T(1024)S(1)} %get-tuple-element.25, s32[64]{0:T(128)S(1)} %get-tuple-element.27, s32[64]{0:T(128)S(1)} %get-tuple-element.28, s32[3712]{0:T(1024)S(1)} %get-tuple-element.20, ...), kind=kOutput, calls=%fused_computation.11 | convolution fusion | flops 36347904 | bytes 1059200 | tf_op jit(solution)/shard_map/dot_general | solution.py:352
  24.2 6.2 %all-to-all-done.parts = f32[4,1032,128]{2,1,0:T(8,128)S(1)} async-done(((f32[4,1032,128]{2,1,0:T(8,128)}), f32[4,1032,128]{2,1,0:T(8,128)S(1)}, u32[]{:S(2)}, u32[]{:S(2)}) %all-to-all-start) | async-done | bytes 2113568 | tf_op jit(solution)/shard_map/all_to_all | solution.py:360
  30.4 0.1 reduce_4.1
  30.5 0.0 copy-start.1
  30.5 11.6 %all_to_all.25.parts = f32[4,264,128]{2,1,0:T(8,128)S(1)} all-to-all(f32[4,264,128]{2,1,0:T(8,128)S(1)} %reduce_4.1), channel_id=1, replica_groups={{0,8,16,24},{32,40,48,56},{64,72,80,88},{96,104,112,120},{128,160,192,2..., dimensions={0} | all-to-all | bytes 1081344 | tf_op jit(solution)/shard_map/all_to_all | solution.py:365
  42.1 17.7 %all_to_all.26.parts = f32[8,40,128]{2,1,0:T(8,128)S(1)} all-to-all(f32[8,40,128]{2,1,0:T(8,128)S(1)} %reduce_8.1), channel_id=1, replica_groups=mesh['half'=2,'row_0'=4,'row_1'=4,'col'=8] {'col'}, dimensions={0} | all-to-all | bytes 327680 | tf_op jit(solution)/shard_map/all_to_all | solution.py:367
  59.8 0.0 copy-done
  59.8 0.5 divide.1.own
  60.3 0.1 collective-permute-start
  60.4 1.2 %collective-permute-done.other = f32[32,128]{1,0:T(8,128)S(1)} collective-permute-done((f32[32,128]{1,0:T(8,128)S(1)}, f32[32,128]{1,0:T(8,128)S(1)}, u32[]{:S(2)}, u32[]{:S(2)}) %collective-permute-start) | collective-permute-done | bytes 16416 | tf_op jit(solution)/shard_map/ppermute | solution.py:369
  61.6 0.9 %spectra.1 = (f32[16,8,128]{2,1,0:T(8,128)S(1)}, f32[1,2,4,512]{3,2,1,0:T(4,128)}) custom-call(f32[32,128]{1,0:T(8,128)S(1)} %divide.1.own, f32[32,128]{1,0:T(8,128)S(1)} %collective-permute-done.other), custom_call_target="tpu_custom_call" | custom-call | tf_op jit(solution)/shard_map/spectra/pallas_call | solution.py:277
  62.5 10.6 %all_to_all.27.parts = f32[16,8,128]{2,1,0:T(8,128)S(1)} all-to-all(f32[16,8,128]{2,1,0:T(8,128)S(1)} %get-tuple-element.16), channel_id=1, replica_groups=mesh['half'=2,'row_0'=4,'row_1'=4,'col'=8] {'row_0','row_1'}, dimensions={0} | all-to-all | bytes 131072 | tf_op jit(solution)/shard_map/all_to_all | solution.py:371
  73.1 10.4 %all_to_all.28.parts = f32[8,8,128]{2,1,0:T(8,128)S(1)} all-to-all(f32[8,8,128]{2,1,0:T(8,128)S(1)} %spread_sum.1), channel_id=1, replica_groups=mesh['half'=2,'row_0'=4,'row_1'=4,'col'=8] {'col'}, dimensions={0} | all-to-all | bytes 65536 | tf_op jit(solution)/shard_map/all_to_all | solution.py:372
  83.5 0.0 copy-done.1
  83.5 0.7 finish.1
  (10 shorter events, 0.1 us)
Async XLA Ops:
  9.4 21.0 %all-to-all-start = ((f32[4,1032,128]{2,1,0:T(8,128)}), f32[4,1032,128]{2,1,0:T(8,128)S(1)}, u32[]{:S(2)}, u32[]{:S(2)}) async-start(f32[4,1032,128]{2,1,0:T(8,128)} %insert.1), calls=%async_computation | async-start | bytes 4227072 | tf_op jit(solution)/shard_map/all_to_all | solution.py:360
  30.4 29.4 %copy-start = (f32[64,3712]{1,0:T(8,128)S(1)}, f32[64,3712]{1,0:T(8,128)}, u32[]{:S(2)}) copy-start(f32[64,3712]{1,0:T(8,128)} %fusion.3.grown) | copy-start | bytes 2850820
  30.5 53.0 %copy-start.1 = (f32[1,29]{1,0:T(1,128)S(1)}, f32[1,29]{1,0:T(1,128)}, u32[]{:S(2)}) copy-start(f32[1,29]{1,0:T(1,128)} %constant.85.clone.counts) | copy-start | bytes 352
  60.3 1.3 %collective-permute-start = (f32[32,128]{1,0:T(8,128)S(1)}, f32[32,128]{1,0:T(8,128)S(1)}, u32[]{:S(2)}, u32[]{:S(2)}) collective-permute-start(f32[32,128]{1,0:T(8,128)S(1)} %divide.1.own), channel_id=1, source_target_pairs={{0,128},{128,0},{1,129},{129,1},{2,130},{130,2},{3,131},{131,3},{4... | collective-permute-start | bytes 49160 | tf_op jit(solution)/shard_map/ppermute | solution.py:369

commit v4 on v3

--- a/solution.py
+++ b/solution.py
@@ -29,8 +29,7 @@
 F32 = jnp.float32
 BF16 = jnp.bfloat16
 VMEM = pl.BlockSpec(memory_space=pltpu.VMEM)
-SMEM = pl.BlockSpec(memory_space=pltpu.SMEM)
-ANY = pl.BlockSpec(memory_space=pl.ANY)
+HBM = pl.BlockSpec(memory_space=pltpu.HBM)
 SMALL = pltpu.CompilerParams(vmem_limit_bytes=6 * 2**20)
 
 
@@ -56,29 +55,62 @@
     return total
 
 
-def insert_kernel(bins, slopes, particles, table, out, volume, planes, third, chosen, blocks, sem_in, sem_out):
-    tables = [
-        pltpu.make_async_copy(table.at[bins[p]], chosen.at[p], sem_in.at[4 + p]) for p in range(2)
+def compute_slab(shift, planes, second, third, counts, out):
+    on_first = lax.axis_index("half") == 0
+    mine = jnp.where(on_first, lax.axis_index("row_0"), lax.axis_index("row_1"))
+    outer = lax.rem(mine + shift, SIDE)
+    out[SIDE * BLOCK : SIDE * BLOCK + 8, :] = counts
+
+    @pl.loop(0, SIDE // 2)
+    def _(step):
+        for g in range(2):
+            inner = step * 2 + g
+            row = jnp.where(on_first, outer * SIDE + inner, inner * SIDE + outer)
+            for i in range(FIRST):
+                parts = []
+                for p in range(2):
+                    plane = planes[p, pl.ds(row * FIRST + i, GRID, stride=PITCH), :].astype(BF16)
+                    along = jnp.dot(second[p], plane, preferred_element_type=F32)
+                    parts.append(along.astype(BF16))
+                full = jnp.dot(
+                    jnp.concatenate(parts, axis=1), third[...], preferred_element_type=F32
+                )
+                for q in range(COLS):
+                    start = inner * BLOCK + (q * FIRST + i) * SECOND
+                    start = pl.multiple_of(start, 8)
+                    out[pl.ds(start, SECOND), :] = full[q * SECOND : (q + 1) * SECOND]
+
+
+def first_kernel(bins_in, slopes_in, particles, table, planes, second, third, counts, out, volume, chosen, bins, slopes, sem):
+    scalars = [
+        pltpu.make_async_copy(bins_in, bins, sem.at[6]),
+        pltpu.make_async_copy(slopes_in, slopes, sem.at[7]),
     ]
     volumes = [
         [
-            pltpu.make_async_copy(particles.at[p, c], volume.at[p, c], sem_in.at[p * 2 + c])
+            pltpu.make_async_copy(particles.at[p, c], volume.at[p, c], sem.at[p * 2 + c])
             for c in range(2)
         ]
         for p in range(2)
     ]
-    for copy in (*tables, *volumes[0], *volumes[1]):
+    for copy in (*scalars, *volumes[0], *volumes[1]):
         copy.start()
     third[...] = jnp.zeros_like(third)
+    for copy in scalars:
+        copy.wait()
+    tables = [
+        pltpu.make_async_copy(table.at[bins[p]], chosen.at[p], sem.at[4 + p]) for p in range(2)
+    ]
+    for copy in tables:
+        copy.start()
     wedges = [
         jnp.concatenate([wedge_tile(slopes[p, 0], slopes[p, 1])] * 4, axis=1) for p in range(2)
     ]
-    counts = histogram_tile(bins, slopes)
-    for k in range(SIDE):
-        blocks[k, SIDE * BLOCK : SIDE * BLOCK + 8, :] = counts
+    counts[...] = histogram_tile(bins, slopes)
     for copy in tables:
         copy.wait()
     for p in range(2):
+        second[p] = chosen[p, 1]
         transposed = chosen[p, 2].astype(F32).T.astype(BF16)
         for c in range(2):
             third[p * 128 + c * 64 : p * 128 + c * 64 + 64, c * 64 : c * 64 + 64] = transposed
@@ -101,54 +133,78 @@
                 planes[p, pl.ds(base, GRID), :] = even
                 planes[p, pl.ds(base + PITCH, GRID), :] = odd
 
-    on_first = lax.axis_index("half") == 0
-
-    @pl.loop(0, ROWS // 2)
-    def _(step):
-        outer = step // 2
-        for g in range(2):
-            inner = (step % 2) * 2 + g
-            row = jnp.where(on_first, outer * SIDE + inner, inner * SIDE + outer)
-            for i in range(FIRST):
-                parts = []
-                for p in range(2):
-                    plane = planes[p, pl.ds(row * FIRST + i, GRID, stride=PITCH), :].astype(BF16)
-                    along = jnp.dot(chosen[p, 1], plane, preferred_element_type=F32)
-                    parts.append(along.astype(BF16))
-                full = jnp.dot(
-                    jnp.concatenate(parts, axis=1), third[...], preferred_element_type=F32
-                )
-                for q in range(COLS):
-                    start = inner * BLOCK + (q * FIRST + i) * SECOND
-                    start = pl.multiple_of(start, 8)
-                    blocks[outer, pl.ds(start, SECOND), :] = full[q * SECOND : (q + 1) * SECOND]
-
-        @pl.when(step % 2 == 1)
-        def _():
-            pltpu.make_async_copy(blocks.at[outer], out.at[outer], sem_out).start()
-
-    pltpu.make_async_copy(blocks, out, sem_out).wait()
-
-
-def insert(particles, orient_bin, tilt_slope, table):
-    rows = SIDE * BLOCK + 8
-    return pl.pallas_call(
-        insert_kernel,
-        out_shape=jax.ShapeDtypeStruct((SIDE, rows, 128), F32),
-        in_specs=[SMEM, SMEM, ANY, ANY],
-        out_specs=ANY,
+    compute_slab(2, planes, second, third, counts[...], out)
+
+
+SLAB = jax.ShapeDtypeStruct((SIDE * BLOCK + 8, 128), F32)
+
+
+def first_slab(particles, orient_bin, tilt_slope, table):
+    return pl.pallas_call(
+        first_kernel,
+        out_shape=(
+            jax.ShapeDtypeStruct((2, GRID * PITCH, 128), F32),
+            jax.ShapeDtypeStruct((2, GRID, GRID), BF16),
+            jax.ShapeDtypeStruct((256, 128), BF16),
+            jax.ShapeDtypeStruct((8, 128), F32),
+            SLAB,
+        ),
+        in_specs=[HBM] * 4,
+        out_specs=(VMEM,) * 5,
         scratch_shapes=[
             pltpu.VMEM((2, 2, GRID, GRID * GRID), BF16),
-            pltpu.VMEM((2, GRID * PITCH, 128), F32),
-            pltpu.VMEM((256, 128), BF16),
             pltpu.VMEM((2, 3, GRID, GRID), BF16),
-            pltpu.VMEM((SIDE, rows, 128), F32),
-            pltpu.SemaphoreType.DMA((6,)),
-            pltpu.SemaphoreType.DMA,
+            pltpu.SMEM((2,), jnp.int32),
+            pltpu.SMEM((2, 2), jnp.int32),
+            pltpu.SemaphoreType.DMA((8,)),
         ],
+        compiler_params=pltpu.CompilerParams(vmem_limit_bytes=20 * 2**20),
         cost_estimate=pl.CostEstimate(flops=10**9, bytes_accessed=4 * 2**20, transcendentals=0),
-        name="insert",
+        name="first_slab",
     )(orient_bin, tilt_slope, particles, table)
+
+
+def slabs_kernel(planes, second, third, counts, *outs):
+    for shift, out in zip((1, 3, 0), outs, strict=True):
+        compute_slab(shift, planes, second, third, counts[...], out)
+
+
+def other_slabs(planes, second, third, counts):
+    return pl.pallas_call(
+        slabs_kernel,
+        out_shape=(SLAB,) * 3,
+        in_specs=[VMEM] * 4,
+        out_specs=(VMEM,) * 3,
+        compiler_params=SMALL,
+        cost_estimate=pl.CostEstimate(flops=10**9, bytes_accessed=2**20, transcendentals=0),
+        name="other_slabs",
+    )(planes, second, third, counts)
+
+
+def gather_kernel(own, *refs):
+    *others, out = refs
+    tail = pl.ds(SIDE * BLOCK, 8)
+    counts = own[tail, :]
+    for other in others:
+        counts = counts + other[tail, :]
+    for n in range(SIDE):
+        span = pl.ds(n * BLOCK, BLOCK)
+        total = own[span, :]
+        for other in others:
+            total = total + other[span, :]
+        out[n, 0:BLOCK, :] = total
+        out[n, BLOCK : BLOCK + 8, :] = counts
+
+
+def gather(*parts):
+    return pl.pallas_call(
+        gather_kernel,
+        out_shape=jax.ShapeDtypeStruct((SIDE, BLOCK + 8, 128), F32),
+        in_specs=[VMEM] * len(parts),
+        out_specs=VMEM,
+        compiler_params=SMALL,
+        name="gather",
+    )(*parts)
 
 
 def reduce_kernel(owners, size, parts, out):
@@ -173,7 +229,6 @@
         in_specs=[VMEM],
         out_specs=VMEM,
         compiler_params=SMALL,
-        name=f"reduce_{owners}",
     )(parts)
 
 
@@ -329,11 +384,20 @@
     )(parts, counts)
 
 
-def groups(swapped):
+def groups():
     along_x = [[x * SIDE + y for x in range(SIDE)] for y in range(SIDE)]
     along_y = [[x * SIDE + y for y in range(SIDE)] for x in range(SIDE)]
-    first, second = (along_y, along_x) if swapped else (along_x, along_y)
-    return first + [[ROWS + k for k in group] for group in second]
+    return along_y + [[ROWS + k for k in group] for group in along_x]
+
+
+def shifted(shift):
+    pairs = []
+    for x in range(SIDE):
+        for y in range(SIDE):
+            source = x * SIDE + y
+            pairs.append((source, (x + shift) % SIDE * SIDE + y))
+            pairs.append((ROWS + source, ROWS + x * SIDE + (y + shift) % SIDE))
+    return pairs
 
 
 def shell_counts():
@@ -356,13 +420,21 @@
     third = jnp.broadcast_to(third[:, None, :, None, :], (BINS, 2, GRID, 2, GRID)).reshape(
         BINS * 128, 128
     )
-    blocks = insert(particles, orient_bin, tilt_slope, table)
-    parts = lax.all_to_all(blocks, HALF_ROW, 0, 0, axis_index_groups=groups(False), tiled=True)
+    inputs = [
+        pltpu.with_memory_space_constraint(x, pltpu.HBM)
+        for x in (particles, orient_bin, tilt_slope, table)
+    ]
+    *held, far = first_slab(*inputs)
+    far = lax.ppermute(far, HALF_ROW, shifted(2))
+    after, before, own = other_slabs(*held)
+    after = lax.ppermute(after, HALF_ROW, shifted(1))
+    before = lax.ppermute(before, HALF_ROW, shifted(3))
+    parts = [own, after, before, far]
     parts, grown, second_sums, third = lax.optimization_barrier(
         (parts, grown, second_sums, third)
     )
-    blocks = reduce(parts, SIDE, BLOCK)
-    parts = lax.all_to_all(blocks, HALF_ROW, 0, 0, axis_index_groups=groups(True), tiled=True)
+    blocks = gather(*parts)
+    parts = lax.all_to_all(blocks, HALF_ROW, 0, 0, axis_index_groups=groups(), tiled=True)
     blocks = reduce(parts, COLS, OWN)
     parts = lax.all_to_all(blocks, "col", 0, 0, tiled=True)
     own = divide(parts, grown, second_sums, third)

time: 84.7 us -> 81.9 us (0.967)
  starting transfers between devices: 5.92 us -> 4.4 us
  waiting for transfers between devices: 7.33 us -> 6.2 us
  matrix products: 1.65 us -> 0.69 us
  blocking collectives: 50.2 us -> 51.1 us
    all_to_all x1 -> x0, waiting for transfers between devices: 6.16 us -> none  [local(): lax.all_to_all(blocks, HALF_ROW, 0, 0, axis_index_groups=groups(False), t...]
    all_to_all x1 -> x0, starting transfers between devices: 5.83 us -> none  [local(): lax.all_to_all(blocks, HALF_ROW, 0, 0, axis_index_groups=groups(False), t...]
    ppermute x0 -> x3, waiting for transfers between devices: none -> 5.03 us  [the longest x1 5.03 us: local(): far = lax.ppermute(far, HALF_ROW, shifted(2))]
    ppermute x0 -> x3, starting transfers between devices: none -> 4.31 us  [the longest x1 2.07 us: local(): far = lax.ppermute(far, HALF_ROW, shifted(2))]
    dot_general x1, matrix products: 1.65 us -> 0.69 us  [local(): grown = jnp.dot(first, quadrant_masks(), preferred_element_type=F32)]
    pallas_call x1 -> x3, Pallas kernels: 8.78 us -> 8.75 us  [the longest x1 5.5 us: first_slab(): pl.pallas_call(first_kernel, out_shape=(jax.ShapeDtypeStruct((2, GRID * P...]
  transfers between devices with their start and end apart: 2 -> 4, of which waited for: 2 -> 2; matrix products, arithmetic and copies ran while one was open for 11% -> 10% of each run, Pallas kernels for 0% -> 0%
where the time goes in v4:
time: 81.9 us; the launch traced here: 81.4 us
  blocking collectives  51.1 us (62%)
  Pallas kernels  10.9 us (13%)
  local copies, waits for them, and re-layouts  6.36 us (8%)
  waiting for transfers between devices  6.2 us (8%)
  starting transfers between devices  4.4 us (5%)
  other arithmetic  0.89 us (1%)
    all_to_all x1, blocking collectives, local(): parts = lax.all_to_all(blocks, 'col', 0, 0, tiled=True)  17.7 us
    all_to_all x1, blocking collectives, local(): lax.all_to_all(blocks, HALF_ROW, 0, 0, axis_index_groups=groups(), tiled=...  12.3 us
    all_to_all x1, blocking collectives, local(): parts = lax.all_to_all(sums, ROW, 0, 0, tiled=True)  10.8 us
    all_to_all x1, blocking collectives, local(): parts = lax.all_to_all(spread_sum(parts), 'col', 0, 0, tiled=True)  10.4 us
    pallas_call x1, Pallas kernels, first_slab(): pl.pallas_call(first_kernel, out_shape=(jax.ShapeDtypeStruct((2, GRID * P...  5.5 us
    ppermute x1, waiting for transfers between devices, local(): far = lax.ppermute(far, HALF_ROW, shifted(2))  5.03 us
    pallas_call x1, Pallas kernels, other_slabs(): pl.pallas_call(slabs_kernel, out_shape=(SLAB,) * 3, in_specs=[VMEM] * 4,...  3.04 us
    reshape x1, local copies, waits for them, and re-layouts, local(): jnp.broadcast_to(third[:, None, :, None, :], (BINS, 2, GRID, 2, GRID))  2.41 us
  transfers between devices with their start and end apart: 4, of which 2 were waited for; matrix products, arithmetic and copies ran while one was open for 10% of the time, Pallas kernels for 0%

profile of v4, /device:TPU:2, one launch (start us, length us, event | category | flops | bytes accessed | tf_op | source)
XLA Modules:
  0.0 81.4 jit_solution(16506308876752500828)
XLA Ops:
  0.6 5.5 %first_slab.1 = (f32[2,4608,128]{2,1,0:T(8,128)S(1)}, bf16[2,64,64]{2,1,0:T(8,128)(2,1)S(1)}, bf16[256,128]{1,0:T(8,128)(2,1)S(1)}, f32[8,128]{1,0:T(8,128)S(1)}, f32[1032,128]{1,0:T(8,128)S(1)}) custom-call(s32[2]{0:T(128)} %bins_in.1, s32[2,2]{1,0:T(2,128)} %slopes_in.1, bf16[2,2,64,4096]{3,2,1,0:T(8,128)(2,1)} %particles.1, bf16[16,3,64,64]{3,2,1,0:T(8,128)(2,1)} %table.1), custom_call_target="tpu_custom_call" | custom-call | flops 1000000000 | bytes 4194304 | tf_op jit(solution)/shard_map/first_slab/pallas_call | solution.py:143
  6.1 3.0 %other_slabs.1 = (f32[1032,128]{1,0:T(8,128)}, f32[1032,128]{1,0:T(8,128)}, f32[1032,128]{1,0:T(8,128)S(1)}) custom-call(f32[2,4608,128]{2,1,0:T(8,128)S(1)} %get-tuple-element.22.planes, bf16[2,64,64]{2,1,0:T(8,128)(2,1)S(1)} %get-tuple-element.23.second, bf16[256,128]{1,0:T(8,128)(2,1)S(1)} %get-tuple-element.24.third, f32[8,128]{1,0:T(8,128)S(1)} %get-tuple-element.25.counts), custom_call_target="tpu_custom_call" | custom-call | flops 1000000000 | bytes 1048576 | tf_op jit(solution)/shard_map/other_slabs/pallas_call | solution.py:173
  9.2 1.5 %collective-permute-start = (f32[1032,128]{1,0:T(8,128)}, f32[1032,128]{1,0:T(8,128)S(1)}, u32[]{:S(2)}, u32[]{:S(2)}) collective-permute-start(f32[1032,128]{1,0:T(8,128)} %get-tuple-element.27), channel_id=1, source_target_pairs={{0,32},{128,136},{8,40},{136,144},{16,48},{144,152},{24,56},{152,1... | collective-permute-start | bytes 1585160 | tf_op jit(solution)/shard_map/ppermute | solution.py:430
  10.7 0.8 collective-permute-start.1
  11.4 2.1 %collective-permute-start.2 = (f32[1032,128]{1,0:T(8,128)S(1)}, f32[1032,128]{1,0:T(8,128)S(1)}, u32[]{:S(2)}, u32[]{:S(2)}) collective-permute-start(f32[1032,128]{1,0:T(8,128)S(1)} %get-tuple-element.29), channel_id=1, source_target_pairs={{0,64},{128,144},{8,72},{136,152},{16,80},{144,128},{24,88},{152,1... | collective-permute-start | bytes 1585160 | tf_op jit(solution)/shard_map/ppermute | solution.py:428
  13.5 1.0 %slice_bitcast_fusion = bf16[16,64,64]{1,2,0:T(8,128)(2,1)S(1)} fusion(bf16[16,3,64,64]{3,2,1,0:T(8,128)(2,1)} %table.1), kind=kLoop, calls=%fused_computation.32 | loop fusion | bytes 262144 | tf_op jit(solution)/shard_map/transpose | solution.py:419
  14.5 0.8 constant_dynamic-slice_fusion
  15.3 0.9 %convert_reduce_fusion = f32[16,8]{1,0:T(8,128)S(1)} fusion(bf16[16,3,64,64]{3,2,1,0:T(8,128)(2,1)} %table.1, s32[]{:T(128)S(6)} %select_n.35), kind=kLoop, calls=%fused_computation.33 | loop fusion | flops 16256 | bytes 16900 | tf_op jit(solution)/shard_map/reduce_sum | solution.py:418
  16.2 0.1 copy.12
  16.2 0.2 copy.13
  16.4 1.9 %broadcast_in_dim.6 = bf16[16,2,64,2,64]{4,3,2,1,0:T(2,128)(2,1)} broadcast(bf16[16,64,64]{2,1,0:T(8,128)(2,1)S(1)} %copy.13), dimensions={0,2,4} | broadcast | bytes 655360 | tf_op jit(solution)/shard_map/broadcast_in_dim | solution.py:420
  18.4 2.4 %reshape.15.third = bf16[2048,128]{1,0:T(8,128)(2,1)S(1)} reshape(bf16[16,2,64,2,64]{4,3,2,1,0:T(2,128)(2,1)} %broadcast_in_dim.6) | data formatting | bytes 1048576 | tf_op jit(solution)/shard_map/reshape | solution.py:420
  20.8 0.7 fusion.3.grown
  21.5 5.0 %collective-permute-done.2.refs_2_ = f32[1032,128]{1,0:T(8,128)S(1)} collective-permute-done((f32[1032,128]{1,0:T(8,128)S(1)}, f32[1032,128]{1,0:T(8,128)S(1)}, u32[]{:S(2)}, u32[]{:S(2)}) %collective-permute-start.2) | collective-permute-done | bytes 528416 | tf_op jit(solution)/shard_map/ppermute | solution.py:428
  26.6 0.2 gather.1
  26.8 12.3 %all_to_all.20.parts = f32[4,264,128]{2,1,0:T(8,128)S(1)} all-to-all(f32[4,264,128]{2,1,0:T(8,128)S(1)} %gather.1), channel_id=1, replica_groups={{0,8,16,24},{32,40,48,56},{64,72,80,88},{96,104,112,120},{128,160,192,2..., dimensions={0} | all-to-all | bytes 1081344 | tf_op jit(solution)/shard_map/all_to_all | solution.py:437
  39.1 17.7 %all_to_all.21.parts = f32[8,40,128]{2,1,0:T(8,128)S(1)} all-to-all(f32[8,40,128]{2,1,0:T(8,128)S(1)} %shard_map.76), channel_id=1, replica_groups=mesh['half'=2,'row_0'=4,'row_1'=4,'col'=8] {'col'}, dimensions={0} | all-to-all | bytes 327680 | tf_op jit(solution)/shard_map/all_to_all | solution.py:439
  56.8 0.5 divide.1.own
  57.3 0.1 collective-permute-start.3
  57.4 1.2 %collective-permute-done.3.other = f32[32,128]{1,0:T(8,128)S(1)} collective-permute-done((f32[32,128]{1,0:T(8,128)S(1)}, f32[32,128]{1,0:T(8,128)S(1)}, u32[]{:S(2)}, u32[]{:S(2)}) %collective-permute-start.3) | collective-permute-done | bytes 16416 | tf_op jit(solution)/shard_map/ppermute | solution.py:441
  58.5 0.9 %spectra.1 = (f32[16,8,128]{2,1,0:T(8,128)S(1)}, f32[1,2,4,512]{3,2,1,0:T(4,128)}) custom-call(f32[32,128]{1,0:T(8,128)S(1)} %divide.1.own, f32[32,128]{1,0:T(8,128)S(1)} %collective-permute-done.3.other), custom_call_target="tpu_custom_call" | custom-call | tf_op jit(solution)/shard_map/spectra/pallas_call | solution.py:332
  59.5 10.8 %all_to_all.22.parts = f32[16,8,128]{2,1,0:T(8,128)S(1)} all-to-all(f32[16,8,128]{2,1,0:T(8,128)S(1)} %get-tuple-element.38), channel_id=1, replica_groups=mesh['half'=2,'row_0'=4,'row_1'=4,'col'=8] {'row_0','row_1'}, dimensions={0} | all-to-all | bytes 131072 | tf_op jit(solution)/shard_map/all_to_all | solution.py:443
  70.3 10.4 %all_to_all.23.parts = f32[8,8,128]{2,1,0:T(8,128)S(1)} all-to-all(f32[8,8,128]{2,1,0:T(8,128)S(1)} %spread_sum.1), channel_id=1, replica_groups=mesh['half'=2,'row_0'=4,'row_1'=4,'col'=8] {'col'}, dimensions={0} | all-to-all | bytes 65536 | tf_op jit(solution)/shard_map/all_to_all | solution.py:444
  80.7 0.7 finish.1
  (13 shorter events, 0.1 us)
Async XLA Ops:
  9.2 12.3 %collective-permute-start = (f32[1032,128]{1,0:T(8,128)}, f32[1032,128]{1,0:T(8,128)S(1)}, u32[]{:S(2)}, u32[]{:S(2)}) collective-permute-start(f32[1032,128]{1,0:T(8,128)} %get-tuple-element.27), channel_id=1, source_target_pairs={{0,32},{128,136},{8,40},{136,144},{16,48},{144,152},{24,56},{152,1... | collective-permute-start | bytes 1585160 | tf_op jit(solution)/shard_map/ppermute | solution.py:430
  10.7 10.9 %collective-permute-start.1 = (f32[1032,128]{1,0:T(8,128)}, f32[1032,128]{1,0:T(8,128)S(1)}, u32[]{:S(2)}, u32[]{:S(2)}) collective-permute-start(f32[1032,128]{1,0:T(8,128)} %get-tuple-element.28), channel_id=1, source_target_pairs={{0,96},{128,152},{8,104},{136,128},{16,112},{144,136},{24,120},{15... | collective-permute-start | bytes 1585160 | tf_op jit(solution)/shard_map/ppermute | solution.py:431
  11.4 15.1 %collective-permute-start.2 = (f32[1032,128]{1,0:T(8,128)S(1)}, f32[1032,128]{1,0:T(8,128)S(1)}, u32[]{:S(2)}, u32[]{:S(2)}) collective-permute-start(f32[1032,128]{1,0:T(8,128)S(1)} %get-tuple-element.29), channel_id=1, source_target_pairs={{0,64},{128,144},{8,72},{136,152},{16,80},{144,128},{24,88},{152,1... | collective-permute-start | bytes 1585160 | tf_op jit(solution)/shard_map/ppermute | solution.py:428
  21.5 59.2 %copy-start = (f32[1,29]{1,0:T(1,128)S(1)}, f32[1,29]{1,0:T(1,128)}, u32[]{:S(2)}) copy-start(f32[1,29]{1,0:T(1,128)} %constant.85.clone.counts) | copy-start | bytes 352
  57.3 1.3 %collective-permute-start.3 = (f32[32,128]{1,0:T(8,128)S(1)}, f32[32,128]{1,0:T(8,128)S(1)}, u32[]{:S(2)}, u32[]{:S(2)}) collective-permute-start(f32[32,128]{1,0:T(8,128)S(1)} %divide.1.own), channel_id=1, source_target_pairs={{0,128},{128,0},{1,129},{129,1},{2,130},{130,2},{3,131},{131,3},{4... | collective-permute-start | bytes 49160 | tf_op jit(solution)/shard_map/ppermute | solution.py:441

commit v5 on v4

--- a/solution.py
+++ b/solution.py
@@ -1,5 +1,3 @@
-import functools
-
 import jax
 import jax.numpy as jnp
 import numpy as np
@@ -20,7 +18,7 @@
 SLOPE_MIN = 12
 SLOPES = 29
 SIDE = 4
-PITCH = 72
+PITCH = 68
 BLOCK = FIRST * GRID
 OWN = FIRST * SECOND
 ROW = ("row_0", "row_1")
@@ -55,53 +53,56 @@
     return total
 
 
-def compute_slab(shift, planes, second, third, counts, out):
+def compute_slab(shift, inners, planes, second, third, out, counts=None):
     on_first = lax.axis_index("half") == 0
     mine = jnp.where(on_first, lax.axis_index("row_0"), lax.axis_index("row_1"))
     outer = lax.rem(mine + shift, SIDE)
-    out[SIDE * BLOCK : SIDE * BLOCK + 8, :] = counts
-
-    @pl.loop(0, SIDE // 2)
-    def _(step):
-        for g in range(2):
-            inner = step * 2 + g
-            row = jnp.where(on_first, outer * SIDE + inner, inner * SIDE + outer)
-            for i in range(FIRST):
-                parts = []
-                for p in range(2):
-                    plane = planes[p, pl.ds(row * FIRST + i, GRID, stride=PITCH), :].astype(BF16)
-                    along = jnp.dot(second[p], plane, preferred_element_type=F32)
-                    parts.append(along.astype(BF16))
-                full = jnp.dot(
-                    jnp.concatenate(parts, axis=1), third[...], preferred_element_type=F32
-                )
-                for q in range(COLS):
-                    start = inner * BLOCK + (q * FIRST + i) * SECOND
-                    start = pl.multiple_of(start, 8)
-                    out[pl.ds(start, SECOND), :] = full[q * SECOND : (q + 1) * SECOND]
-
-
-def first_kernel(bins_in, slopes_in, particles, table, planes, second, third, counts, out, volume, chosen, bins, slopes, sem):
+    for n, inner in enumerate(inners):
+        row = jnp.where(on_first, outer * SIDE + inner, inner * SIDE + outer)
+        for i in range(FIRST):
+            parts = []
+            for p in range(2):
+                plane = planes[p, pl.ds(row * FIRST + i, GRID, stride=PITCH), :].astype(BF16)
+                along = jnp.dot(second[p], plane, preferred_element_type=F32)
+                parts.append(along.astype(BF16))
+            full = jnp.dot(jnp.concatenate(parts, axis=1), third[...], preferred_element_type=F32)
+            for q in range(COLS):
+                start = n * BLOCK + (q * FIRST + i) * SECOND
+                out[start : start + SECOND, :] = full[q * SECOND : (q + 1) * SECOND]
+    if counts is not None:
+        out[len(inners) * BLOCK : len(inners) * BLOCK + 8, :] = counts[...]
+
+
+LOW = (0, 1)
+HIGH = (2, 3)
+HALF_SLAB = jax.ShapeDtypeStruct((2 * BLOCK, 128), F32)
+HALF_SLAB_COUNTS = jax.ShapeDtypeStruct((2 * BLOCK + 8, 128), F32)
+SLAB = jax.ShapeDtypeStruct((SIDE * BLOCK + 8, 128), F32)
+
+
+def first_kernel(bins_in, slopes_in, particles, table, planes, second, third, counts, far_low, far_high, volume, chosen, bins, slopes, sem):
     scalars = [
         pltpu.make_async_copy(bins_in, bins, sem.at[6]),
         pltpu.make_async_copy(slopes_in, slopes, sem.at[7]),
     ]
     volumes = [
-        [
-            pltpu.make_async_copy(particles.at[p, c], volume.at[p, c], sem.at[p * 2 + c])
-            for c in range(2)
-        ]
-        for p in range(2)
+        pltpu.make_async_copy(
+            particles.at[:, :, :, pl.ds(k * 1024, 1024)],
+            volume.at[:, :, :, pl.ds(k * 1024, 1024)],
+            sem.at[k],
+        )
+        for k in range(4)
     ]
-    for copy in (*scalars, *volumes[0], *volumes[1]):
+    for copy in (*scalars, volumes[0]):
         copy.start()
     third[...] = jnp.zeros_like(third)
+    low = iota((GRID, 128), 1) < GRID
     for copy in scalars:
         copy.wait()
     tables = [
         pltpu.make_async_copy(table.at[bins[p]], chosen.at[p], sem.at[4 + p]) for p in range(2)
     ]
-    for copy in tables:
+    for copy in (*tables, *volumes[1:]):
         copy.start()
     wedges = [
         jnp.concatenate([wedge_tile(slopes[p, 0], slopes[p, 1])] * 4, axis=1) for p in range(2)
@@ -114,29 +115,31 @@
         transposed = chosen[p, 2].astype(F32).T.astype(BF16)
         for c in range(2):
             third[p * 128 + c * 64 : p * 128 + c * 64 + 64, c * 64 : c * 64 + 64] = transposed
-    low = iota((GRID, 128), 1) < GRID
-    for p in range(2):
-        for copy in volumes[p]:
-            copy.wait()
-
-        @pl.loop(0, 16, unroll=4)
-        def _(chunk):
-            lanes = pl.ds(pl.multiple_of(chunk * 256, 256), 256)
+    first = [chosen[p, 0] for p in range(2)]
+
+    def transform(chunk):
+        lanes = pl.ds(pl.multiple_of(chunk * 256, 256), 256)
+        for p in range(2):
             both = jnp.concatenate([volume[p, 0, :, lanes], volume[p, 1, :, lanes]], axis=1)
-            along = jnp.dot(chosen[p, 0], both * wedges[p], preferred_element_type=F32)
+            along = jnp.dot(first[p], both * wedges[p], preferred_element_type=F32)
             for j in range(2):
                 real = along[:, j * 128 : j * 128 + 128]
                 imag = along[:, 256 + j * 128 : 256 + j * 128 + 128]
                 even = jnp.where(low, real, pltpu.roll(imag, 64, 1))
                 odd = jnp.where(low, pltpu.roll(real, 64, 1), imag)
-                base = pl.multiple_of((chunk * 4 + j * 2) * PITCH, 8)
+                base = pl.multiple_of((chunk * 4 + j * 2) * PITCH, 4)
                 planes[p, pl.ds(base, GRID), :] = even
                 planes[p, pl.ds(base + PITCH, GRID), :] = odd
 
-    compute_slab(2, planes, second, third, counts[...], out)
-
-
-SLAB = jax.ShapeDtypeStruct((SIDE * BLOCK + 8, 128), F32)
+    for k in range(4):
+        volumes[k].wait()
+
+        @pl.loop(k * 4, k * 4 + 4, unroll=4)
+        def _(chunk):
+            transform(chunk)
+
+    compute_slab(2, LOW, planes, second, third, far_low, counts)
+    compute_slab(2, HIGH, planes, second, third, far_high)
 
 
 def first_slab(particles, orient_bin, tilt_slope, table):
@@ -147,10 +150,11 @@
             jax.ShapeDtypeStruct((2, GRID, GRID), BF16),
             jax.ShapeDtypeStruct((256, 128), BF16),
             jax.ShapeDtypeStruct((8, 128), F32),
-            SLAB,
+            HALF_SLAB_COUNTS,
+            HALF_SLAB,
         ),
         in_specs=[HBM] * 4,
-        out_specs=(VMEM,) * 5,
+        out_specs=(VMEM,) * 6,
         scratch_shapes=[
             pltpu.VMEM((2, 2, GRID, GRID * GRID), BF16),
             pltpu.VMEM((2, 3, GRID, GRID), BF16),
@@ -164,15 +168,33 @@
     )(orient_bin, tilt_slope, particles, table)
 
 
-def slabs_kernel(planes, second, third, counts, *outs):
-    for shift, out in zip((1, 3, 0), outs, strict=True):
-        compute_slab(shift, planes, second, third, counts[...], out)
+def direct_kernel(planes, second, third, counts, after_high, before_low):
+    compute_slab(1, HIGH, planes, second, third, after_high)
+    compute_slab(3, LOW, planes, second, third, before_low, counts)
+
+
+def direct_slabs(planes, second, third, counts):
+    return pl.pallas_call(
+        direct_kernel,
+        out_shape=(HALF_SLAB, HALF_SLAB_COUNTS),
+        in_specs=[VMEM] * 4,
+        out_specs=(VMEM,) * 2,
+        compiler_params=SMALL,
+        cost_estimate=pl.CostEstimate(flops=10**9, bytes_accessed=2**20, transcendentals=0),
+        name="direct_slabs",
+    )(planes, second, third, counts)
+
+
+def other_kernel(planes, second, third, counts, after_low, before_high, own):
+    compute_slab(1, LOW, planes, second, third, after_low, counts)
+    compute_slab(3, HIGH, planes, second, third, before_high)
+    compute_slab(0, LOW + HIGH, planes, second, third, own, counts)
 
 
 def other_slabs(planes, second, third, counts):
     return pl.pallas_call(
-        slabs_kernel,
-        out_shape=(SLAB,) * 3,
+        other_kernel,
+        out_shape=(HALF_SLAB_COUNTS, HALF_SLAB, SLAB),
         in_specs=[VMEM] * 4,
         out_specs=(VMEM,) * 3,
         compiler_params=SMALL,
@@ -181,70 +203,124 @@
     )(planes, second, third, counts)
 
 
-def gather_kernel(own, *refs):
-    *others, out = refs
-    tail = pl.ds(SIDE * BLOCK, 8)
-    counts = own[tail, :]
-    for other in others:
-        counts = counts + other[tail, :]
-    for n in range(SIDE):
-        span = pl.ds(n * BLOCK, BLOCK)
-        total = own[span, :]
-        for other in others:
-            total = total + other[span, :]
-        out[n, 0:BLOCK, :] = total
-        out[n, BLOCK : BLOCK + 8, :] = counts
+def add_kernel(after_low, far_low, before_high, far_high, after_out, before_out):
+    after_out[...] = after_low[...] + far_low[...]
+    before_out[...] = before_high[...] + far_high[...]
+
+
+def add_far(after_low, far_low, before_high, far_high):
+    return pl.pallas_call(
+        add_kernel,
+        out_shape=(HALF_SLAB_COUNTS, HALF_SLAB),
+        in_specs=[VMEM] * 4,
+        out_specs=(VMEM,) * 2,
+        compiler_params=SMALL,
+        cost_estimate=pl.CostEstimate(flops=10**8, bytes_accessed=2**20, transcendentals=0),
+        name="add_far",
+    )(after_low, far_low, before_high, far_high)
+
+
+def gather_kernel(own, after_low, after_high, before_low, before_high, *refs):
+    *outs, sums = refs
+    on_first = lax.axis_index("half") == 0
+    mine = jnp.where(on_first, lax.axis_index("row_1"), lax.axis_index("row_0"))
+    half = 2 * BLOCK
+    tail = pl.ds(half, 8)
+    counts = own[pl.ds(2 * half, 8), :] + after_low[tail, :] + before_low[tail, :]
+    for n, parts in enumerate(((after_low, before_low), (after_high, before_high))):
+        span = pl.ds(n * half, half)
+        sums[span, :] = own[span, :] + parts[0][0:half, :] + parts[1][0:half, :]
+    for shift, out in zip((2, 1, 3, 0), outs, strict=True):
+        span = pl.ds(pl.multiple_of(lax.rem(mine + shift, SIDE) * BLOCK, 8), BLOCK)
+        out[0:BLOCK, :] = sums[span, :]
+        out[BLOCK : BLOCK + 8, :] = counts
 
 
 def gather(*parts):
     return pl.pallas_call(
         gather_kernel,
-        out_shape=jax.ShapeDtypeStruct((SIDE, BLOCK + 8, 128), F32),
+        out_shape=(jax.ShapeDtypeStruct((BLOCK + 8, 128), F32),) * SIDE,
+        in_specs=[VMEM] * len(parts),
+        out_specs=(VMEM,) * SIDE,
+        scratch_shapes=[pltpu.VMEM((SIDE * BLOCK, 128), F32)],
+        compiler_params=SMALL,
+        name="gather",
+    )(*parts)
+
+
+def reduce_kernel(*refs):
+    *parts, out = refs
+    tail = pl.ds(BLOCK, 8)
+    counts = parts[0][tail, :]
+    for part in parts[1:]:
+        counts = counts + part[tail, :]
+    for n in range(COLS):
+        span = pl.ds(n * OWN, OWN)
+        total = parts[0][span, :]
+        for part in parts[1:]:
+            total = total + part[span, :]
+        out[n, 0:OWN, :] = total
+        out[n, OWN : OWN + 8, :] = counts
+
+
+def reduce(*parts):
+    return pl.pallas_call(
+        reduce_kernel,
+        out_shape=jax.ShapeDtypeStruct((COLS, OWN + 8, 128), F32),
         in_specs=[VMEM] * len(parts),
         out_specs=VMEM,
         compiler_params=SMALL,
-        name="gather",
+        name="reduce",
     )(*parts)
 
 
-def reduce_kernel(owners, size, parts, out):
-    senders = parts.shape[0]
-    tail = pl.ds(owners * size, 8)
-    counts = parts[0, tail, :]
-    for k in range(1, senders):
-        counts = counts + parts[k, tail, :]
-    for n in range(owners):
-        span = pl.ds(n * size, size)
-        total = parts[0, span, :]
-        for k in range(1, senders):
-            total = total + parts[k, span, :]
-        out[n, 0:size, :] = total
-        out[n, size : size + 8, :] = counts
-
-
-def reduce(parts, owners, size):
-    return pl.pallas_call(
-        functools.partial(reduce_kernel, owners, size),
-        out_shape=jax.ShapeDtypeStruct((owners, size + 8, 128), F32),
+def operators_kernel(table, third, grown, second_sums, first):
+    row, col = lax.axis_index(ROW), lax.axis_index("col")
+    place = iota((8, GRID), 0)
+    own_first = (iota((8, GRID), 1) == row * FIRST + place).astype(BF16)
+    own_second = (iota((8, GRID), 1) == col * SECOND + place).astype(BF16)
+    ones = jnp.ones((GRID, 128), BF16)
+    for k in range(BINS):
+        block = table[k, 2]
+        block = jnp.concatenate([block, block], axis=1)
+        for c in range(2):
+            third[c * GRID : (c + 1) * GRID, k * 128 : (k + 1) * 128] = block
+        rows = jnp.dot(own_first, table[k, 0], preferred_element_type=F32)
+        for i in range(FIRST):
+            first[i * BINS + k : i * BINS + k + 1, :] = rows[i : i + 1]
+        rows = jnp.dot(own_second, table[k, 1], preferred_element_type=F32).astype(BF16)
+        second_sums[k] = jnp.dot(rows, ones, preferred_element_type=F32)
+    shape = (GRID, 128)
+    wave_first = iota(shape, 0) - CENTRE
+    wave_third = iota(shape, 1) % GRID - CENTRE
+    quadrant = jnp.where(wave_first * wave_third >= 0, 0, 1)
+    own = quadrant == iota(shape, 1) // GRID
+    height = jnp.where(own, 16 * jnp.abs(wave_third), 16 * GRID * GRID)
+    width = jnp.abs(wave_first)
+    rows = first[...].astype(BF16)
+    for k in range(SLOPES):
+        held = jnp.where(height <= (k + SLOPE_MIN) * width, 1.0, 0.0).astype(BF16)
+        grown[:, k * 128 : (k + 1) * 128] = jnp.dot(rows, held, preferred_element_type=F32)
+
+
+def operators(table):
+    return pl.pallas_call(
+        operators_kernel,
+        out_shape=(
+            jax.ShapeDtypeStruct((128, BINS * 128), BF16),
+            jax.ShapeDtypeStruct((FIRST * BINS, SLOPES * 128), F32),
+            jax.ShapeDtypeStruct((BINS, SECOND, 128), F32),
+        ),
         in_specs=[VMEM],
-        out_specs=VMEM,
-        compiler_params=SMALL,
-    )(parts)
-
-
-def quadrant_masks():
-    shape = (GRID, SLOPES * 128)
-    wave_first = iota(shape, 0) - CENTRE
-    lane = iota(shape, 1)
-    wave_third = lane % GRID - CENTRE
-    quadrant = (lane // GRID) % 2
-    slope = lane // 128 + SLOPE_MIN
-    inside = 16 * jnp.abs(wave_third) <= slope * jnp.abs(wave_first)
-    own = jnp.where(wave_first * wave_third >= 0, 0, 1) == quadrant
-    return (inside & own).astype(BF16)
-
-
-def divide_kernel(parts, grown, second_sums, third, out, left):
+        out_specs=(VMEM,) * 3,
+        scratch_shapes=[pltpu.VMEM((FIRST * BINS, GRID), F32)],
+        compiler_params=SMALL,
+        cost_estimate=pl.CostEstimate(flops=10**8, bytes_accessed=2**20, transcendentals=0),
+        name="operators",
+    )(table)
+
+
+def divide_kernel(parts, third, grown, second_sums, out, left):
     total = parts[0]
     for k in range(1, COLS):
         total = total + parts[k]
@@ -263,7 +339,7 @@
                 start = i * BINS + upper * 8
                 held[i][upper] += spread * grown[start : start + 8, k * 128 : k * 128 + 128]
     for k in range(BINS):
-        sums = jnp.broadcast_to(second_sums[:, k : k + 1], (8, 128))
+        sums = second_sums[k]
         for i in range(FIRST):
             value = sums * held[i][k // 8][k % 8 : k % 8 + 1, :]
             upper = value.astype(BF16)
@@ -271,11 +347,13 @@
             lanes = slice(k * 128, k * 128 + 128)
             left[i * SECOND : (i + 1) * SECOND, lanes] = upper.astype(F32)
             left[OWN + i * SECOND : OWN + (i + 1) * SECOND, lanes] = lower.astype(F32)
-    weight = jnp.dot(left[...].astype(BF16), third[...], preferred_element_type=F32)
+    weight = lax.dot_general(
+        left[...].astype(BF16), third[...], (((1,), (1,)), ((), ())), preferred_element_type=F32
+    )
     out[...] = total[0:OWN] / (weight[0:OWN] + weight[OWN:] + 1.0)
 
 
-def divide(parts, grown, second_sums, third):
+def divide(parts, third, grown, second_sums):
     return pl.pallas_call(
         divide_kernel,
         out_shape=jax.ShapeDtypeStruct((OWN, 128), F32),
@@ -284,7 +362,7 @@
         scratch_shapes=[pltpu.VMEM((2 * OWN, BINS * 128), F32)],
         compiler_params=SMALL,
         name="divide",
-    )(parts, grown, second_sums, third)
+    )(parts, third, grown, second_sums)
 
 
 def spectra_kernel(own, other, out, maps, rows):
@@ -384,19 +462,15 @@
     )(parts, counts)
 
 
-def groups():
-    along_x = [[x * SIDE + y for x in range(SIDE)] for y in range(SIDE)]
-    along_y = [[x * SIDE + y for y in range(SIDE)] for x in range(SIDE)]
-    return along_y + [[ROWS + k for k in group] for group in along_x]
-
-
-def shifted(shift):
+def shifted(shift, swapped=False):
     pairs = []
-    for x in range(SIDE):
-        for y in range(SIDE):
-            source = x * SIDE + y
-            pairs.append((source, (x + shift) % SIDE * SIDE + y))
-            pairs.append((ROWS + source, ROWS + x * SIDE + (y + shift) % SIDE))
+    for half in range(2):
+        for x in range(SIDE):
+            for y in range(SIDE):
+                along_x = (half == 0) != swapped
+                to_x = (x + shift) % SIDE if along_x else x
+                to_y = y if along_x else (y + shift) % SIDE
+                pairs.append((half * ROWS + x * SIDE + y, half * ROWS + to_x * SIDE + to_y))
     return pairs
 
 
@@ -410,34 +484,30 @@
 
 
 def local(particles, orient_bin, tilt_slope, table):
-    row, col = lax.axis_index(ROW), lax.axis_index("col")
-    first = lax.dynamic_slice(table, (0, 0, row * FIRST, 0), (BINS, 1, FIRST, GRID))[:, 0]
-    first = jnp.swapaxes(first, 0, 1).reshape(FIRST * BINS, GRID)
-    grown = jnp.dot(first, quadrant_masks(), preferred_element_type=F32)
-    second = lax.dynamic_slice(table, (0, 1, col * SECOND, 0), (BINS, 1, SECOND, GRID))[:, 0]
-    second_sums = jnp.sum(second.astype(F32), axis=2).T
-    third = jnp.swapaxes(table[:, 2], 1, 2)
-    third = jnp.broadcast_to(third[:, None, :, None, :], (BINS, 2, GRID, 2, GRID)).reshape(
-        BINS * 128, 128
-    )
     inputs = [
         pltpu.with_memory_space_constraint(x, pltpu.HBM)
         for x in (particles, orient_bin, tilt_slope, table)
     ]
-    *held, far = first_slab(*inputs)
-    far = lax.ppermute(far, HALF_ROW, shifted(2))
-    after, before, own = other_slabs(*held)
-    after = lax.ppermute(after, HALF_ROW, shifted(1))
-    before = lax.ppermute(before, HALF_ROW, shifted(3))
-    parts = [own, after, before, far]
-    parts, grown, second_sums, third = lax.optimization_barrier(
-        (parts, grown, second_sums, third)
-    )
-    blocks = gather(*parts)
-    parts = lax.all_to_all(blocks, HALF_ROW, 0, 0, axis_index_groups=groups(), tiled=True)
-    blocks = reduce(parts, COLS, OWN)
+    *held, far_low, far_high = first_slab(*inputs)
+    far_low = lax.ppermute(far_low, HALF_ROW, shifted(1))
+    far_high = lax.ppermute(far_high, HALF_ROW, shifted(3))
+    after_high, before_low = direct_slabs(*held)
+    after_high = lax.ppermute(after_high, HALF_ROW, shifted(1))
+    before_low = lax.ppermute(before_low, HALF_ROW, shifted(3))
+    after_low, before_high, own = other_slabs(*held)
+    after_low, before_high = add_far(after_low, far_low, before_high, far_high)
+    after_low = lax.ppermute(after_low, HALF_ROW, shifted(1))
+    before_high = lax.ppermute(before_high, HALF_ROW, shifted(3))
+    prepared = operators(table)
+    parts = [own, after_low, after_high, before_low, before_high]
+    *others, own = gather(*parts)
+    parts = [
+        lax.ppermute(block, HALF_ROW, shifted(shift, True))
+        for shift, block in zip((2, 1, 3), others, strict=True)
+    ]
+    blocks = reduce(own, *parts)
     parts = lax.all_to_all(blocks, "col", 0, 0, tiled=True)
-    own = divide(parts, grown, second_sums, third)
+    own = divide(parts, *prepared)
     other = lax.ppermute(own, "half", [(0, 1), (1, 0)])
     sums, half_maps = spectra(own, other)
     parts = lax.all_to_all(sums, ROW, 0, 0, tiled=True)

time: 81.9 us -> 78.5 us (0.958)
  blocking collectives: 51.1 us -> 24.3 us
  starting transfers between devices: 4.4 us -> 23.4 us
  waiting for transfers between devices: 6.2 us -> 18.9 us
  local copies, waits for them, and re-layouts: 6.36 us -> 0.01 us
  other arithmetic: 0.89 us -> 0 us
    all_to_all x2 -> x0, blocking collectives: 30 us -> none  [the longest x1 17.7 us: local(): parts = lax.all_to_all(blocks, 'col', 0, 0, tiled=True)]
    ppermute x3 -> x9, starting transfers between devices: 4.31 us -> 15.1 us  [the longest x3 4.81 us: local(): lax.ppermute(block, HALF_ROW, shifted(shift, True))]
    all_to_all x0 -> x1, starting transfers between devices: none -> 8.21 us  [local(): parts = lax.all_to_all(blocks, 'col', 0, 0, tiled=True)]
    all_to_all x0 -> x1, waiting for transfers between devices: none -> 7.18 us  [local(): parts = lax.all_to_all(blocks, 'col', 0, 0, tiled=True)]
    ppermute x3 -> x9, waiting for transfers between devices: 5.03 us -> 10.6 us  [the longest x1 4.63 us: local(): after_high = lax.ppermute(after_high, HALF_ROW, shifted(1))]
    all_to_all x1, blocking collectives: 10.8 us -> 13.9 us  [local(): parts = lax.all_to_all(sums, ROW, 0, 0, tiled=True)]
    reshape x1 -> x0, local copies, waits for them, and re-layouts: 2.41 us -> none  [local(): jnp.broadcast_to(third[:, None, :, None, :], (BINS, 2, GRID, 2, GRID))]
    broadcast_in_dim x1 -> x0, local copies, waits for them, and re-layouts: 1.92 us -> none  [local(): jnp.broadcast_to(third[:, None, :, None, :], (BINS, 2, GRID, 2, GRID))]
  transfers between devices with their start and end apart: 4 -> 11, of which waited for: 2 -> 7; matrix products, arithmetic and copies ran while one was open for 10% -> 0% of each run, Pallas kernels for 0% -> 5%
where the time goes in v5:
time: 78.5 us; the launch traced here: 78.3 us
  blocking collectives  24.3 us (31%)
  starting transfers between devices  23.4 us (30%)
  waiting for transfers between devices  18.9 us (24%)
  Pallas kernels  10.9 us (14%)
    all_to_all x1, blocking collectives, local(): parts = lax.all_to_all(sums, ROW, 0, 0, tiled=True)  13.9 us
    all_to_all x1, blocking collectives, local(): parts = lax.all_to_all(spread_sum(parts), 'col', 0, 0, tiled=True)  10.4 us
    all_to_all x1, starting transfers between devices, local(): parts = lax.all_to_all(blocks, 'col', 0, 0, tiled=True)  8.21 us
    all_to_all x1, waiting for transfers between devices, local(): parts = lax.all_to_all(blocks, 'col', 0, 0, tiled=True)  7.18 us
    ppermute x3, starting transfers between devices, local(): lax.ppermute(block, HALF_ROW, shifted(shift, True))  4.81 us
    ppermute x1, waiting for transfers between devices, local(): after_high = lax.ppermute(after_high, HALF_ROW, shifted(1))  4.63 us
    pallas_call x1, Pallas kernels, first_slab(): pl.pallas_call(first_kernel, out_shape=(jax.ShapeDtypeStruct((2, GRID * P...  4.32 us
    ppermute x3, waiting for transfers between devices, local(): lax.ppermute(block, HALF_ROW, shifted(shift, True))  3.24 us
  transfers between devices with their start and end apart: 11, of which 7 were waited for; matrix products, arithmetic and copies ran while one was open for 0% of the time, Pallas kernels for 5%

profile of v5, /device:TPU:2, one launch (start us, length us, event | category | flops | bytes accessed | tf_op | source)
XLA Modules:
  0.0 78.3 jit_solution(13419529720679638807)
XLA Ops:
  0.6 4.3 %first_slab.1 = (f32[2,4352,128]{2,1,0:T(8,128)S(1)}, bf16[2,64,64]{2,1,0:T(8,128)(2,1)S(1)}, bf16[256,128]{1,0:T(8,128)(2,1)S(1)}, f32[8,128]{1,0:T(8,128)S(1)}...) custom-call(s32[2]{0:T(128)} %bins_in.1, s32[2,2]{1,0:T(2,128)} %slopes_in.1, bf16[2,2,64,4096]{3,2,1,0:T(8,128)(2,1)} %particles.1, ...), custom_call_target="tpu_custom_call" | custom-call | flops 1000000000 | bytes 4194304 | tf_op jit(solution)/shard_map/first_slab/pallas_call | solution.py:146
  5.0 1.6 %collective-permute-start = (f32[520,128]{1,0:T(8,128)S(1)}, f32[520,128]{1,0:T(8,128)S(1)}, u32[]{:S(2)}, u32[]{:S(2)}) collective-permute-start(f32[520,128]{1,0:T(8,128)S(1)} %get-tuple-element.33), channel_id=1, source_target_pairs={{0,32},{8,40},{16,48},{24,56},{32,64},{40,72},{48,80},{56,88},{64,... | collective-permute-start | bytes 798728 | tf_op jit(solution)/shard_map/ppermute | solution.py:492
  6.5 0.8 %collective-permute-start.1 = (f32[512,128]{1,0:T(8,128)S(1)}, f32[512,128]{1,0:T(8,128)S(1)}, u32[]{:S(2)}, u32[]{:S(2)}) collective-permute-start(f32[512,128]{1,0:T(8,128)S(1)} %get-tuple-element.35), channel_id=1, source_target_pairs={{0,96},{8,104},{16,112},{24,120},{32,0},{40,8},{48,16},{56,24},{64... | collective-permute-start | bytes 786440 | tf_op jit(solution)/shard_map/ppermute | solution.py:493
  7.9 3.2 %collective-permute-start.4 = (f32[520,128]{1,0:T(8,128)S(1)}, f32[520,128]{1,0:T(8,128)S(1)}, u32[]{:S(2)}, u32[]{:S(2)}) collective-permute-start(f32[520,128]{1,0:T(8,128)S(1)} %get-tuple-element.38), channel_id=1, source_target_pairs={{0,96},{8,104},{16,112},{24,120},{32,0},{40,8},{48,16},{56,24},{64... | collective-permute-start | bytes 798728 | tf_op jit(solution)/shard_map/ppermute | solution.py:496
  11.1 0.8 %other_slabs.1 = (f32[520,128]{1,0:T(8,128)S(1)}, f32[512,128]{1,0:T(8,128)S(1)}, f32[1032,128]{1,0:T(8,128)S(1)}) custom-call(f32[2,4352,128]{2,1,0:T(8,128)S(1)} %get-tuple-element.27.planes, bf16[2,64,64]{2,1,0:T(8,128)(2,1)S(1)} %get-tuple-element.28.second, bf16[256,128]{1,0:T(8,128)(2,1)S(1)} %get-tuple-element.29.third, ...), custom_call_target="tpu_custom_call" | custom-call | flops 1000000000 | bytes 1048576 | tf_op jit(solution)/shard_map/other_slabs/pallas_call | solution.py:195
  11.9 1.0 %collective-permute-done.1.far_high = f32[512,128]{1,0:T(8,128)S(1)} collective-permute-done((f32[512,128]{1,0:T(8,128)S(1)}, f32[512,128]{1,0:T(8,128)S(1)}, u32[]{:S(2)}, u32[]{:S(2)}) %collective-permute-start.1) | collective-permute-done | bytes 262176 | tf_op jit(solution)/shard_map/ppermute | solution.py:493
  13.0 1.4 %collective-permute-start.2 = (f32[520,128]{1,0:T(8,128)S(1)}, f32[520,128]{1,0:T(8,128)S(1)}, u32[]{:S(2)}, u32[]{:S(2)}) collective-permute-start(f32[520,128]{1,0:T(8,128)S(1)} %get-tuple-element.36), channel_id=1, source_target_pairs={{0,32},{8,40},{16,48},{24,56},{32,64},{40,72},{48,80},{56,88},{64,... | collective-permute-start | bytes 798728 | tf_op jit(solution)/shard_map/ppermute | solution.py:499
  14.4 3.2 %collective-permute-start.3 = (f32[512,128]{1,0:T(8,128)S(1)}, f32[512,128]{1,0:T(8,128)S(1)}, u32[]{:S(2)}, u32[]{:S(2)}) collective-permute-start(f32[512,128]{1,0:T(8,128)S(1)} %get-tuple-element.37), channel_id=1, source_target_pairs={{0,32},{8,40},{16,48},{24,56},{32,64},{40,72},{48,80},{56,88},{64,... | collective-permute-start | bytes 786440 | tf_op jit(solution)/shard_map/ppermute | solution.py:495
  17.6 4.6 %collective-permute-done.3.after_high = f32[512,128]{1,0:T(8,128)S(1)} collective-permute-done((f32[512,128]{1,0:T(8,128)S(1)}, f32[512,128]{1,0:T(8,128)S(1)}, u32[]{:S(2)}, u32[]{:S(2)}) %collective-permute-start.3) | collective-permute-done | bytes 262176 | tf_op jit(solution)/shard_map/ppermute | solution.py:495
  22.3 1.7 %collective-permute-done.5.before_high = f32[512,128]{1,0:T(8,128)S(1)} collective-permute-done((f32[512,128]{1,0:T(8,128)S(1)}, f32[512,128]{1,0:T(8,128)S(1)}, u32[]{:S(2)}, u32[]{:S(2)}) %collective-permute-start.5) | collective-permute-done | bytes 262176 | tf_op jit(solution)/shard_map/ppermute | solution.py:500
  24.2 1.6 %collective-permute-start.6 = (f32[264,128]{1,0:T(8,128)S(1)}, f32[264,128]{1,0:T(8,128)S(1)}, u32[]{:S(2)}, u32[]{:S(2)}) collective-permute-start(f32[264,128]{1,0:T(8,128)S(1)} %get-tuple-element.41), channel_id=1, source_target_pairs={{0,16},{8,24},{16,0},{24,8},{32,48},{40,56},{48,32},{56,40},{64,80... | collective-permute-start | bytes 405512 | tf_op jit(solution)/shard_map/ppermute | solution.py:505
  25.7 0.7 collective-permute-start.7
  26.4 2.6 %collective-permute-start.8 = (f32[264,128]{1,0:T(8,128)S(1)}, f32[264,128]{1,0:T(8,128)S(1)}, u32[]{:S(2)}, u32[]{:S(2)}) collective-permute-start(f32[264,128]{1,0:T(8,128)S(1)} %get-tuple-element.43), channel_id=1, source_target_pairs={{0,24},{8,0},{16,8},{24,16},{32,56},{40,32},{48,40},{56,48},{64,88... | collective-permute-start | bytes 405512 | tf_op jit(solution)/shard_map/ppermute | solution.py:505
  29.0 1.8 %collective-permute-done.6.refs_1_ = f32[264,128]{1,0:T(8,128)S(1)} collective-permute-done((f32[264,128]{1,0:T(8,128)S(1)}, f32[264,128]{1,0:T(8,128)S(1)}, u32[]{:S(2)}, u32[]{:S(2)}) %collective-permute-start.6) | collective-permute-done | bytes 135200 | tf_op jit(solution)/shard_map/ppermute | solution.py:505
  30.8 1.4 %collective-permute-done.7.refs_2_ = f32[264,128]{1,0:T(8,128)S(1)} collective-permute-done((f32[264,128]{1,0:T(8,128)S(1)}, f32[264,128]{1,0:T(8,128)S(1)}, u32[]{:S(2)}, u32[]{:S(2)}) %collective-permute-start.7) | collective-permute-done | bytes 135200 | tf_op jit(solution)/shard_map/ppermute | solution.py:505
  32.2 0.7 reduce.1
  32.9 8.2 %all-to-all-start = ((f32[8,40,128]{2,1,0:T(8,128)}), f32[8,40,128]{2,1,0:T(8,128)S(1)}, u32[]{:S(2)}, u32[]{:S(2)}) async-start(f32[8,40,128]{2,1,0:T(8,128)} %reduce.1), calls=%async_computation | async-start | bytes 327680 | tf_op jit(solution)/shard_map/all_to_all | solution.py:509
  41.1 2.2 %operators.1 = (bf16[128,2048]{1,0:T(8,128)(2,1)S(1)}, f32[64,3712]{1,0:T(8,128)S(1)}, f32[16,8,128]{2,1,0:T(8,128)S(1)}) custom-call(bf16[16,3,64,64]{3,2,1,0:T(8,128)(2,1)S(1)} %copy-done), custom_call_target="tpu_custom_call" | custom-call | flops 100000000 | bytes 1048576 | tf_op jit(solution)/shard_map/operators/pallas_call | solution.py:307
  43.4 7.2 %all-to-all-done.parts = f32[8,40,128]{2,1,0:T(8,128)S(1)} async-done(((f32[8,40,128]{2,1,0:T(8,128)}), f32[8,40,128]{2,1,0:T(8,128)S(1)}, u32[]{:S(2)}, u32[]{:S(2)}) %all-to-all-start) | async-done | bytes 163872 | tf_op jit(solution)/shard_map/all_to_all | solution.py:509
  51.2 1.2 %collective-permute-done.9.other = f32[32,128]{1,0:T(8,128)S(1)} collective-permute-done((f32[32,128]{1,0:T(8,128)S(1)}, f32[32,128]{1,0:T(8,128)S(1)}, u32[]{:S(2)}, u32[]{:S(2)}) %collective-permute-start.9) | collective-permute-done | bytes 16416 | tf_op jit(solution)/shard_map/ppermute | solution.py:511
  52.3 0.9 %spectra.1 = (f32[16,8,128]{2,1,0:T(8,128)S(1)}, f32[1,2,4,512]{3,2,1,0:T(4,128)}) custom-call(f32[32,128]{1,0:T(8,128)S(1)} %divide.1.own, f32[32,128]{1,0:T(8,128)S(1)} %collective-permute-done.9.other), custom_call_target="tpu_custom_call" | custom-call | tf_op jit(solution)/shard_map/spectra/pallas_call | solution.py:410
  53.3 13.9 %all_to_all.15.parts = f32[16,8,128]{2,1,0:T(8,128)S(1)} all-to-all(f32[16,8,128]{2,1,0:T(8,128)S(1)} %get-tuple-element.48), channel_id=1, replica_groups=mesh['half'=2,'row_0'=4,'row_1'=4,'col'=8] {'row_0','row_1'}, dimensions={0} | all-to-all | bytes 131072 | tf_op jit(solution)/shard_map/all_to_all | solution.py:513
  67.2 10.4 %all_to_all.16.parts = f32[8,8,128]{2,1,0:T(8,128)S(1)} all-to-all(f32[8,8,128]{2,1,0:T(8,128)S(1)} %spread_sum.1), channel_id=1, replica_groups=mesh['half'=2,'row_0'=4,'row_1'=4,'col'=8] {'col'}, dimensions={0} | all-to-all | bytes 65536 | tf_op jit(solution)/shard_map/all_to_all | solution.py:514
  77.5 0.7 finish.1
  (15 shorter events, 1.3 us)
Async XLA Ops:
  5.0 7.9 %collective-permute-start = (f32[520,128]{1,0:T(8,128)S(1)}, f32[520,128]{1,0:T(8,128)S(1)}, u32[]{:S(2)}, u32[]{:S(2)}) collective-permute-start(f32[520,128]{1,0:T(8,128)S(1)} %get-tuple-element.33), channel_id=1, source_target_pairs={{0,32},{8,40},{16,48},{24,56},{32,64},{40,72},{48,80},{56,88},{64,... | collective-permute-start | bytes 798728 | tf_op jit(solution)/shard_map/ppermute | solution.py:492
  6.5 6.4 %collective-permute-start.1 = (f32[512,128]{1,0:T(8,128)S(1)}, f32[512,128]{1,0:T(8,128)S(1)}, u32[]{:S(2)}, u32[]{:S(2)}) collective-permute-start(f32[512,128]{1,0:T(8,128)S(1)} %get-tuple-element.35), channel_id=1, source_target_pairs={{0,96},{8,104},{16,112},{24,120},{32,0},{40,8},{48,16},{56,24},{64... | collective-permute-start | bytes 786440 | tf_op jit(solution)/shard_map/ppermute | solution.py:493
  7.9 33.2 %copy-start = (bf16[16,3,64,64]{3,2,1,0:T(8,128)(2,1)S(1)}, bf16[16,3,64,64]{3,2,1,0:T(8,128)(2,1)}, u32[]{:S(2)}) copy-start(bf16[16,3,64,64]{3,2,1,0:T(8,128)(2,1)} %table.3) | copy-start | bytes 1179652
  7.9 69.6 %copy-start.1 = (f32[1,29]{1,0:T(1,128)S(1)}, f32[1,29]{1,0:T(1,128)}, u32[]{:S(2)}) copy-start(f32[1,29]{1,0:T(1,128)} %constant.2.clone.counts) | copy-start | bytes 352
  7.9 14.3 %collective-permute-start.4 = (f32[520,128]{1,0:T(8,128)S(1)}, f32[520,128]{1,0:T(8,128)S(1)}, u32[]{:S(2)}, u32[]{:S(2)}) collective-permute-start(f32[520,128]{1,0:T(8,128)S(1)} %get-tuple-element.38), channel_id=1, source_target_pairs={{0,96},{8,104},{16,112},{24,120},{32,0},{40,8},{48,16},{56,24},{64... | collective-permute-start | bytes 798728 | tf_op jit(solution)/shard_map/ppermute | solution.py:496
  13.0 11.0 %collective-permute-start.2 = (f32[520,128]{1,0:T(8,128)S(1)}, f32[520,128]{1,0:T(8,128)S(1)}, u32[]{:S(2)}, u32[]{:S(2)}) collective-permute-start(f32[520,128]{1,0:T(8,128)S(1)} %get-tuple-element.36), channel_id=1, source_target_pairs={{0,32},{8,40},{16,48},{24,56},{32,64},{40,72},{48,80},{56,88},{64,... | collective-permute-start | bytes 798728 | tf_op jit(solution)/shard_map/ppermute | solution.py:499
  14.4 7.9 %collective-permute-start.3 = (f32[512,128]{1,0:T(8,128)S(1)}, f32[512,128]{1,0:T(8,128)S(1)}, u32[]{:S(2)}, u32[]{:S(2)}) collective-permute-start(f32[512,128]{1,0:T(8,128)S(1)} %get-tuple-element.37), channel_id=1, source_target_pairs={{0,32},{8,40},{16,48},{24,56},{32,64},{40,72},{48,80},{56,88},{64,... | collective-permute-start | bytes 786440 | tf_op jit(solution)/shard_map/ppermute | solution.py:495
  17.6 6.4 %collective-permute-start.5 = (f32[512,128]{1,0:T(8,128)S(1)}, f32[512,128]{1,0:T(8,128)S(1)}, u32[]{:S(2)}, u32[]{:S(2)}) collective-permute-start(f32[512,128]{1,0:T(8,128)S(1)} %get-tuple-element.39), channel_id=1, source_target_pairs={{0,96},{8,104},{16,112},{24,120},{32,0},{40,8},{48,16},{56,24},{64... | collective-permute-start | bytes 786440 | tf_op jit(solution)/shard_map/ppermute | solution.py:500
  24.2 6.6 %collective-permute-start.6 = (f32[264,128]{1,0:T(8,128)S(1)}, f32[264,128]{1,0:T(8,128)S(1)}, u32[]{:S(2)}, u32[]{:S(2)}) collective-permute-start(f32[264,128]{1,0:T(8,128)S(1)} %get-tuple-element.41), channel_id=1, source_target_pairs={{0,16},{8,24},{16,0},{24,8},{32,48},{40,56},{48,32},{56,40},{64,80... | collective-permute-start | bytes 405512 | tf_op jit(solution)/shard_map/ppermute | solution.py:505
  25.7 6.5 %collective-permute-start.7 = (f32[264,128]{1,0:T(8,128)S(1)}, f32[264,128]{1,0:T(8,128)S(1)}, u32[]{:S(2)}, u32[]{:S(2)}) collective-permute-start(f32[264,128]{1,0:T(8,128)S(1)} %get-tuple-element.42), channel_id=1, source_target_pairs={{0,8},{8,16},{16,24},{24,0},{32,40},{40,48},{48,56},{56,32},{64,72... | collective-permute-start | bytes 405512 | tf_op jit(solution)/shard_map/ppermute | solution.py:505
  26.4 5.8 %collective-permute-start.8 = (f32[264,128]{1,0:T(8,128)S(1)}, f32[264,128]{1,0:T(8,128)S(1)}, u32[]{:S(2)}, u32[]{:S(2)}) collective-permute-start(f32[264,128]{1,0:T(8,128)S(1)} %get-tuple-element.43), channel_id=1, source_target_pairs={{0,24},{8,0},{16,8},{24,16},{32,56},{40,32},{48,40},{56,48},{64,88... | collective-permute-start | bytes 405512 | tf_op jit(solution)/shard_map/ppermute | solution.py:505
  32.9 17.6 %all-to-all-start = ((f32[8,40,128]{2,1,0:T(8,128)}), f32[8,40,128]{2,1,0:T(8,128)S(1)}, u32[]{:S(2)}, u32[]{:S(2)}) async-start(f32[8,40,128]{2,1,0:T(8,128)} %reduce.1), calls=%async_computation | async-start | bytes 327680 | tf_op jit(solution)/shard_map/all_to_all | solution.py:509
  51.1 1.3 %collective-permute-start.9 = (f32[32,128]{1,0:T(8,128)S(1)}, f32[32,128]{1,0:T(8,128)S(1)}, u32[]{:S(2)}, u32[]{:S(2)}) collective-permute-start(f32[32,128]{1,0:T(8,128)S(1)} %divide.1.own), channel_id=1, source_target_pairs={{0,128},{128,0},{1,129},{129,1},{2,130},{130,2},{3,131},{131,3},{4... | collective-permute-start | bytes 49160 | tf_op jit(solution)/shard_map/ppermute | solution.py:511

commit v6 on v5

--- a/solution.py
+++ b/solution.py
@@ -118,18 +118,18 @@
     first = [chosen[p, 0] for p in range(2)]
 
     def transform(chunk):
-        lanes = pl.ds(pl.multiple_of(chunk * 256, 256), 256)
         for p in range(2):
-            both = jnp.concatenate([volume[p, 0, :, lanes], volume[p, 1, :, lanes]], axis=1)
+            tiles = []
+            for j in range(2):
+                tile = pl.ds(pl.multiple_of(chunk * 256 + j * 128, 128), 128)
+                real, imag = (volume[p, c, :, tile] for c in range(2))
+                tiles.append(jnp.concatenate([real[:, :GRID], imag[:, :GRID]], axis=1))
+                tiles.append(jnp.concatenate([real[:, GRID:], imag[:, GRID:]], axis=1))
+            both = jnp.concatenate(tiles, axis=1)
             along = jnp.dot(first[p], both * wedges[p], preferred_element_type=F32)
-            for j in range(2):
-                real = along[:, j * 128 : j * 128 + 128]
-                imag = along[:, 256 + j * 128 : 256 + j * 128 + 128]
-                even = jnp.where(low, real, pltpu.roll(imag, 64, 1))
-                odd = jnp.where(low, pltpu.roll(real, 64, 1), imag)
-                base = pl.multiple_of((chunk * 4 + j * 2) * PITCH, 4)
-                planes[p, pl.ds(base, GRID), :] = even
-                planes[p, pl.ds(base + PITCH, GRID), :] = odd
+            for j in range(4):
+                base = pl.multiple_of((chunk * 4 + j) * PITCH, 4)
+                planes[p, pl.ds(base, GRID), :] = along[:, j * 128 : j * 128 + 128]
 
     for k in range(4):
         volumes[k].wait()
@@ -365,7 +365,7 @@
     )(parts, third, grown, second_sums)
 
 
-def spectra_kernel(own, other, out, maps, rows):
+def spectra_kernel(own, other, out, rows):
     on_first = lax.axis_index("half") == 0
     a, b = own[...], other[...]
     cross = a * b
@@ -393,7 +393,46 @@
         rest = rest - piece.astype(F32)
         total += lax.dot_general(ones, piece, (((1,), (1,)), ((), ())), preferred_element_type=F32)
     for k in range(ROWS):
+        out[k] = total[0:1]
+
+
+def spectra(own, other):
+    return pl.pallas_call(
+        spectra_kernel,
+        out_shape=jax.ShapeDtypeStruct((ROWS, 1, 128), F32),
+        in_specs=[VMEM, VMEM],
+        out_specs=VMEM,
+        scratch_shapes=[pltpu.VMEM((128, 128), F32)],
+        compiler_params=SMALL,
+        name="spectra",
+    )(own, other)
+
+
+def spread_kernel(parts, out):
+    total = jnp.sum(parts[...], axis=0)
+    for k in range(COLS):
         out[k] = total
+
+
+def spread_sum(parts):
+    return pl.pallas_call(
+        spread_kernel,
+        out_shape=jax.ShapeDtypeStruct((COLS, 1, 128), F32),
+        in_specs=[VMEM],
+        out_specs=VMEM,
+        compiler_params=SMALL,
+        name="spread_sum",
+    )(parts)
+
+
+def finish_kernel(parts, own, counts, maps, power, correlation):
+    total = jnp.sum(parts[...], axis=0)
+    cross = total[0:1, 0:SHELLS]
+    first = total[0:1, 32 : 32 + SHELLS]
+    second = total[0:1, 64 : 64 + SHELLS]
+    power[0:1, :] = first / counts[...]
+    power[1:2, :] = second / counts[...]
+    correlation[...] = cross / jnp.sqrt(first * second + 1e-06)
     low = iota((SECOND // 2, 128), 1) < GRID
     for i in range(FIRST):
         even = own[pl.ds(i * SECOND, SECOND // 2, stride=2), :]
@@ -406,60 +445,19 @@
             maps[0, 1, i : i + 1, lanes] = imag[j : j + 1]
 
 
-def spectra(own, other):
-    return pl.pallas_call(
-        spectra_kernel,
-        out_shape=(
-            jax.ShapeDtypeStruct((ROWS, 8, 128), F32),
-            jax.ShapeDtypeStruct((1, 2, FIRST, SECOND * GRID), F32),
-        ),
-        in_specs=[VMEM, VMEM],
-        out_specs=(VMEM, VMEM),
-        scratch_shapes=[pltpu.VMEM((128, 128), F32)],
-        compiler_params=SMALL,
-        name="spectra",
-    )(own, other)
-
-
-def spread_kernel(parts, out):
-    total = jnp.sum(parts[...], axis=0)
-    for k in range(COLS):
-        out[k] = total
-
-
-def spread_sum(parts):
-    return pl.pallas_call(
-        spread_kernel,
-        out_shape=jax.ShapeDtypeStruct((COLS, 8, 128), F32),
-        in_specs=[VMEM],
-        out_specs=VMEM,
-        compiler_params=SMALL,
-        name="spread_sum",
-    )(parts)
-
-
-def finish_kernel(parts, counts, power, correlation):
-    total = jnp.sum(parts[...], axis=0)
-    cross = total[0:1, 0:SHELLS]
-    first = total[0:1, 32 : 32 + SHELLS]
-    second = total[0:1, 64 : 64 + SHELLS]
-    power[0:1, :] = first / counts[...]
-    power[1:2, :] = second / counts[...]
-    correlation[...] = cross / jnp.sqrt(first * second + 1e-06)
-
-
-def finish(parts, counts):
+def finish(parts, own, counts):
     return pl.pallas_call(
         finish_kernel,
         out_shape=(
+            jax.ShapeDtypeStruct((1, 2, FIRST, SECOND * GRID), F32),
             jax.ShapeDtypeStruct((2, SHELLS), F32),
             jax.ShapeDtypeStruct((1, SHELLS), F32),
         ),
-        in_specs=[VMEM, VMEM],
-        out_specs=(VMEM, VMEM),
+        in_specs=[VMEM] * 3,
+        out_specs=(VMEM,) * 3,
         compiler_params=SMALL,
         name="finish",
-    )(parts, counts)
+    )(parts, own, counts)
 
 
 def shifted(shift, swapped=False):
@@ -509,10 +507,9 @@
     parts = lax.all_to_all(blocks, "col", 0, 0, tiled=True)
     own = divide(parts, *prepared)
     other = lax.ppermute(own, "half", [(0, 1), (1, 0)])
-    sums, half_maps = spectra(own, other)
-    parts = lax.all_to_all(sums, ROW, 0, 0, tiled=True)
+    parts = lax.all_to_all(spectra(own, other), ROW, 0, 0, tiled=True)
     parts = lax.all_to_all(spread_sum(parts), "col", 0, 0, tiled=True)
-    power, correlation = finish(parts, jnp.asarray(shell_counts()))
+    half_maps, power, correlation = finish(parts, own, jnp.asarray(shell_counts()))
     return half_maps, power, correlation
 
 

time: 78.5 us -> 77.2 us (0.983)
  Pallas kernels: 10.9 us -> 9.88 us
where the time goes in v6:
time: 77.2 us; the launch traced here: 76.9 us
  blocking collectives  24 us (31%)
  starting transfers between devices  23.4 us (30%)
  waiting for transfers between devices  18.9 us (24%)
  Pallas kernels  9.88 us (13%)
    all_to_all x1, blocking collectives, local(): parts = lax.all_to_all(spectra(own, other), ROW, 0, 0, tiled=True)  13.9 us
    all_to_all x1, blocking collectives, local(): parts = lax.all_to_all(spread_sum(parts), 'col', 0, 0, tiled=True)  10.1 us
    all_to_all x1, starting transfers between devices, local(): parts = lax.all_to_all(blocks, 'col', 0, 0, tiled=True)  8.22 us
    all_to_all x1, waiting for transfers between devices, local(): parts = lax.all_to_all(blocks, 'col', 0, 0, tiled=True)  7.18 us
    ppermute x3, starting transfers between devices, local(): lax.ppermute(block, HALF_ROW, shifted(shift, True))  4.81 us
    ppermute x1, waiting for transfers between devices, local(): after_high = lax.ppermute(after_high, HALF_ROW, shifted(1))  4.63 us
    pallas_call x1, Pallas kernels, first_slab(): pl.pallas_call(first_kernel, out_shape=(jax.ShapeDtypeStruct((2, GRID * P...  3.77 us
    ppermute x3, waiting for transfers between devices, local(): lax.ppermute(block, HALF_ROW, shifted(shift, True))  3.24 us
  transfers between devices with their start and end apart: 11, of which 7 were waited for; matrix products, arithmetic and copies ran while one was open for 0% of the time, Pallas kernels for 5%

profile of v6, /device:TPU:2, one launch (start us, length us, event | category | flops | bytes accessed | tf_op | source)
XLA Modules:
  0.0 76.9 jit_solution(4026617173203844256)
XLA Ops:
  0.6 3.8 %first_slab.1 = (f32[2,4352,128]{2,1,0:T(8,128)S(1)}, bf16[2,64,64]{2,1,0:T(8,128)(2,1)S(1)}, bf16[256,128]{1,0:T(8,128)(2,1)S(1)}, f32[8,128]{1,0:T(8,128)S(1)}...) custom-call(s32[2]{0:T(128)} %bins_in.1, s32[2,2]{1,0:T(2,128)} %slopes_in.1, bf16[2,2,64,4096]{3,2,1,0:T(8,128)(2,1)} %particles.1, ...), custom_call_target="tpu_custom_call" | custom-call | flops 1000000000 | bytes 4194304 | tf_op jit(solution)/shard_map/first_slab/pallas_call | solution.py:146
  4.4 1.6 %collective-permute-start = (f32[520,128]{1,0:T(8,128)S(1)}, f32[520,128]{1,0:T(8,128)S(1)}, u32[]{:S(2)}, u32[]{:S(2)}) collective-permute-start(f32[520,128]{1,0:T(8,128)S(1)} %get-tuple-element.29), channel_id=1, source_target_pairs={{0,32},{8,40},{16,48},{24,56},{32,64},{40,72},{48,80},{56,88},{64,... | collective-permute-start | bytes 798728 | tf_op jit(solution)/shard_map/ppermute | solution.py:490
  6.0 0.8 %collective-permute-start.1 = (f32[512,128]{1,0:T(8,128)S(1)}, f32[512,128]{1,0:T(8,128)S(1)}, u32[]{:S(2)}, u32[]{:S(2)}) collective-permute-start(f32[512,128]{1,0:T(8,128)S(1)} %get-tuple-element.31), channel_id=1, source_target_pairs={{0,96},{8,104},{16,112},{24,120},{32,0},{40,8},{48,16},{56,24},{64... | collective-permute-start | bytes 786440 | tf_op jit(solution)/shard_map/ppermute | solution.py:491
  6.8 0.5 direct_slabs.1
  7.4 3.2 %collective-permute-start.4 = (f32[520,128]{1,0:T(8,128)S(1)}, f32[520,128]{1,0:T(8,128)S(1)}, u32[]{:S(2)}, u32[]{:S(2)}) collective-permute-start(f32[520,128]{1,0:T(8,128)S(1)} %get-tuple-element.34), channel_id=1, source_target_pairs={{0,96},{8,104},{16,112},{24,120},{32,0},{40,8},{48,16},{56,24},{64... | collective-permute-start | bytes 798728 | tf_op jit(solution)/shard_map/ppermute | solution.py:494
  10.6 0.8 %other_slabs.1 = (f32[520,128]{1,0:T(8,128)S(1)}, f32[512,128]{1,0:T(8,128)S(1)}, f32[1032,128]{1,0:T(8,128)S(1)}) custom-call(f32[2,4352,128]{2,1,0:T(8,128)S(1)} %get-tuple-element.23.planes, bf16[2,64,64]{2,1,0:T(8,128)(2,1)S(1)} %get-tuple-element.24.second, bf16[256,128]{1,0:T(8,128)(2,1)S(1)} %get-tuple-element.25.third, ...), custom_call_target="tpu_custom_call" | custom-call | flops 1000000000 | bytes 1048576 | tf_op jit(solution)/shard_map/other_slabs/pallas_call | solution.py:195
  11.4 1.0 %collective-permute-done.1.far_high = f32[512,128]{1,0:T(8,128)S(1)} collective-permute-done((f32[512,128]{1,0:T(8,128)S(1)}, f32[512,128]{1,0:T(8,128)S(1)}, u32[]{:S(2)}, u32[]{:S(2)}) %collective-permute-start.1) | collective-permute-done | bytes 262176 | tf_op jit(solution)/shard_map/ppermute | solution.py:491
  12.4 1.4 %collective-permute-start.2 = (f32[520,128]{1,0:T(8,128)S(1)}, f32[520,128]{1,0:T(8,128)S(1)}, u32[]{:S(2)}, u32[]{:S(2)}) collective-permute-start(f32[520,128]{1,0:T(8,128)S(1)} %get-tuple-element.32), channel_id=1, source_target_pairs={{0,32},{8,40},{16,48},{24,56},{32,64},{40,72},{48,80},{56,88},{64,... | collective-permute-start | bytes 798728 | tf_op jit(solution)/shard_map/ppermute | solution.py:497
  13.9 3.2 %collective-permute-start.3 = (f32[512,128]{1,0:T(8,128)S(1)}, f32[512,128]{1,0:T(8,128)S(1)}, u32[]{:S(2)}, u32[]{:S(2)}) collective-permute-start(f32[512,128]{1,0:T(8,128)S(1)} %get-tuple-element.33), channel_id=1, source_target_pairs={{0,32},{8,40},{16,48},{24,56},{32,64},{40,72},{48,80},{56,88},{64,... | collective-permute-start | bytes 786440 | tf_op jit(solution)/shard_map/ppermute | solution.py:493
  17.1 4.6 %collective-permute-done.3.after_high = f32[512,128]{1,0:T(8,128)S(1)} collective-permute-done((f32[512,128]{1,0:T(8,128)S(1)}, f32[512,128]{1,0:T(8,128)S(1)}, u32[]{:S(2)}, u32[]{:S(2)}) %collective-permute-start.3) | collective-permute-done | bytes 262176 | tf_op jit(solution)/shard_map/ppermute | solution.py:493
  21.7 1.7 %collective-permute-done.5.before_high = f32[512,128]{1,0:T(8,128)S(1)} collective-permute-done((f32[512,128]{1,0:T(8,128)S(1)}, f32[512,128]{1,0:T(8,128)S(1)}, u32[]{:S(2)}, u32[]{:S(2)}) %collective-permute-start.5) | collective-permute-done | bytes 262176 | tf_op jit(solution)/shard_map/ppermute | solution.py:498
  23.6 1.6 %collective-permute-start.6 = (f32[264,128]{1,0:T(8,128)S(1)}, f32[264,128]{1,0:T(8,128)S(1)}, u32[]{:S(2)}, u32[]{:S(2)}) collective-permute-start(f32[264,128]{1,0:T(8,128)S(1)} %get-tuple-element.37), channel_id=1, source_target_pairs={{0,16},{8,24},{16,0},{24,8},{32,48},{40,56},{48,32},{56,40},{64,80... | collective-permute-start | bytes 405512 | tf_op jit(solution)/shard_map/ppermute | solution.py:503
  25.2 0.7 collective-permute-start.7
  25.9 2.6 %collective-permute-start.8 = (f32[264,128]{1,0:T(8,128)S(1)}, f32[264,128]{1,0:T(8,128)S(1)}, u32[]{:S(2)}, u32[]{:S(2)}) collective-permute-start(f32[264,128]{1,0:T(8,128)S(1)} %get-tuple-element.39), channel_id=1, source_target_pairs={{0,24},{8,0},{16,8},{24,16},{32,56},{40,32},{48,40},{56,48},{64,88... | collective-permute-start | bytes 405512 | tf_op jit(solution)/shard_map/ppermute | solution.py:503
  28.4 1.8 %collective-permute-done.6.refs_1_ = f32[264,128]{1,0:T(8,128)S(1)} collective-permute-done((f32[264,128]{1,0:T(8,128)S(1)}, f32[264,128]{1,0:T(8,128)S(1)}, u32[]{:S(2)}, u32[]{:S(2)}) %collective-permute-start.6) | collective-permute-done | bytes 135200 | tf_op jit(solution)/shard_map/ppermute | solution.py:503
  30.2 1.4 %collective-permute-done.7.refs_2_ = f32[264,128]{1,0:T(8,128)S(1)} collective-permute-done((f32[264,128]{1,0:T(8,128)S(1)}, f32[264,128]{1,0:T(8,128)S(1)}, u32[]{:S(2)}, u32[]{:S(2)}) %collective-permute-start.7) | collective-permute-done | bytes 135200 | tf_op jit(solution)/shard_map/ppermute | solution.py:503
  31.7 0.7 reduce.1
  32.4 8.2 %all-to-all-start = ((f32[8,40,128]{2,1,0:T(8,128)}), f32[8,40,128]{2,1,0:T(8,128)S(1)}, u32[]{:S(2)}, u32[]{:S(2)}) async-start(f32[8,40,128]{2,1,0:T(8,128)} %reduce.1), calls=%async_computation | async-start | bytes 327680 | tf_op jit(solution)/shard_map/all_to_all | solution.py:507
  40.6 2.2 %operators.1 = (bf16[128,2048]{1,0:T(8,128)(2,1)S(1)}, f32[64,3712]{1,0:T(8,128)S(1)}, f32[16,8,128]{2,1,0:T(8,128)S(1)}) custom-call(bf16[16,3,64,64]{3,2,1,0:T(8,128)(2,1)S(1)} %copy-done), custom_call_target="tpu_custom_call" | custom-call | flops 100000000 | bytes 1048576 | tf_op jit(solution)/shard_map/operators/pallas_call | solution.py:307
  42.8 7.2 %all-to-all-done.parts = f32[8,40,128]{2,1,0:T(8,128)S(1)} async-done(((f32[8,40,128]{2,1,0:T(8,128)}), f32[8,40,128]{2,1,0:T(8,128)S(1)}, u32[]{:S(2)}, u32[]{:S(2)}) %all-to-all-start) | async-done | bytes 163872 | tf_op jit(solution)/shard_map/all_to_all | solution.py:507
  50.6 1.2 %collective-permute-done.9.other = f32[32,128]{1,0:T(8,128)S(1)} collective-permute-done((f32[32,128]{1,0:T(8,128)S(1)}, f32[32,128]{1,0:T(8,128)S(1)}, u32[]{:S(2)}, u32[]{:S(2)}) %collective-permute-start.9) | collective-permute-done | bytes 16416 | tf_op jit(solution)/shard_map/ppermute | solution.py:509
  52.2 13.9 %all_to_all.15.parts = f32[16,1,128]{2,1,0:T(1,128)S(1)} all-to-all(f32[16,1,128]{2,1,0:T(1,128)S(1)} %spectra.1), channel_id=1, replica_groups=mesh['half'=2,'row_0'=4,'row_1'=4,'col'=8] {'row_0','row_1'}, dimensions={0} | all-to-all | bytes 16384 | tf_op jit(solution)/shard_map/all_to_all | solution.py:510
  66.1 10.1 %all_to_all.16.parts = f32[8,1,128]{2,1,0:T(1,128)S(1)} all-to-all(f32[8,1,128]{2,1,0:T(1,128)S(1)} %spread_sum.1), channel_id=1, replica_groups=mesh['half'=2,'row_0'=4,'row_1'=4,'col'=8] {'col'}, dimensions={0} | all-to-all | bytes 8192 | tf_op jit(solution)/shard_map/all_to_all | solution.py:511
  76.2 0.8 finish.1
  (15 shorter events, 1.2 us)
Async XLA Ops:
  4.4 7.9 %collective-permute-start = (f32[520,128]{1,0:T(8,128)S(1)}, f32[520,128]{1,0:T(8,128)S(1)}, u32[]{:S(2)}, u32[]{:S(2)}) collective-permute-start(f32[520,128]{1,0:T(8,128)S(1)} %get-tuple-element.29), channel_id=1, source_target_pairs={{0,32},{8,40},{16,48},{24,56},{32,64},{40,72},{48,80},{56,88},{64,... | collective-permute-start | bytes 798728 | tf_op jit(solution)/shard_map/ppermute | solution.py:490
  6.0 6.4 %collective-permute-start.1 = (f32[512,128]{1,0:T(8,128)S(1)}, f32[512,128]{1,0:T(8,128)S(1)}, u32[]{:S(2)}, u32[]{:S(2)}) collective-permute-start(f32[512,128]{1,0:T(8,128)S(1)} %get-tuple-element.31), channel_id=1, source_target_pairs={{0,96},{8,104},{16,112},{24,120},{32,0},{40,8},{48,16},{56,24},{64... | collective-permute-start | bytes 786440 | tf_op jit(solution)/shard_map/ppermute | solution.py:491
  7.3 33.2 %copy-start = (bf16[16,3,64,64]{3,2,1,0:T(8,128)(2,1)S(1)}, bf16[16,3,64,64]{3,2,1,0:T(8,128)(2,1)}, u32[]{:S(2)}) copy-start(bf16[16,3,64,64]{3,2,1,0:T(8,128)(2,1)} %table.3) | copy-start | bytes 1179652
  7.4 68.8 %copy-start.1 = (f32[1,29]{1,0:T(1,128)S(1)}, f32[1,29]{1,0:T(1,128)}, u32[]{:S(2)}) copy-start(f32[1,29]{1,0:T(1,128)} %constant.2.clone.counts) | copy-start | bytes 352
  7.4 14.3 %collective-permute-start.4 = (f32[520,128]{1,0:T(8,128)S(1)}, f32[520,128]{1,0:T(8,128)S(1)}, u32[]{:S(2)}, u32[]{:S(2)}) collective-permute-start(f32[520,128]{1,0:T(8,128)S(1)} %get-tuple-element.34), channel_id=1, source_target_pairs={{0,96},{8,104},{16,112},{24,120},{32,0},{40,8},{48,16},{56,24},{64... | collective-permute-start | bytes 798728 | tf_op jit(solution)/shard_map/ppermute | solution.py:494
  12.4 11.0 %collective-permute-start.2 = (f32[520,128]{1,0:T(8,128)S(1)}, f32[520,128]{1,0:T(8,128)S(1)}, u32[]{:S(2)}, u32[]{:S(2)}) collective-permute-start(f32[520,128]{1,0:T(8,128)S(1)} %get-tuple-element.32), channel_id=1, source_target_pairs={{0,32},{8,40},{16,48},{24,56},{32,64},{40,72},{48,80},{56,88},{64,... | collective-permute-start | bytes 798728 | tf_op jit(solution)/shard_map/ppermute | solution.py:497
  13.9 7.9 %collective-permute-start.3 = (f32[512,128]{1,0:T(8,128)S(1)}, f32[512,128]{1,0:T(8,128)S(1)}, u32[]{:S(2)}, u32[]{:S(2)}) collective-permute-start(f32[512,128]{1,0:T(8,128)S(1)} %get-tuple-element.33), channel_id=1, source_target_pairs={{0,32},{8,40},{16,48},{24,56},{32,64},{40,72},{48,80},{56,88},{64,... | collective-permute-start | bytes 786440 | tf_op jit(solution)/shard_map/ppermute | solution.py:493
  17.1 6.4 %collective-permute-start.5 = (f32[512,128]{1,0:T(8,128)S(1)}, f32[512,128]{1,0:T(8,128)S(1)}, u32[]{:S(2)}, u32[]{:S(2)}) collective-permute-start(f32[512,128]{1,0:T(8,128)S(1)} %get-tuple-element.35), channel_id=1, source_target_pairs={{0,96},{8,104},{16,112},{24,120},{32,0},{40,8},{48,16},{56,24},{64... | collective-permute-start | bytes 786440 | tf_op jit(solution)/shard_map/ppermute | solution.py:498
  23.6 6.6 %collective-permute-start.6 = (f32[264,128]{1,0:T(8,128)S(1)}, f32[264,128]{1,0:T(8,128)S(1)}, u32[]{:S(2)}, u32[]{:S(2)}) collective-permute-start(f32[264,128]{1,0:T(8,128)S(1)} %get-tuple-element.37), channel_id=1, source_target_pairs={{0,16},{8,24},{16,0},{24,8},{32,48},{40,56},{48,32},{56,40},{64,80... | collective-permute-start | bytes 405512 | tf_op jit(solution)/shard_map/ppermute | solution.py:503
  25.2 6.5 %collective-permute-start.7 = (f32[264,128]{1,0:T(8,128)S(1)}, f32[264,128]{1,0:T(8,128)S(1)}, u32[]{:S(2)}, u32[]{:S(2)}) collective-permute-start(f32[264,128]{1,0:T(8,128)S(1)} %get-tuple-element.38), channel_id=1, source_target_pairs={{0,8},{8,16},{16,24},{24,0},{32,40},{40,48},{48,56},{56,32},{64,72... | collective-permute-start | bytes 405512 | tf_op jit(solution)/shard_map/ppermute | solution.py:503
  25.9 5.8 %collective-permute-start.8 = (f32[264,128]{1,0:T(8,128)S(1)}, f32[264,128]{1,0:T(8,128)S(1)}, u32[]{:S(2)}, u32[]{:S(2)}) collective-permute-start(f32[264,128]{1,0:T(8,128)S(1)} %get-tuple-element.39), channel_id=1, source_target_pairs={{0,24},{8,0},{16,8},{24,16},{32,56},{40,32},{48,40},{56,48},{64,88... | collective-permute-start | bytes 405512 | tf_op jit(solution)/shard_map/ppermute | solution.py:503
  32.4 17.7 %all-to-all-start = ((f32[8,40,128]{2,1,0:T(8,128)}), f32[8,40,128]{2,1,0:T(8,128)S(1)}, u32[]{:S(2)}, u32[]{:S(2)}) async-start(f32[8,40,128]{2,1,0:T(8,128)} %reduce.1), calls=%async_computation | async-start | bytes 327680 | tf_op jit(solution)/shard_map/all_to_all | solution.py:507
  50.5 1.3 %collective-permute-start.9 = (f32[32,128]{1,0:T(8,128)S(1)}, f32[32,128]{1,0:T(8,128)S(1)}, u32[]{:S(2)}, u32[]{:S(2)}) collective-permute-start(f32[32,128]{1,0:T(8,128)S(1)} %divide.1.own), channel_id=1, source_target_pairs={{0,128},{128,0},{1,129},{129,1},{2,130},{130,2},{3,131},{131,3},{4... | collective-permute-start | bytes 49160 | tf_op jit(solution)/shard_map/ppermute | solution.py:509

commit v7 on v6

--- a/solution.py
+++ b/solution.py
@@ -93,29 +93,24 @@
         )
         for k in range(4)
     ]
-    for copy in (*scalars, volumes[0]):
+    whole = pltpu.make_async_copy(table, chosen, sem.at[4])
+    for copy in (*scalars, whole, *volumes):
         copy.start()
     third[...] = jnp.zeros_like(third)
     low = iota((GRID, 128), 1) < GRID
     for copy in scalars:
         copy.wait()
-    tables = [
-        pltpu.make_async_copy(table.at[bins[p]], chosen.at[p], sem.at[4 + p]) for p in range(2)
-    ]
-    for copy in (*tables, *volumes[1:]):
-        copy.start()
     wedges = [
         jnp.concatenate([wedge_tile(slopes[p, 0], slopes[p, 1])] * 4, axis=1) for p in range(2)
     ]
     counts[...] = histogram_tile(bins, slopes)
-    for copy in tables:
-        copy.wait()
+    whole.wait()
     for p in range(2):
-        second[p] = chosen[p, 1]
-        transposed = chosen[p, 2].astype(F32).T.astype(BF16)
+        second[p] = chosen[bins[p], 1]
+        transposed = chosen[bins[p], 2].astype(F32).T.astype(BF16)
         for c in range(2):
             third[p * 128 + c * 64 : p * 128 + c * 64 + 64, c * 64 : c * 64 + 64] = transposed
-    first = [chosen[p, 0] for p in range(2)]
+    first = [chosen[bins[p], 0] for p in range(2)]
 
     def transform(chunk):
         for p in range(2):
@@ -157,7 +152,7 @@
         out_specs=(VMEM,) * 6,
         scratch_shapes=[
             pltpu.VMEM((2, 2, GRID, GRID * GRID), BF16),
-            pltpu.VMEM((2, 3, GRID, GRID), BF16),
+            pltpu.VMEM((BINS, 3, GRID, GRID), BF16),
             pltpu.SMEM((2,), jnp.int32),
             pltpu.SMEM((2, 2), jnp.int32),
             pltpu.SemaphoreType.DMA((8,)),
@@ -230,7 +225,7 @@
     for n, parts in enumerate(((after_low, before_low), (after_high, before_high))):
         span = pl.ds(n * half, half)
         sums[span, :] = own[span, :] + parts[0][0:half, :] + parts[1][0:half, :]
-    for shift, out in zip((2, 1, 3, 0), outs, strict=True):
+    for shift, out in zip((1, 3, 2, 0), outs, strict=True):
         span = pl.ds(pl.multiple_of(lax.rem(mine + shift, SIDE) * BLOCK, 8), BLOCK)
         out[0:BLOCK, :] = sums[span, :]
         out[BLOCK : BLOCK + 8, :] = counts
@@ -501,7 +496,7 @@
     *others, own = gather(*parts)
     parts = [
         lax.ppermute(block, HALF_ROW, shifted(shift, True))
-        for shift, block in zip((2, 1, 3), others, strict=True)
+        for shift, block in zip((1, 3, 2), others, strict=True)
     ]
     blocks = reduce(own, *parts)
     parts = lax.all_to_all(blocks, "col", 0, 0, tiled=True)

time: 77.2 us -> 75.5 us (0.978)
  waiting for transfers between devices: 18.9 us -> 21.9 us
  starting transfers between devices: 23.4 us -> 20.7 us
  blocking collectives: 24 us -> 22.4 us
    ppermute x3, waiting for transfers between devices: 3.24 us -> 6.24 us  [local(): lax.ppermute(block, HALF_ROW, shifted(shift, True))]
    all_to_all x1, blocking collectives: 13.9 us -> 12.3 us  [local(): parts = lax.all_to_all(spectra(own, other), ROW, 0, 0, tiled=True)]
    all_to_all x1, starting transfers between devices: 8.22 us -> 6.76 us  [local(): parts = lax.all_to_all(blocks, 'col', 0, 0, tiled=True)]
    ppermute x3, starting transfers between devices: 4.81 us -> 3.58 us  [local(): lax.ppermute(block, HALF_ROW, shifted(shift, True))]
  transfers between devices with their start and end apart: 11 -> 11, of which waited for: 7 -> 8; matrix products, arithmetic and copies ran while one was open for 0% -> 0% of each run, Pallas kernels for 5% -> 5%
where the time goes in v7:
time: 75.5 us; the launch traced here: 75.3 us
  blocking collectives  22.4 us (30%)
  waiting for transfers between devices  21.9 us (29%)
  starting transfers between devices  20.7 us (27%)
  Pallas kernels  9.47 us (13%)
    all_to_all x1, blocking collectives, local(): parts = lax.all_to_all(spectra(own, other), ROW, 0, 0, tiled=True)  12.3 us
    all_to_all x1, blocking collectives, local(): parts = lax.all_to_all(spread_sum(parts), 'col', 0, 0, tiled=True)  10.1 us
    all_to_all x1, waiting for transfers between devices, local(): parts = lax.all_to_all(blocks, 'col', 0, 0, tiled=True)  7.18 us
    all_to_all x1, starting transfers between devices, local(): parts = lax.all_to_all(blocks, 'col', 0, 0, tiled=True)  6.76 us
    ppermute x3, waiting for transfers between devices, local(): lax.ppermute(block, HALF_ROW, shifted(shift, True))  6.24 us
    ppermute x1, waiting for transfers between devices, local(): after_high = lax.ppermute(after_high, HALF_ROW, shifted(1))  4.63 us
    ppermute x3, starting transfers between devices, local(): lax.ppermute(block, HALF_ROW, shifted(shift, True))  3.58 us
    pallas_call x1, Pallas kernels, first_slab(): pl.pallas_call(first_kernel, out_shape=(jax.ShapeDtypeStruct((2, GRID * P...  3.36 us
  transfers between devices with their start and end apart: 11, of which 8 were waited for; matrix products, arithmetic and copies ran while one was open for 0% of the time, Pallas kernels for 5%

profile of v7, /device:TPU:2, one launch (start us, length us, event | category | flops | bytes accessed | tf_op | source)
XLA Modules:
  0.0 75.3 jit_solution(7901641919110492591)
XLA Ops:
  0.6 3.4 %first_slab.1 = (f32[2,4352,128]{2,1,0:T(8,128)S(1)}, bf16[2,64,64]{2,1,0:T(8,128)(2,1)S(1)}, bf16[256,128]{1,0:T(8,128)(2,1)S(1)}, f32[8,128]{1,0:T(8,128)S(1)}...) custom-call(s32[2]{0:T(128)} %bins_in.1, s32[2,2]{1,0:T(2,128)} %slopes_in.1, bf16[2,2,64,4096]{3,2,1,0:T(8,128)(2,1)} %particles.1, ...), custom_call_target="tpu_custom_call" | custom-call | flops 1000000000 | bytes 4194304 | tf_op jit(solution)/shard_map/first_slab/pallas_call | solution.py:141
  4.0 1.6 %collective-permute-start = (f32[520,128]{1,0:T(8,128)S(1)}, f32[520,128]{1,0:T(8,128)S(1)}, u32[]{:S(2)}, u32[]{:S(2)}) collective-permute-start(f32[520,128]{1,0:T(8,128)S(1)} %get-tuple-element.29), channel_id=1, source_target_pairs={{0,32},{8,40},{16,48},{24,56},{32,64},{40,72},{48,80},{56,88},{64,... | collective-permute-start | bytes 798728 | tf_op jit(solution)/shard_map/ppermute | solution.py:485
  5.6 0.8 %collective-permute-start.1 = (f32[512,128]{1,0:T(8,128)S(1)}, f32[512,128]{1,0:T(8,128)S(1)}, u32[]{:S(2)}, u32[]{:S(2)}) collective-permute-start(f32[512,128]{1,0:T(8,128)S(1)} %get-tuple-element.31), channel_id=1, source_target_pairs={{0,96},{8,104},{16,112},{24,120},{32,0},{40,8},{48,16},{56,24},{64... | collective-permute-start | bytes 786440 | tf_op jit(solution)/shard_map/ppermute | solution.py:486
  6.4 0.5 direct_slabs.1
  7.0 3.2 %collective-permute-start.4 = (f32[520,128]{1,0:T(8,128)S(1)}, f32[520,128]{1,0:T(8,128)S(1)}, u32[]{:S(2)}, u32[]{:S(2)}) collective-permute-start(f32[520,128]{1,0:T(8,128)S(1)} %get-tuple-element.34), channel_id=1, source_target_pairs={{0,96},{8,104},{16,112},{24,120},{32,0},{40,8},{48,16},{56,24},{64... | collective-permute-start | bytes 798728 | tf_op jit(solution)/shard_map/ppermute | solution.py:489
  10.2 0.8 %other_slabs.1 = (f32[520,128]{1,0:T(8,128)S(1)}, f32[512,128]{1,0:T(8,128)S(1)}, f32[1032,128]{1,0:T(8,128)S(1)}) custom-call(f32[2,4352,128]{2,1,0:T(8,128)S(1)} %get-tuple-element.23.planes, bf16[2,64,64]{2,1,0:T(8,128)(2,1)S(1)} %get-tuple-element.24.second, bf16[256,128]{1,0:T(8,128)(2,1)S(1)} %get-tuple-element.25.third, ...), custom_call_target="tpu_custom_call" | custom-call | flops 1000000000 | bytes 1048576 | tf_op jit(solution)/shard_map/other_slabs/pallas_call | solution.py:190
  11.0 0.9 %collective-permute-done.1.far_high = f32[512,128]{1,0:T(8,128)S(1)} collective-permute-done((f32[512,128]{1,0:T(8,128)S(1)}, f32[512,128]{1,0:T(8,128)S(1)}, u32[]{:S(2)}, u32[]{:S(2)}) %collective-permute-start.1) | collective-permute-done | bytes 262176 | tf_op jit(solution)/shard_map/ppermute | solution.py:486
  12.0 1.4 %collective-permute-start.2 = (f32[520,128]{1,0:T(8,128)S(1)}, f32[520,128]{1,0:T(8,128)S(1)}, u32[]{:S(2)}, u32[]{:S(2)}) collective-permute-start(f32[520,128]{1,0:T(8,128)S(1)} %get-tuple-element.32), channel_id=1, source_target_pairs={{0,32},{8,40},{16,48},{24,56},{32,64},{40,72},{48,80},{56,88},{64,... | collective-permute-start | bytes 798728 | tf_op jit(solution)/shard_map/ppermute | solution.py:492
  13.4 3.2 %collective-permute-start.3 = (f32[512,128]{1,0:T(8,128)S(1)}, f32[512,128]{1,0:T(8,128)S(1)}, u32[]{:S(2)}, u32[]{:S(2)}) collective-permute-start(f32[512,128]{1,0:T(8,128)S(1)} %get-tuple-element.33), channel_id=1, source_target_pairs={{0,32},{8,40},{16,48},{24,56},{32,64},{40,72},{48,80},{56,88},{64,... | collective-permute-start | bytes 786440 | tf_op jit(solution)/shard_map/ppermute | solution.py:488
  16.7 4.6 %collective-permute-done.3.after_high = f32[512,128]{1,0:T(8,128)S(1)} collective-permute-done((f32[512,128]{1,0:T(8,128)S(1)}, f32[512,128]{1,0:T(8,128)S(1)}, u32[]{:S(2)}, u32[]{:S(2)}) %collective-permute-start.3) | collective-permute-done | bytes 262176 | tf_op jit(solution)/shard_map/ppermute | solution.py:488
  21.3 1.7 %collective-permute-done.5.before_high = f32[512,128]{1,0:T(8,128)S(1)} collective-permute-done((f32[512,128]{1,0:T(8,128)S(1)}, f32[512,128]{1,0:T(8,128)S(1)}, u32[]{:S(2)}, u32[]{:S(2)}) %collective-permute-start.5) | collective-permute-done | bytes 262176 | tf_op jit(solution)/shard_map/ppermute | solution.py:493
  23.3 3.2 %collective-permute-start.7 = (f32[264,128]{1,0:T(8,128)S(1)}, f32[264,128]{1,0:T(8,128)S(1)}, u32[]{:S(2)}, u32[]{:S(2)}) collective-permute-start(f32[264,128]{1,0:T(8,128)S(1)} %get-tuple-element.38), channel_id=1, source_target_pairs={{0,24},{8,0},{16,8},{24,16},{32,56},{40,32},{48,40},{56,48},{64,88... | collective-permute-start | bytes 405512 | tf_op jit(solution)/shard_map/ppermute | solution.py:498
  26.8 2.7 %collective-permute-done.6.refs_1_ = f32[264,128]{1,0:T(8,128)S(1)} collective-permute-done((f32[264,128]{1,0:T(8,128)S(1)}, f32[264,128]{1,0:T(8,128)S(1)}, u32[]{:S(2)}, u32[]{:S(2)}) %collective-permute-start.6) | collective-permute-done | bytes 135200 | tf_op jit(solution)/shard_map/ppermute | solution.py:498
  29.5 1.0 %collective-permute-done.7.refs_2_ = f32[264,128]{1,0:T(8,128)S(1)} collective-permute-done((f32[264,128]{1,0:T(8,128)S(1)}, f32[264,128]{1,0:T(8,128)S(1)}, u32[]{:S(2)}, u32[]{:S(2)}) %collective-permute-start.7) | collective-permute-done | bytes 135200 | tf_op jit(solution)/shard_map/ppermute | solution.py:498
  30.5 2.5 %collective-permute-done.8.refs_3_ = f32[264,128]{1,0:T(8,128)S(1)} collective-permute-done((f32[264,128]{1,0:T(8,128)S(1)}, f32[264,128]{1,0:T(8,128)S(1)}, u32[]{:S(2)}, u32[]{:S(2)}) %collective-permute-start.8) | collective-permute-done | bytes 135200 | tf_op jit(solution)/shard_map/ppermute | solution.py:498
  33.0 0.7 reduce.1
  33.7 6.8 %all-to-all-start = ((f32[8,40,128]{2,1,0:T(8,128)}), f32[8,40,128]{2,1,0:T(8,128)S(1)}, u32[]{:S(2)}, u32[]{:S(2)}) async-start(f32[8,40,128]{2,1,0:T(8,128)} %reduce.1), calls=%async_computation | async-start | bytes 327680 | tf_op jit(solution)/shard_map/all_to_all | solution.py:502
  40.5 2.2 %operators.1 = (bf16[128,2048]{1,0:T(8,128)(2,1)S(1)}, f32[64,3712]{1,0:T(8,128)S(1)}, f32[16,8,128]{2,1,0:T(8,128)S(1)}) custom-call(bf16[16,3,64,64]{3,2,1,0:T(8,128)(2,1)S(1)} %copy-done), custom_call_target="tpu_custom_call" | custom-call | flops 100000000 | bytes 1048576 | tf_op jit(solution)/shard_map/operators/pallas_call | solution.py:302
  42.7 7.2 %all-to-all-done.parts = f32[8,40,128]{2,1,0:T(8,128)S(1)} async-done(((f32[8,40,128]{2,1,0:T(8,128)}), f32[8,40,128]{2,1,0:T(8,128)S(1)}, u32[]{:S(2)}, u32[]{:S(2)}) %all-to-all-start) | async-done | bytes 163872 | tf_op jit(solution)/shard_map/all_to_all | solution.py:502
  49.9 0.5 divide.1.own
  50.5 1.2 %collective-permute-done.9.other = f32[32,128]{1,0:T(8,128)S(1)} collective-permute-done((f32[32,128]{1,0:T(8,128)S(1)}, f32[32,128]{1,0:T(8,128)S(1)}, u32[]{:S(2)}, u32[]{:S(2)}) %collective-permute-start.9) | collective-permute-done | bytes 16416 | tf_op jit(solution)/shard_map/ppermute | solution.py:504
  52.1 12.3 %all_to_all.15.parts = f32[16,1,128]{2,1,0:T(1,128)S(1)} all-to-all(f32[16,1,128]{2,1,0:T(1,128)S(1)} %spectra.1), channel_id=1, replica_groups=mesh['half'=2,'row_0'=4,'row_1'=4,'col'=8] {'row_0','row_1'}, dimensions={0} | all-to-all | bytes 16384 | tf_op jit(solution)/shard_map/all_to_all | solution.py:505
  64.4 10.1 %all_to_all.16.parts = f32[8,1,128]{2,1,0:T(1,128)S(1)} all-to-all(f32[8,1,128]{2,1,0:T(1,128)S(1)} %spread_sum.1), channel_id=1, replica_groups=mesh['half'=2,'row_0'=4,'row_1'=4,'col'=8] {'col'}, dimensions={0} | all-to-all | bytes 8192 | tf_op jit(solution)/shard_map/all_to_all | solution.py:506
  74.5 0.8 %finish.1 = (f32[1,2,4,512]{3,2,1,0:T(4,128)}, f32[2,29]{1,0:T(2,128)}, f32[1,29]{1,0:T(1,128)}) custom-call(f32[8,1,128]{2,1,0:T(1,128)S(1)} %all_to_all.16.parts, f32[32,128]{1,0:T(8,128)S(1)} %divide.1.own, f32[1,29]{1,0:T(1,128)S(1)} %copy-done.1), custom_call_target="tpu_custom_call" | custom-call | tf_op jit(solution)/shard_map/finish/pallas_call | solution.py:444
  (15 shorter events, 1.1 us)
Async XLA Ops:
  4.0 7.9 %collective-permute-start = (f32[520,128]{1,0:T(8,128)S(1)}, f32[520,128]{1,0:T(8,128)S(1)}, u32[]{:S(2)}, u32[]{:S(2)}) collective-permute-start(f32[520,128]{1,0:T(8,128)S(1)} %get-tuple-element.29), channel_id=1, source_target_pairs={{0,32},{8,40},{16,48},{24,56},{32,64},{40,72},{48,80},{56,88},{64,... | collective-permute-start | bytes 798728 | tf_op jit(solution)/shard_map/ppermute | solution.py:485
  5.6 6.4 %collective-permute-start.1 = (f32[512,128]{1,0:T(8,128)S(1)}, f32[512,128]{1,0:T(8,128)S(1)}, u32[]{:S(2)}, u32[]{:S(2)}) collective-permute-start(f32[512,128]{1,0:T(8,128)S(1)} %get-tuple-element.31), channel_id=1, source_target_pairs={{0,96},{8,104},{16,112},{24,120},{32,0},{40,8},{48,16},{56,24},{64... | collective-permute-start | bytes 786440 | tf_op jit(solution)/shard_map/ppermute | solution.py:486
  6.9 33.6 %copy-start = (bf16[16,3,64,64]{3,2,1,0:T(8,128)(2,1)S(1)}, bf16[16,3,64,64]{3,2,1,0:T(8,128)(2,1)}, u32[]{:S(2)}) copy-start(bf16[16,3,64,64]{3,2,1,0:T(8,128)(2,1)} %table.3) | copy-start | bytes 1179652
  6.9 67.6 %copy-start.1 = (f32[1,29]{1,0:T(1,128)S(1)}, f32[1,29]{1,0:T(1,128)}, u32[]{:S(2)}) copy-start(f32[1,29]{1,0:T(1,128)} %constant.2.clone.counts) | copy-start | bytes 352
  7.0 14.3 %collective-permute-start.4 = (f32[520,128]{1,0:T(8,128)S(1)}, f32[520,128]{1,0:T(8,128)S(1)}, u32[]{:S(2)}, u32[]{:S(2)}) collective-permute-start(f32[520,128]{1,0:T(8,128)S(1)} %get-tuple-element.34), channel_id=1, source_target_pairs={{0,96},{8,104},{16,112},{24,120},{32,0},{40,8},{48,16},{56,24},{64... | collective-permute-start | bytes 798728 | tf_op jit(solution)/shard_map/ppermute | solution.py:489
  12.0 11.0 %collective-permute-start.2 = (f32[520,128]{1,0:T(8,128)S(1)}, f32[520,128]{1,0:T(8,128)S(1)}, u32[]{:S(2)}, u32[]{:S(2)}) collective-permute-start(f32[520,128]{1,0:T(8,128)S(1)} %get-tuple-element.32), channel_id=1, source_target_pairs={{0,32},{8,40},{16,48},{24,56},{32,64},{40,72},{48,80},{56,88},{64,... | collective-permute-start | bytes 798728 | tf_op jit(solution)/shard_map/ppermute | solution.py:492
  13.4 7.9 %collective-permute-start.3 = (f32[512,128]{1,0:T(8,128)S(1)}, f32[512,128]{1,0:T(8,128)S(1)}, u32[]{:S(2)}, u32[]{:S(2)}) collective-permute-start(f32[512,128]{1,0:T(8,128)S(1)} %get-tuple-element.33), channel_id=1, source_target_pairs={{0,32},{8,40},{16,48},{24,56},{32,64},{40,72},{48,80},{56,88},{64,... | collective-permute-start | bytes 786440 | tf_op jit(solution)/shard_map/ppermute | solution.py:488
  16.7 6.4 %collective-permute-start.5 = (f32[512,128]{1,0:T(8,128)S(1)}, f32[512,128]{1,0:T(8,128)S(1)}, u32[]{:S(2)}, u32[]{:S(2)}) collective-permute-start(f32[512,128]{1,0:T(8,128)S(1)} %get-tuple-element.35), channel_id=1, source_target_pairs={{0,96},{8,104},{16,112},{24,120},{32,0},{40,8},{48,16},{56,24},{64... | collective-permute-start | bytes 786440 | tf_op jit(solution)/shard_map/ppermute | solution.py:493
  23.2 6.3 %collective-permute-start.6 = (f32[264,128]{1,0:T(8,128)S(1)}, f32[264,128]{1,0:T(8,128)S(1)}, u32[]{:S(2)}, u32[]{:S(2)}) collective-permute-start(f32[264,128]{1,0:T(8,128)S(1)} %get-tuple-element.37), channel_id=1, source_target_pairs={{0,8},{8,16},{16,24},{24,0},{32,40},{40,48},{48,56},{56,32},{64,72... | collective-permute-start | bytes 405512 | tf_op jit(solution)/shard_map/ppermute | solution.py:498
  23.3 7.2 %collective-permute-start.7 = (f32[264,128]{1,0:T(8,128)S(1)}, f32[264,128]{1,0:T(8,128)S(1)}, u32[]{:S(2)}, u32[]{:S(2)}) collective-permute-start(f32[264,128]{1,0:T(8,128)S(1)} %get-tuple-element.38), channel_id=1, source_target_pairs={{0,24},{8,0},{16,8},{24,16},{32,56},{40,32},{48,40},{56,48},{64,88... | collective-permute-start | bytes 405512 | tf_op jit(solution)/shard_map/ppermute | solution.py:498
  26.5 6.5 %collective-permute-start.8 = (f32[264,128]{1,0:T(8,128)S(1)}, f32[264,128]{1,0:T(8,128)S(1)}, u32[]{:S(2)}, u32[]{:S(2)}) collective-permute-start(f32[264,128]{1,0:T(8,128)S(1)} %get-tuple-element.39), channel_id=1, source_target_pairs={{0,16},{8,24},{16,0},{24,8},{32,48},{40,56},{48,32},{56,40},{64,80... | collective-permute-start | bytes 405512 | tf_op jit(solution)/shard_map/ppermute | solution.py:498
  33.7 16.2 %all-to-all-start = ((f32[8,40,128]{2,1,0:T(8,128)}), f32[8,40,128]{2,1,0:T(8,128)S(1)}, u32[]{:S(2)}, u32[]{:S(2)}) async-start(f32[8,40,128]{2,1,0:T(8,128)} %reduce.1), calls=%async_computation | async-start | bytes 327680 | tf_op jit(solution)/shard_map/all_to_all | solution.py:502
  50.4 1.3 %collective-permute-start.9 = (f32[32,128]{1,0:T(8,128)S(1)}, f32[32,128]{1,0:T(8,128)S(1)}, u32[]{:S(2)}, u32[]{:S(2)}) collective-permute-start(f32[32,128]{1,0:T(8,128)S(1)} %divide.1.own), channel_id=1, source_target_pairs={{0,128},{128,0},{1,129},{129,1},{2,130},{130,2},{3,131},{131,3},{4... | collective-permute-start | bytes 49160 | tf_op jit(solution)/shard_map/ppermute | solution.py:504

commit v8 on v7

--- a/solution.py
+++ b/solution.py
@@ -87,11 +87,11 @@
     ]
     volumes = [
         pltpu.make_async_copy(
-            particles.at[:, :, :, pl.ds(k * 1024, 1024)],
-            volume.at[:, :, :, pl.ds(k * 1024, 1024)],
+            particles.at[:, :, :, pl.ds(k * 2048, 2048)],
+            volume.at[:, :, :, pl.ds(k * 2048, 2048)],
             sem.at[k],
         )
-        for k in range(4)
+        for k in range(2)
     ]
     whole = pltpu.make_async_copy(table, chosen, sem.at[4])
     for copy in (*scalars, whole, *volumes):
@@ -126,10 +126,10 @@
                 base = pl.multiple_of((chunk * 4 + j) * PITCH, 4)
                 planes[p, pl.ds(base, GRID), :] = along[:, j * 128 : j * 128 + 128]
 
-    for k in range(4):
+    for k in range(2):
         volumes[k].wait()
 
-        @pl.loop(k * 4, k * 4 + 4, unroll=4)
+        @pl.loop(k * 8, k * 8 + 8, unroll=8)
         def _(chunk):
             transform(chunk)
 
@@ -387,14 +387,14 @@
         piece = rest.astype(BF16)
         rest = rest - piece.astype(F32)
         total += lax.dot_general(ones, piece, (((1,), (1,)), ((), ())), preferred_element_type=F32)
-    for k in range(ROWS):
+    for k in range(COLS):
         out[k] = total[0:1]
 
 
 def spectra(own, other):
     return pl.pallas_call(
         spectra_kernel,
-        out_shape=jax.ShapeDtypeStruct((ROWS, 1, 128), F32),
+        out_shape=jax.ShapeDtypeStruct((COLS, 1, 128), F32),
         in_specs=[VMEM, VMEM],
         out_specs=VMEM,
         scratch_shapes=[pltpu.VMEM((128, 128), F32)],
@@ -405,14 +405,14 @@
 
 def spread_kernel(parts, out):
     total = jnp.sum(parts[...], axis=0)
-    for k in range(COLS):
+    for k in range(ROWS):
         out[k] = total
 
 
 def spread_sum(parts):
     return pl.pallas_call(
         spread_kernel,
-        out_shape=jax.ShapeDtypeStruct((COLS, 1, 128), F32),
+        out_shape=jax.ShapeDtypeStruct((ROWS, 1, 128), F32),
         in_specs=[VMEM],
         out_specs=VMEM,
         compiler_params=SMALL,
@@ -502,8 +502,8 @@
     parts = lax.all_to_all(blocks, "col", 0, 0, tiled=True)
     own = divide(parts, *prepared)
     other = lax.ppermute(own, "half", [(0, 1), (1, 0)])
-    parts = lax.all_to_all(spectra(own, other), ROW, 0, 0, tiled=True)
-    parts = lax.all_to_all(spread_sum(parts), "col", 0, 0, tiled=True)
+    parts = lax.all_to_all(spectra(own, other), "col", 0, 0, tiled=True)
+    parts = lax.all_to_all(spread_sum(parts), ROW, 0, 0, tiled=True)
     half_maps, power, correlation = finish(parts, own, jnp.asarray(shell_counts()))
     return half_maps, power, correlation
 

time: 75.5 us -> 75.3 us (level)
  no operation moved by 1% of the time
where the time goes in v8:
time: 75.3 us; the launch traced here: 75 us
  blocking collectives  22.4 us (30%)
  waiting for transfers between devices  21.9 us (29%)
  starting transfers between devices  20.7 us (27%)
  Pallas kernels  9.16 us (12%)
    all_to_all x1, blocking collectives, local(): parts = lax.all_to_all(spread_sum(parts), ROW, 0, 0, tiled=True)  12.3 us
    all_to_all x1, blocking collectives, local(): parts = lax.all_to_all(spectra(own, other), 'col', 0, 0, tiled=True)  10.1 us
    all_to_all x1, waiting for transfers between devices, local(): parts = lax.all_to_all(blocks, 'col', 0, 0, tiled=True)  7.18 us
    all_to_all x1, starting transfers between devices, local(): parts = lax.all_to_all(blocks, 'col', 0, 0, tiled=True)  6.75 us
    ppermute x3, waiting for transfers between devices, local(): lax.ppermute(block, HALF_ROW, shifted(shift, True))  6.24 us
    ppermute x1, waiting for transfers between devices, local(): after_high = lax.ppermute(after_high, HALF_ROW, shifted(1))  4.62 us
    ppermute x3, starting transfers between devices, local(): lax.ppermute(block, HALF_ROW, shifted(shift, True))  3.58 us
    ppermute x1, starting transfers between devices, local(): after_high = lax.ppermute(after_high, HALF_ROW, shifted(1))  3.23 us
  transfers between devices with their start and end apart: 11, of which 8 were waited for; matrix products, arithmetic and copies ran while one was open for 0% of the time, Pallas kernels for 5%

profile of v8, /device:TPU:2, one launch (start us, length us, event | category | flops | bytes accessed | tf_op | source)
XLA Modules:
  0.0 75.0 jit_solution(8101319744496635595)
XLA Ops:
  0.6 3.1 %first_slab.1 = (f32[2,4352,128]{2,1,0:T(8,128)S(1)}, bf16[2,64,64]{2,1,0:T(8,128)(2,1)S(1)}, bf16[256,128]{1,0:T(8,128)(2,1)S(1)}, f32[8,128]{1,0:T(8,128)S(1)}...) custom-call(s32[2]{0:T(128)} %bins_in.1, s32[2,2]{1,0:T(2,128)} %slopes_in.1, bf16[2,2,64,4096]{3,2,1,0:T(8,128)(2,1)} %particles.1, ...), custom_call_target="tpu_custom_call" | custom-call | flops 1000000000 | bytes 4194304 | tf_op jit(solution)/shard_map/first_slab/pallas_call | solution.py:141
  3.7 1.6 %collective-permute-start = (f32[520,128]{1,0:T(8,128)S(1)}, f32[520,128]{1,0:T(8,128)S(1)}, u32[]{:S(2)}, u32[]{:S(2)}) collective-permute-start(f32[520,128]{1,0:T(8,128)S(1)} %get-tuple-element.29), channel_id=1, source_target_pairs={{0,32},{8,40},{16,48},{24,56},{32,64},{40,72},{48,80},{56,88},{64,... | collective-permute-start | bytes 798728 | tf_op jit(solution)/shard_map/ppermute | solution.py:485
  5.3 0.8 %collective-permute-start.1 = (f32[512,128]{1,0:T(8,128)S(1)}, f32[512,128]{1,0:T(8,128)S(1)}, u32[]{:S(2)}, u32[]{:S(2)}) collective-permute-start(f32[512,128]{1,0:T(8,128)S(1)} %get-tuple-element.31), channel_id=1, source_target_pairs={{0,96},{8,104},{16,112},{24,120},{32,0},{40,8},{48,16},{56,24},{64... | collective-permute-start | bytes 786440 | tf_op jit(solution)/shard_map/ppermute | solution.py:486
  6.1 0.5 direct_slabs.1
  6.7 3.2 %collective-permute-start.4 = (f32[520,128]{1,0:T(8,128)S(1)}, f32[520,128]{1,0:T(8,128)S(1)}, u32[]{:S(2)}, u32[]{:S(2)}) collective-permute-start(f32[520,128]{1,0:T(8,128)S(1)} %get-tuple-element.34), channel_id=1, source_target_pairs={{0,96},{8,104},{16,112},{24,120},{32,0},{40,8},{48,16},{56,24},{64... | collective-permute-start | bytes 798728 | tf_op jit(solution)/shard_map/ppermute | solution.py:489
  9.9 0.8 %other_slabs.1 = (f32[520,128]{1,0:T(8,128)S(1)}, f32[512,128]{1,0:T(8,128)S(1)}, f32[1032,128]{1,0:T(8,128)S(1)}) custom-call(f32[2,4352,128]{2,1,0:T(8,128)S(1)} %get-tuple-element.23.planes, bf16[2,64,64]{2,1,0:T(8,128)(2,1)S(1)} %get-tuple-element.24.second, bf16[256,128]{1,0:T(8,128)(2,1)S(1)} %get-tuple-element.25.third, ...), custom_call_target="tpu_custom_call" | custom-call | flops 1000000000 | bytes 1048576 | tf_op jit(solution)/shard_map/other_slabs/pallas_call | solution.py:190
  10.7 0.9 %collective-permute-done.1.far_high = f32[512,128]{1,0:T(8,128)S(1)} collective-permute-done((f32[512,128]{1,0:T(8,128)S(1)}, f32[512,128]{1,0:T(8,128)S(1)}, u32[]{:S(2)}, u32[]{:S(2)}) %collective-permute-start.1) | collective-permute-done | bytes 262176 | tf_op jit(solution)/shard_map/ppermute | solution.py:486
  11.7 1.4 %collective-permute-start.2 = (f32[520,128]{1,0:T(8,128)S(1)}, f32[520,128]{1,0:T(8,128)S(1)}, u32[]{:S(2)}, u32[]{:S(2)}) collective-permute-start(f32[520,128]{1,0:T(8,128)S(1)} %get-tuple-element.32), channel_id=1, source_target_pairs={{0,32},{8,40},{16,48},{24,56},{32,64},{40,72},{48,80},{56,88},{64,... | collective-permute-start | bytes 798728 | tf_op jit(solution)/shard_map/ppermute | solution.py:492
  13.2 3.2 %collective-permute-start.3 = (f32[512,128]{1,0:T(8,128)S(1)}, f32[512,128]{1,0:T(8,128)S(1)}, u32[]{:S(2)}, u32[]{:S(2)}) collective-permute-start(f32[512,128]{1,0:T(8,128)S(1)} %get-tuple-element.33), channel_id=1, source_target_pairs={{0,32},{8,40},{16,48},{24,56},{32,64},{40,72},{48,80},{56,88},{64,... | collective-permute-start | bytes 786440 | tf_op jit(solution)/shard_map/ppermute | solution.py:488
  16.4 4.6 %collective-permute-done.3.after_high = f32[512,128]{1,0:T(8,128)S(1)} collective-permute-done((f32[512,128]{1,0:T(8,128)S(1)}, f32[512,128]{1,0:T(8,128)S(1)}, u32[]{:S(2)}, u32[]{:S(2)}) %collective-permute-start.3) | collective-permute-done | bytes 262176 | tf_op jit(solution)/shard_map/ppermute | solution.py:488
  21.0 1.7 %collective-permute-done.5.before_high = f32[512,128]{1,0:T(8,128)S(1)} collective-permute-done((f32[512,128]{1,0:T(8,128)S(1)}, f32[512,128]{1,0:T(8,128)S(1)}, u32[]{:S(2)}, u32[]{:S(2)}) %collective-permute-start.5) | collective-permute-done | bytes 262176 | tf_op jit(solution)/shard_map/ppermute | solution.py:493
  23.0 3.2 %collective-permute-start.7 = (f32[264,128]{1,0:T(8,128)S(1)}, f32[264,128]{1,0:T(8,128)S(1)}, u32[]{:S(2)}, u32[]{:S(2)}) collective-permute-start(f32[264,128]{1,0:T(8,128)S(1)} %get-tuple-element.38), channel_id=1, source_target_pairs={{0,24},{8,0},{16,8},{24,16},{32,56},{40,32},{48,40},{56,48},{64,88... | collective-permute-start | bytes 405512 | tf_op jit(solution)/shard_map/ppermute | solution.py:498
  26.5 2.7 %collective-permute-done.6.refs_1_ = f32[264,128]{1,0:T(8,128)S(1)} collective-permute-done((f32[264,128]{1,0:T(8,128)S(1)}, f32[264,128]{1,0:T(8,128)S(1)}, u32[]{:S(2)}, u32[]{:S(2)}) %collective-permute-start.6) | collective-permute-done | bytes 135200 | tf_op jit(solution)/shard_map/ppermute | solution.py:498
  29.2 1.0 %collective-permute-done.7.refs_2_ = f32[264,128]{1,0:T(8,128)S(1)} collective-permute-done((f32[264,128]{1,0:T(8,128)S(1)}, f32[264,128]{1,0:T(8,128)S(1)}, u32[]{:S(2)}, u32[]{:S(2)}) %collective-permute-start.7) | collective-permute-done | bytes 135200 | tf_op jit(solution)/shard_map/ppermute | solution.py:498
  30.2 2.5 %collective-permute-done.8.refs_3_ = f32[264,128]{1,0:T(8,128)S(1)} collective-permute-done((f32[264,128]{1,0:T(8,128)S(1)}, f32[264,128]{1,0:T(8,128)S(1)}, u32[]{:S(2)}, u32[]{:S(2)}) %collective-permute-start.8) | collective-permute-done | bytes 135200 | tf_op jit(solution)/shard_map/ppermute | solution.py:498
  32.7 0.7 reduce.1
  33.4 6.7 %all-to-all-start = ((f32[8,40,128]{2,1,0:T(8,128)}), f32[8,40,128]{2,1,0:T(8,128)S(1)}, u32[]{:S(2)}, u32[]{:S(2)}) async-start(f32[8,40,128]{2,1,0:T(8,128)} %reduce.1), calls=%async_computation | async-start | bytes 327680 | tf_op jit(solution)/shard_map/all_to_all | solution.py:502
  40.2 2.2 %operators.1 = (bf16[128,2048]{1,0:T(8,128)(2,1)S(1)}, f32[64,3712]{1,0:T(8,128)S(1)}, f32[16,8,128]{2,1,0:T(8,128)S(1)}) custom-call(bf16[16,3,64,64]{3,2,1,0:T(8,128)(2,1)S(1)} %copy-done), custom_call_target="tpu_custom_call" | custom-call | flops 100000000 | bytes 1048576 | tf_op jit(solution)/shard_map/operators/pallas_call | solution.py:302
  42.4 7.2 %all-to-all-done.parts = f32[8,40,128]{2,1,0:T(8,128)S(1)} async-done(((f32[8,40,128]{2,1,0:T(8,128)}), f32[8,40,128]{2,1,0:T(8,128)S(1)}, u32[]{:S(2)}, u32[]{:S(2)}) %all-to-all-start) | async-done | bytes 163872 | tf_op jit(solution)/shard_map/all_to_all | solution.py:502
  49.6 0.5 divide.1.own
  50.2 1.2 %collective-permute-done.9.other = f32[32,128]{1,0:T(8,128)S(1)} collective-permute-done((f32[32,128]{1,0:T(8,128)S(1)}, f32[32,128]{1,0:T(8,128)S(1)}, u32[]{:S(2)}, u32[]{:S(2)}) %collective-permute-start.9) | collective-permute-done | bytes 16416 | tf_op jit(solution)/shard_map/ppermute | solution.py:504
  51.8 10.1 %all_to_all.15.parts = f32[8,1,128]{2,1,0:T(1,128)S(1)} all-to-all(f32[8,1,128]{2,1,0:T(1,128)S(1)} %spectra.1), channel_id=1, replica_groups=mesh['half'=2,'row_0'=4,'row_1'=4,'col'=8] {'col'}, dimensions={0} | all-to-all | bytes 8192 | tf_op jit(solution)/shard_map/all_to_all | solution.py:505
  61.9 12.3 %all_to_all.16.parts = f32[16,1,128]{2,1,0:T(1,128)S(1)} all-to-all(f32[16,1,128]{2,1,0:T(1,128)S(1)} %spread_sum.1), channel_id=1, replica_groups=mesh['half'=2,'row_0'=4,'row_1'=4,'col'=8] {'row_0','row_1'}, dimensions={0} | all-to-all | bytes 16384 | tf_op jit(solution)/shard_map/all_to_all | solution.py:506
  74.2 0.8 %finish.1 = (f32[1,2,4,512]{3,2,1,0:T(4,128)}, f32[2,29]{1,0:T(2,128)}, f32[1,29]{1,0:T(1,128)}) custom-call(f32[16,1,128]{2,1,0:T(1,128)S(1)} %all_to_all.16.parts, f32[32,128]{1,0:T(8,128)S(1)} %divide.1.own, f32[1,29]{1,0:T(1,128)S(1)} %copy-done.1), custom_call_target="tpu_custom_call" | custom-call | tf_op jit(solution)/shard_map/finish/pallas_call | solution.py:444
  (15 shorter events, 1.1 us)
Async XLA Ops:
  3.7 8.0 %collective-permute-start = (f32[520,128]{1,0:T(8,128)S(1)}, f32[520,128]{1,0:T(8,128)S(1)}, u32[]{:S(2)}, u32[]{:S(2)}) collective-permute-start(f32[520,128]{1,0:T(8,128)S(1)} %get-tuple-element.29), channel_id=1, source_target_pairs={{0,32},{8,40},{16,48},{24,56},{32,64},{40,72},{48,80},{56,88},{64,... | collective-permute-start | bytes 798728 | tf_op jit(solution)/shard_map/ppermute | solution.py:485
  5.3 6.4 %collective-permute-start.1 = (f32[512,128]{1,0:T(8,128)S(1)}, f32[512,128]{1,0:T(8,128)S(1)}, u32[]{:S(2)}, u32[]{:S(2)}) collective-permute-start(f32[512,128]{1,0:T(8,128)S(1)} %get-tuple-element.31), channel_id=1, source_target_pairs={{0,96},{8,104},{16,112},{24,120},{32,0},{40,8},{48,16},{56,24},{64... | collective-permute-start | bytes 786440 | tf_op jit(solution)/shard_map/ppermute | solution.py:486
  6.6 33.5 %copy-start = (bf16[16,3,64,64]{3,2,1,0:T(8,128)(2,1)S(1)}, bf16[16,3,64,64]{3,2,1,0:T(8,128)(2,1)}, u32[]{:S(2)}) copy-start(bf16[16,3,64,64]{3,2,1,0:T(8,128)(2,1)} %table.3) | copy-start | bytes 1179652
  6.7 67.6 %copy-start.1 = (f32[1,29]{1,0:T(1,128)S(1)}, f32[1,29]{1,0:T(1,128)}, u32[]{:S(2)}) copy-start(f32[1,29]{1,0:T(1,128)} %constant.2.clone.counts) | copy-start | bytes 352
  6.7 14.3 %collective-permute-start.4 = (f32[520,128]{1,0:T(8,128)S(1)}, f32[520,128]{1,0:T(8,128)S(1)}, u32[]{:S(2)}, u32[]{:S(2)}) collective-permute-start(f32[520,128]{1,0:T(8,128)S(1)} %get-tuple-element.34), channel_id=1, source_target_pairs={{0,96},{8,104},{16,112},{24,120},{32,0},{40,8},{48,16},{56,24},{64... | collective-permute-start | bytes 798728 | tf_op jit(solution)/shard_map/ppermute | solution.py:489
  11.7 11.1 %collective-permute-start.2 = (f32[520,128]{1,0:T(8,128)S(1)}, f32[520,128]{1,0:T(8,128)S(1)}, u32[]{:S(2)}, u32[]{:S(2)}) collective-permute-start(f32[520,128]{1,0:T(8,128)S(1)} %get-tuple-element.32), channel_id=1, source_target_pairs={{0,32},{8,40},{16,48},{24,56},{32,64},{40,72},{48,80},{56,88},{64,... | collective-permute-start | bytes 798728 | tf_op jit(solution)/shard_map/ppermute | solution.py:492
  13.2 7.9 %collective-permute-start.3 = (f32[512,128]{1,0:T(8,128)S(1)}, f32[512,128]{1,0:T(8,128)S(1)}, u32[]{:S(2)}, u32[]{:S(2)}) collective-permute-start(f32[512,128]{1,0:T(8,128)S(1)} %get-tuple-element.33), channel_id=1, source_target_pairs={{0,32},{8,40},{16,48},{24,56},{32,64},{40,72},{48,80},{56,88},{64,... | collective-permute-start | bytes 786440 | tf_op jit(solution)/shard_map/ppermute | solution.py:488
  16.4 6.4 %collective-permute-start.5 = (f32[512,128]{1,0:T(8,128)S(1)}, f32[512,128]{1,0:T(8,128)S(1)}, u32[]{:S(2)}, u32[]{:S(2)}) collective-permute-start(f32[512,128]{1,0:T(8,128)S(1)} %get-tuple-element.35), channel_id=1, source_target_pairs={{0,96},{8,104},{16,112},{24,120},{32,0},{40,8},{48,16},{56,24},{64... | collective-permute-start | bytes 786440 | tf_op jit(solution)/shard_map/ppermute | solution.py:493
  22.9 6.3 %collective-permute-start.6 = (f32[264,128]{1,0:T(8,128)S(1)}, f32[264,128]{1,0:T(8,128)S(1)}, u32[]{:S(2)}, u32[]{:S(2)}) collective-permute-start(f32[264,128]{1,0:T(8,128)S(1)} %get-tuple-element.37), channel_id=1, source_target_pairs={{0,8},{8,16},{16,24},{24,0},{32,40},{40,48},{48,56},{56,32},{64,72... | collective-permute-start | bytes 405512 | tf_op jit(solution)/shard_map/ppermute | solution.py:498
  23.0 7.2 %collective-permute-start.7 = (f32[264,128]{1,0:T(8,128)S(1)}, f32[264,128]{1,0:T(8,128)S(1)}, u32[]{:S(2)}, u32[]{:S(2)}) collective-permute-start(f32[264,128]{1,0:T(8,128)S(1)} %get-tuple-element.38), channel_id=1, source_target_pairs={{0,24},{8,0},{16,8},{24,16},{32,56},{40,32},{48,40},{56,48},{64,88... | collective-permute-start | bytes 405512 | tf_op jit(solution)/shard_map/ppermute | solution.py:498
  26.2 6.5 %collective-permute-start.8 = (f32[264,128]{1,0:T(8,128)S(1)}, f32[264,128]{1,0:T(8,128)S(1)}, u32[]{:S(2)}, u32[]{:S(2)}) collective-permute-start(f32[264,128]{1,0:T(8,128)S(1)} %get-tuple-element.39), channel_id=1, source_target_pairs={{0,16},{8,24},{16,0},{24,8},{32,48},{40,56},{48,32},{56,40},{64,80... | collective-permute-start | bytes 405512 | tf_op jit(solution)/shard_map/ppermute | solution.py:498
  33.4 16.2 %all-to-all-start = ((f32[8,40,128]{2,1,0:T(8,128)}), f32[8,40,128]{2,1,0:T(8,128)S(1)}, u32[]{:S(2)}, u32[]{:S(2)}) async-start(f32[8,40,128]{2,1,0:T(8,128)} %reduce.1), calls=%async_computation | async-start | bytes 327680 | tf_op jit(solution)/shard_map/all_to_all | solution.py:502
  50.1 1.3 %collective-permute-start.9 = (f32[32,128]{1,0:T(8,128)S(1)}, f32[32,128]{1,0:T(8,128)S(1)}, u32[]{:S(2)}, u32[]{:S(2)}) collective-permute-start(f32[32,128]{1,0:T(8,128)S(1)} %divide.1.own), channel_id=1, source_target_pairs={{0,128},{128,0},{1,129},{129,1},{2,130},{130,2},{3,131},{131,3},{4... | collective-permute-start | bytes 49160 | tf_op jit(solution)/shard_map/ppermute | solution.py:504

commit v9 on v7

--- a/solution.py
+++ b/solution.py
@@ -19,6 +19,7 @@
 SLOPES = 29
 SIDE = 4
 PITCH = 68
+PIECES = ((0, 4), (4, 12))
 BLOCK = FIRST * GRID
 OWN = FIRST * SECOND
 ROW = ("row_0", "row_1")
@@ -87,11 +88,11 @@
     ]
     volumes = [
         pltpu.make_async_copy(
-            particles.at[:, :, :, pl.ds(k * 1024, 1024)],
-            volume.at[:, :, :, pl.ds(k * 1024, 1024)],
+            particles.at[:, :, :, pl.ds(start * 256, size * 256)],
+            volume.at[:, :, :, pl.ds(start * 256, size * 256)],
             sem.at[k],
         )
-        for k in range(4)
+        for k, (start, size) in enumerate(PIECES)
     ]
     whole = pltpu.make_async_copy(table, chosen, sem.at[4])
     for copy in (*scalars, whole, *volumes):
@@ -126,10 +127,10 @@
                 base = pl.multiple_of((chunk * 4 + j) * PITCH, 4)
                 planes[p, pl.ds(base, GRID), :] = along[:, j * 128 : j * 128 + 128]
 
-    for k in range(4):
+    for k, (start, size) in enumerate(PIECES):
         volumes[k].wait()
 
-        @pl.loop(k * 4, k * 4 + 4, unroll=4)
+        @pl.loop(start, start + size, unroll=size)
         def _(chunk):
             transform(chunk)
 

time: 75.5 us -> 75.3 us (level)
  no operation moved by 1% of the time
where the time goes in v9:
time: 75.3 us; the launch traced here: 75 us
  blocking collectives  22.4 us (30%)
  waiting for transfers between devices  21.9 us (29%)
  starting transfers between devices  20.7 us (27%)
  Pallas kernels  9.16 us (12%)
    all_to_all x1, blocking collectives, local(): parts = lax.all_to_all(spectra(own, other), ROW, 0, 0, tiled=True)  12.3 us
    all_to_all x1, blocking collectives, local(): parts = lax.all_to_all(spread_sum(parts), 'col', 0, 0, tiled=True)  10.1 us
    all_to_all x1, waiting for transfers between devices, local(): parts = lax.all_to_all(blocks, 'col', 0, 0, tiled=True)  7.18 us
    all_to_all x1, starting transfers between devices, local(): parts = lax.all_to_all(blocks, 'col', 0, 0, tiled=True)  6.77 us
    ppermute x3, waiting for transfers between devices, local(): lax.ppermute(block, HALF_ROW, shifted(shift, True))  6.24 us
    ppermute x1, waiting for transfers between devices, local(): after_high = lax.ppermute(after_high, HALF_ROW, shifted(1))  4.63 us
    ppermute x3, starting transfers between devices, local(): lax.ppermute(block, HALF_ROW, shifted(shift, True))  3.58 us
    ppermute x1, starting transfers between devices, local(): after_high = lax.ppermute(after_high, HALF_ROW, shifted(1))  3.23 us
  transfers between devices with their start and end apart: 11, of which 8 were waited for; matrix products, arithmetic and copies ran while one was open for 0% of the time, Pallas kernels for 5%

profile of v9, /device:TPU:2, one launch (start us, length us, event | category | flops | bytes accessed | tf_op | source)
XLA Modules:
  0.0 75.0 jit_solution(17376387057751454726)
XLA Ops:
  0.6 3.1 %first_slab.1 = (f32[2,4352,128]{2,1,0:T(8,128)S(1)}, bf16[2,64,64]{2,1,0:T(8,128)(2,1)S(1)}, bf16[256,128]{1,0:T(8,128)(2,1)S(1)}, f32[8,128]{1,0:T(8,128)S(1)}...) custom-call(s32[2]{0:T(128)} %bins_in.1, s32[2,2]{1,0:T(2,128)} %slopes_in.1, bf16[2,2,64,4096]{3,2,1,0:T(8,128)(2,1)} %particles.1, ...), custom_call_target="tpu_custom_call" | custom-call | flops 1000000000 | bytes 4194304 | tf_op jit(solution)/shard_map/first_slab/pallas_call | solution.py:142
  3.7 1.6 %collective-permute-start = (f32[520,128]{1,0:T(8,128)S(1)}, f32[520,128]{1,0:T(8,128)S(1)}, u32[]{:S(2)}, u32[]{:S(2)}) collective-permute-start(f32[520,128]{1,0:T(8,128)S(1)} %get-tuple-element.29), channel_id=1, source_target_pairs={{0,32},{8,40},{16,48},{24,56},{32,64},{40,72},{48,80},{56,88},{64,... | collective-permute-start | bytes 798728 | tf_op jit(solution)/shard_map/ppermute | solution.py:486
  5.3 0.8 %collective-permute-start.1 = (f32[512,128]{1,0:T(8,128)S(1)}, f32[512,128]{1,0:T(8,128)S(1)}, u32[]{:S(2)}, u32[]{:S(2)}) collective-permute-start(f32[512,128]{1,0:T(8,128)S(1)} %get-tuple-element.31), channel_id=1, source_target_pairs={{0,96},{8,104},{16,112},{24,120},{32,0},{40,8},{48,16},{56,24},{64... | collective-permute-start | bytes 786440 | tf_op jit(solution)/shard_map/ppermute | solution.py:487
  6.1 0.5 direct_slabs.1
  6.6 3.2 %collective-permute-start.4 = (f32[520,128]{1,0:T(8,128)S(1)}, f32[520,128]{1,0:T(8,128)S(1)}, u32[]{:S(2)}, u32[]{:S(2)}) collective-permute-start(f32[520,128]{1,0:T(8,128)S(1)} %get-tuple-element.34), channel_id=1, source_target_pairs={{0,96},{8,104},{16,112},{24,120},{32,0},{40,8},{48,16},{56,24},{64... | collective-permute-start | bytes 798728 | tf_op jit(solution)/shard_map/ppermute | solution.py:490
  9.9 0.8 %other_slabs.1 = (f32[520,128]{1,0:T(8,128)S(1)}, f32[512,128]{1,0:T(8,128)S(1)}, f32[1032,128]{1,0:T(8,128)S(1)}) custom-call(f32[2,4352,128]{2,1,0:T(8,128)S(1)} %get-tuple-element.23.planes, bf16[2,64,64]{2,1,0:T(8,128)(2,1)S(1)} %get-tuple-element.24.second, bf16[256,128]{1,0:T(8,128)(2,1)S(1)} %get-tuple-element.25.third, ...), custom_call_target="tpu_custom_call" | custom-call | flops 1000000000 | bytes 1048576 | tf_op jit(solution)/shard_map/other_slabs/pallas_call | solution.py:191
  10.7 1.0 %collective-permute-done.1.far_high = f32[512,128]{1,0:T(8,128)S(1)} collective-permute-done((f32[512,128]{1,0:T(8,128)S(1)}, f32[512,128]{1,0:T(8,128)S(1)}, u32[]{:S(2)}, u32[]{:S(2)}) %collective-permute-start.1) | collective-permute-done | bytes 262176 | tf_op jit(solution)/shard_map/ppermute | solution.py:487
  11.7 1.4 %collective-permute-start.2 = (f32[520,128]{1,0:T(8,128)S(1)}, f32[520,128]{1,0:T(8,128)S(1)}, u32[]{:S(2)}, u32[]{:S(2)}) collective-permute-start(f32[520,128]{1,0:T(8,128)S(1)} %get-tuple-element.32), channel_id=1, source_target_pairs={{0,32},{8,40},{16,48},{24,56},{32,64},{40,72},{48,80},{56,88},{64,... | collective-permute-start | bytes 798728 | tf_op jit(solution)/shard_map/ppermute | solution.py:493
  13.1 3.2 %collective-permute-start.3 = (f32[512,128]{1,0:T(8,128)S(1)}, f32[512,128]{1,0:T(8,128)S(1)}, u32[]{:S(2)}, u32[]{:S(2)}) collective-permute-start(f32[512,128]{1,0:T(8,128)S(1)} %get-tuple-element.33), channel_id=1, source_target_pairs={{0,32},{8,40},{16,48},{24,56},{32,64},{40,72},{48,80},{56,88},{64,... | collective-permute-start | bytes 786440 | tf_op jit(solution)/shard_map/ppermute | solution.py:489
  16.4 4.6 %collective-permute-done.3.after_high = f32[512,128]{1,0:T(8,128)S(1)} collective-permute-done((f32[512,128]{1,0:T(8,128)S(1)}, f32[512,128]{1,0:T(8,128)S(1)}, u32[]{:S(2)}, u32[]{:S(2)}) %collective-permute-start.3) | collective-permute-done | bytes 262176 | tf_op jit(solution)/shard_map/ppermute | solution.py:489
  21.0 1.7 %collective-permute-done.5.before_high = f32[512,128]{1,0:T(8,128)S(1)} collective-permute-done((f32[512,128]{1,0:T(8,128)S(1)}, f32[512,128]{1,0:T(8,128)S(1)}, u32[]{:S(2)}, u32[]{:S(2)}) %collective-permute-start.5) | collective-permute-done | bytes 262176 | tf_op jit(solution)/shard_map/ppermute | solution.py:494
  23.0 3.2 %collective-permute-start.7 = (f32[264,128]{1,0:T(8,128)S(1)}, f32[264,128]{1,0:T(8,128)S(1)}, u32[]{:S(2)}, u32[]{:S(2)}) collective-permute-start(f32[264,128]{1,0:T(8,128)S(1)} %get-tuple-element.38), channel_id=1, source_target_pairs={{0,24},{8,0},{16,8},{24,16},{32,56},{40,32},{48,40},{56,48},{64,88... | collective-permute-start | bytes 405512 | tf_op jit(solution)/shard_map/ppermute | solution.py:499
  26.5 2.7 %collective-permute-done.6.refs_1_ = f32[264,128]{1,0:T(8,128)S(1)} collective-permute-done((f32[264,128]{1,0:T(8,128)S(1)}, f32[264,128]{1,0:T(8,128)S(1)}, u32[]{:S(2)}, u32[]{:S(2)}) %collective-permute-start.6) | collective-permute-done | bytes 135200 | tf_op jit(solution)/shard_map/ppermute | solution.py:499
  29.2 1.0 %collective-permute-done.7.refs_2_ = f32[264,128]{1,0:T(8,128)S(1)} collective-permute-done((f32[264,128]{1,0:T(8,128)S(1)}, f32[264,128]{1,0:T(8,128)S(1)}, u32[]{:S(2)}, u32[]{:S(2)}) %collective-permute-start.7) | collective-permute-done | bytes 135200 | tf_op jit(solution)/shard_map/ppermute | solution.py:499
  30.2 2.5 %collective-permute-done.8.refs_3_ = f32[264,128]{1,0:T(8,128)S(1)} collective-permute-done((f32[264,128]{1,0:T(8,128)S(1)}, f32[264,128]{1,0:T(8,128)S(1)}, u32[]{:S(2)}, u32[]{:S(2)}) %collective-permute-start.8) | collective-permute-done | bytes 135200 | tf_op jit(solution)/shard_map/ppermute | solution.py:499
  32.7 0.7 reduce.1
  33.4 6.8 %all-to-all-start = ((f32[8,40,128]{2,1,0:T(8,128)}), f32[8,40,128]{2,1,0:T(8,128)S(1)}, u32[]{:S(2)}, u32[]{:S(2)}) async-start(f32[8,40,128]{2,1,0:T(8,128)} %reduce.1), calls=%async_computation | async-start | bytes 327680 | tf_op jit(solution)/shard_map/all_to_all | solution.py:503
  40.2 2.2 %operators.1 = (bf16[128,2048]{1,0:T(8,128)(2,1)S(1)}, f32[64,3712]{1,0:T(8,128)S(1)}, f32[16,8,128]{2,1,0:T(8,128)S(1)}) custom-call(bf16[16,3,64,64]{3,2,1,0:T(8,128)(2,1)S(1)} %copy-done), custom_call_target="tpu_custom_call" | custom-call | flops 100000000 | bytes 1048576 | tf_op jit(solution)/shard_map/operators/pallas_call | solution.py:303
  42.4 7.2 %all-to-all-done.parts = f32[8,40,128]{2,1,0:T(8,128)S(1)} async-done(((f32[8,40,128]{2,1,0:T(8,128)}), f32[8,40,128]{2,1,0:T(8,128)S(1)}, u32[]{:S(2)}, u32[]{:S(2)}) %all-to-all-start) | async-done | bytes 163872 | tf_op jit(solution)/shard_map/all_to_all | solution.py:503
  49.6 0.5 divide.1.own
  50.2 1.2 %collective-permute-done.9.other = f32[32,128]{1,0:T(8,128)S(1)} collective-permute-done((f32[32,128]{1,0:T(8,128)S(1)}, f32[32,128]{1,0:T(8,128)S(1)}, u32[]{:S(2)}, u32[]{:S(2)}) %collective-permute-start.9) | collective-permute-done | bytes 16416 | tf_op jit(solution)/shard_map/ppermute | solution.py:505
  51.8 12.3 %all_to_all.15.parts = f32[16,1,128]{2,1,0:T(1,128)S(1)} all-to-all(f32[16,1,128]{2,1,0:T(1,128)S(1)} %spectra.1), channel_id=1, replica_groups=mesh['half'=2,'row_0'=4,'row_1'=4,'col'=8] {'row_0','row_1'}, dimensions={0} | all-to-all | bytes 16384 | tf_op jit(solution)/shard_map/all_to_all | solution.py:506
  64.1 10.1 %all_to_all.16.parts = f32[8,1,128]{2,1,0:T(1,128)S(1)} all-to-all(f32[8,1,128]{2,1,0:T(1,128)S(1)} %spread_sum.1), channel_id=1, replica_groups=mesh['half'=2,'row_0'=4,'row_1'=4,'col'=8] {'col'}, dimensions={0} | all-to-all | bytes 8192 | tf_op jit(solution)/shard_map/all_to_all | solution.py:507
  74.2 0.8 %finish.1 = (f32[1,2,4,512]{3,2,1,0:T(4,128)}, f32[2,29]{1,0:T(2,128)}, f32[1,29]{1,0:T(1,128)}) custom-call(f32[8,1,128]{2,1,0:T(1,128)S(1)} %all_to_all.16.parts, f32[32,128]{1,0:T(8,128)S(1)} %divide.1.own, f32[1,29]{1,0:T(1,128)S(1)} %copy-done.1), custom_call_target="tpu_custom_call" | custom-call | tf_op jit(solution)/shard_map/finish/pallas_call | solution.py:445
  (15 shorter events, 1.1 us)
Async XLA Ops:
  3.7 7.9 %collective-permute-start = (f32[520,128]{1,0:T(8,128)S(1)}, f32[520,128]{1,0:T(8,128)S(1)}, u32[]{:S(2)}, u32[]{:S(2)}) collective-permute-start(f32[520,128]{1,0:T(8,128)S(1)} %get-tuple-element.29), channel_id=1, source_target_pairs={{0,32},{8,40},{16,48},{24,56},{32,64},{40,72},{48,80},{56,88},{64,... | collective-permute-start | bytes 798728 | tf_op jit(solution)/shard_map/ppermute | solution.py:486
  5.3 6.4 %collective-permute-start.1 = (f32[512,128]{1,0:T(8,128)S(1)}, f32[512,128]{1,0:T(8,128)S(1)}, u32[]{:S(2)}, u32[]{:S(2)}) collective-permute-start(f32[512,128]{1,0:T(8,128)S(1)} %get-tuple-element.31), channel_id=1, source_target_pairs={{0,96},{8,104},{16,112},{24,120},{32,0},{40,8},{48,16},{56,24},{64... | collective-permute-start | bytes 786440 | tf_op jit(solution)/shard_map/ppermute | solution.py:487
  6.6 33.6 %copy-start = (bf16[16,3,64,64]{3,2,1,0:T(8,128)(2,1)S(1)}, bf16[16,3,64,64]{3,2,1,0:T(8,128)(2,1)}, u32[]{:S(2)}) copy-start(bf16[16,3,64,64]{3,2,1,0:T(8,128)(2,1)} %table.3) | copy-start | bytes 1179652
  6.6 67.6 %copy-start.1 = (f32[1,29]{1,0:T(1,128)S(1)}, f32[1,29]{1,0:T(1,128)}, u32[]{:S(2)}) copy-start(f32[1,29]{1,0:T(1,128)} %constant.2.clone.counts) | copy-start | bytes 352
  6.6 14.3 %collective-permute-start.4 = (f32[520,128]{1,0:T(8,128)S(1)}, f32[520,128]{1,0:T(8,128)S(1)}, u32[]{:S(2)}, u32[]{:S(2)}) collective-permute-start(f32[520,128]{1,0:T(8,128)S(1)} %get-tuple-element.34), channel_id=1, source_target_pairs={{0,96},{8,104},{16,112},{24,120},{32,0},{40,8},{48,16},{56,24},{64... | collective-permute-start | bytes 798728 | tf_op jit(solution)/shard_map/ppermute | solution.py:490
  11.7 11.0 %collective-permute-start.2 = (f32[520,128]{1,0:T(8,128)S(1)}, f32[520,128]{1,0:T(8,128)S(1)}, u32[]{:S(2)}, u32[]{:S(2)}) collective-permute-start(f32[520,128]{1,0:T(8,128)S(1)} %get-tuple-element.32), channel_id=1, source_target_pairs={{0,32},{8,40},{16,48},{24,56},{32,64},{40,72},{48,80},{56,88},{64,... | collective-permute-start | bytes 798728 | tf_op jit(solution)/shard_map/ppermute | solution.py:493
  13.1 7.9 %collective-permute-start.3 = (f32[512,128]{1,0:T(8,128)S(1)}, f32[512,128]{1,0:T(8,128)S(1)}, u32[]{:S(2)}, u32[]{:S(2)}) collective-permute-start(f32[512,128]{1,0:T(8,128)S(1)} %get-tuple-element.33), channel_id=1, source_target_pairs={{0,32},{8,40},{16,48},{24,56},{32,64},{40,72},{48,80},{56,88},{64,... | collective-permute-start | bytes 786440 | tf_op jit(solution)/shard_map/ppermute | solution.py:489
  16.4 6.4 %collective-permute-start.5 = (f32[512,128]{1,0:T(8,128)S(1)}, f32[512,128]{1,0:T(8,128)S(1)}, u32[]{:S(2)}, u32[]{:S(2)}) collective-permute-start(f32[512,128]{1,0:T(8,128)S(1)} %get-tuple-element.35), channel_id=1, source_target_pairs={{0,96},{8,104},{16,112},{24,120},{32,0},{40,8},{48,16},{56,24},{64... | collective-permute-start | bytes 786440 | tf_op jit(solution)/shard_map/ppermute | solution.py:494
  22.9 6.3 %collective-permute-start.6 = (f32[264,128]{1,0:T(8,128)S(1)}, f32[264,128]{1,0:T(8,128)S(1)}, u32[]{:S(2)}, u32[]{:S(2)}) collective-permute-start(f32[264,128]{1,0:T(8,128)S(1)} %get-tuple-element.37), channel_id=1, source_target_pairs={{0,8},{8,16},{16,24},{24,0},{32,40},{40,48},{48,56},{56,32},{64,72... | collective-permute-start | bytes 405512 | tf_op jit(solution)/shard_map/ppermute | solution.py:499
  23.0 7.2 %collective-permute-start.7 = (f32[264,128]{1,0:T(8,128)S(1)}, f32[264,128]{1,0:T(8,128)S(1)}, u32[]{:S(2)}, u32[]{:S(2)}) collective-permute-start(f32[264,128]{1,0:T(8,128)S(1)} %get-tuple-element.38), channel_id=1, source_target_pairs={{0,24},{8,0},{16,8},{24,16},{32,56},{40,32},{48,40},{56,48},{64,88... | collective-permute-start | bytes 405512 | tf_op jit(solution)/shard_map/ppermute | solution.py:499
  26.2 6.5 %collective-permute-start.8 = (f32[264,128]{1,0:T(8,128)S(1)}, f32[264,128]{1,0:T(8,128)S(1)}, u32[]{:S(2)}, u32[]{:S(2)}) collective-permute-start(f32[264,128]{1,0:T(8,128)S(1)} %get-tuple-element.39), channel_id=1, source_target_pairs={{0,16},{8,24},{16,0},{24,8},{32,48},{40,56},{48,32},{56,40},{64,80... | collective-permute-start | bytes 405512 | tf_op jit(solution)/shard_map/ppermute | solution.py:499
  33.4 16.2 %all-to-all-start = ((f32[8,40,128]{2,1,0:T(8,128)}), f32[8,40,128]{2,1,0:T(8,128)S(1)}, u32[]{:S(2)}, u32[]{:S(2)}) async-start(f32[8,40,128]{2,1,0:T(8,128)} %reduce.1), calls=%async_computation | async-start | bytes 327680 | tf_op jit(solution)/shard_map/all_to_all | solution.py:503
  50.1 1.3 %collective-permute-start.9 = (f32[32,128]{1,0:T(8,128)S(1)}, f32[32,128]{1,0:T(8,128)S(1)}, u32[]{:S(2)}, u32[]{:S(2)}) collective-permute-start(f32[32,128]{1,0:T(8,128)S(1)} %divide.1.own), channel_id=1, source_target_pairs={{0,128},{128,0},{1,129},{129,1},{2,130},{130,2},{3,131},{131,3},{4... | collective-permute-start | bytes 49160 | tf_op jit(solution)/shard_map/ppermute | solution.py:505
